TPU v7x, 32 devices: a whole 2x2x4 slice. The times are simulated.
32 devices in a mesh: section: 2 (over x), dp: 8 (over z, y), tensor: 2 (over core).
Axes of the slice: x: 2, y: 2, z: 4, core: 2. Of those that a mesh axis runs over, the one named last changes fastest.
Arguments:
- inputs: float32 [2, 1024, 2048], P(None, ('dp', 'tensor')), may hold values from -6 to 6
- table: int32 [2, 8], replicated, may hold values from 0 to 7, each once within a row
- cotangent: float32 [2, 1024, 2048], P(None, ('dp', 'tensor')), may hold values from -6 to 6
- wq: bfloat16 [2, 2048, 2048], P('section', 'dp', 'tensor'), may hold values from -0.125 to 0.125
- wk: bfloat16 [2, 2048, 512], P('section', 'dp', 'tensor'), may hold values from -0.125 to 0.125
- wv: bfloat16 [2, 2048, 512], P('section', 'dp', 'tensor'), may hold values from -0.125 to 0.125
- wo: bfloat16 [2, 2048, 2048], P('section', 'tensor', 'dp'), may hold values from -1 to 1
- w_gate: bfloat16 [2, 2048, 8192], P('section', 'dp', 'tensor'), may hold values from -0.125 to 0.125
- w_up: bfloat16 [2, 2048, 8192], P('section', 'dp', 'tensor'), may hold values from -0.125 to 0.125
- w_down: bfloat16 [2, 8192, 2048], P('section', 'tensor', 'dp'), may hold values from -0.0625 to 0.0625
- gain_attn: bfloat16 [2, 2048], P('section', 'dp'), may hold values from 0.5 to 1.5
- gain_mlp: bfloat16 [2, 2048], P('section', 'dp'), may hold values from 0.5 to 1.5
Outputs:
- outputs: float32 [2, 2, 1024, 2048], P('section', None, ('dp', 'tensor'))
- input_grad: float32 [2, 2, 1024, 2048], P('section', None, ('dp', 'tensor'))
- grad_wq: float32 [2, 2048, 2048], P('section', 'dp', 'tensor')
- grad_wk: float32 [2, 2048, 512], P('section', 'dp', 'tensor')
- grad_wv: float32 [2, 2048, 512], P('section', 'dp', 'tensor')
- grad_wo: float32 [2, 2048, 2048], P('section', 'tensor', 'dp')
- grad_gate: float32 [2, 2048, 8192], P('section', 'dp', 'tensor')
- grad_up: float32 [2, 2048, 8192], P('section', 'dp', 'tensor')
- grad_down: float32 [2, 8192, 2048], P('section', 'tensor', 'dp')
- grad_gain_attn: float32 [2, 2048], P('section', ('dp', 'tensor'))
- grad_gain_mlp: float32 [2, 2048], P('section', ('dp', 'tensor'))
Inputs may be any that keep to these rules, and one draw needn't show every extreme that they name: `table`: each row holds every number from 0 to 7 once.
All inputs are finite; a program needn't handle non-finite values.
Results may differ from a plain program's by a relative error of at most 0.025.
Values may be sent and summed in bfloat16 or wider, within the bound.
A program may use at most 384 MiB of HBM per device.

v0:
```python
import math

import jax
import jax.numpy as jnp
from jax import lax
from jax.sharding import PartitionSpec as P

HEAD_SIZE = 64


epsilon = 1e-05


def passed_along(value, axis, steps):
    count = lax.axis_size(axis)
    initial, last = (max(0, -steps), min(count, count - steps))
    return lax.ppermute(value, axis, [(source, source + steps) for source in range(initial, last)])


def rope_frequencies(head):
    index = jnp.arange(head // 2, dtype=jnp.float32)
    base = 1.0 / 500000.0 ** (index * 2.0 / head)
    wavelength = 2.0 * math.pi / base
    blend = (8192.0 / wavelength - 1.0) / 3.0
    middle = (1.0 - blend) * base / 32.0 + blend * base
    return jnp.where(wavelength < 2048.0, base, jnp.where(wavelength > 8192.0, base / 32.0, middle))


def rotate(values, positions, head):
    step_count = values.shape[0]
    shaped = values.reshape(step_count, -1, head)
    angle = positions.astype(jnp.float32)[:, None] * rope_frequencies(head)[None, :]
    cosine = jnp.cos(angle)[:, None, :]
    sine = jnp.sin(angle)[:, None, :]
    first = shaped[:, :, : head // 2]
    second = shaped[:, :, head // 2 :]
    return jnp.concatenate(
        [first * cosine - second * sine, second * cosine + first * sine], axis=-1
    ).reshape(step_count, -1)


def unrotate(values, positions, head):
    step_count = values.shape[0]
    shaped = values.reshape(step_count, -1, head)
    angle = positions.astype(jnp.float32)[:, None] * rope_frequencies(head)[None, :]
    cosine = jnp.cos(angle)[:, None, :]
    sine = jnp.sin(angle)[:, None, :]
    first = shaped[:, :, : head // 2]
    second = shaped[:, :, head // 2 :]
    return jnp.concatenate(
        [first * cosine + second * sine, second * cosine - first * sine], axis=-1
    ).reshape(step_count, -1)


def norm_stats(rows):
    inverse = lax.rsqrt(jnp.mean(rows * rows, axis=-1, keepdims=True) + epsilon)
    return (rows * inverse, inverse)


def norm_back(grad, unit, inverse, gain):
    scaled = grad * gain
    inner = jnp.mean(scaled * unit, axis=-1, keepdims=True)
    return (inverse * (scaled - unit * inner), jnp.sum(grad * unit, axis=0))


def matmul(left, right):
    return jnp.dot(left, right, preferred_element_type=jnp.float32)


def block_layout(table, micro, groups, block):
    layout_row = lax.dynamic_index_in_dim(table, micro, 0, keepdims=False)
    span = groups // 2
    mine = lax.dynamic_index_in_dim(layout_row, lax.axis_index("dp"), 0, keepdims=False)
    sequence = mine // span
    place = mine % span
    slot_ids = jnp.arange(groups, dtype=jnp.int32)
    holder = jnp.sum(
        jnp.where(layout_row[None, :] == slot_ids[:, None], slot_ids[None, :], 0), axis=1
    )
    slots = lax.dynamic_slice_in_dim(holder, sequence * span, span)
    positions = place * block + jnp.arange(block, dtype=jnp.int32)
    return (slots, positions)


def attend(query_rows, key_seq, value_seq, positions, heads_kv, head):
    step_count = query_rows.shape[0]
    keys_total = key_seq.shape[0]
    head_group = query_rows.shape[1] // (heads_kv * head)
    scale = 1.0 / math.sqrt(head)
    allowed = jnp.arange(keys_total, dtype=jnp.int32)[None, :] <= positions[:, None]
    query_layers = query_rows.reshape(step_count, heads_kv, head_group * head).transpose(1, 0, 2)
    key_layers = key_seq.reshape(keys_total, heads_kv, head).transpose(1, 0, 2)
    value_layers = value_seq.reshape(keys_total, heads_kv, head).transpose(1, 0, 2)

    def one_head(parts):
        q_head, k_head, v_head = parts
        q_three = q_head.reshape(step_count, head_group, head)
        scores = (
            jnp.einsum("qgd,kd->gqk", q_three, k_head, preferred_element_type=jnp.float32) * scale
        )
        total = jnp.sum(jnp.where(allowed, jnp.exp(scores), 0.0), axis=-1)
        log_total = jnp.log(total)
        probs = jnp.where(allowed, jnp.exp(scores - log_total[..., None]), 0.0).astype(jnp.bfloat16)
        mixed = jnp.einsum("gqk,kd->qgd", probs, v_head, preferred_element_type=jnp.float32).astype(
            jnp.bfloat16
        )
        return (mixed.reshape(step_count, head_group * head), log_total)

    mixed, log_total = lax.map(one_head, (query_layers, key_layers, value_layers))
    return (mixed.transpose(1, 0, 2).reshape(step_count, -1), log_total)


def attend_back(
    blended_gradient, query_rows, key_seq, value_seq, log_total, positions, heads_kv, head
):
    step_count = query_rows.shape[0]
    keys_total = key_seq.shape[0]
    head_group = query_rows.shape[1] // (heads_kv * head)
    scale = 1.0 / math.sqrt(head)
    allowed = jnp.arange(keys_total, dtype=jnp.int32)[None, :] <= positions[:, None]
    query_layers = query_rows.reshape(step_count, heads_kv, head_group * head).transpose(1, 0, 2)
    key_layers = key_seq.reshape(keys_total, heads_kv, head).transpose(1, 0, 2)
    value_layers = value_seq.reshape(keys_total, heads_kv, head).transpose(1, 0, 2)
    gain_layers = blended_gradient.reshape(step_count, heads_kv, head_group * head).transpose(
        1, 0, 2
    )

    def one_head(parts):
        q_head, k_head, v_head, g_head, l_head = parts
        q_three = q_head.reshape(step_count, head_group, head)
        g_three = g_head.reshape(step_count, head_group, head)
        scores = (
            jnp.einsum("qgd,kd->gqk", q_three, k_head, preferred_element_type=jnp.float32) * scale
        )
        probs = jnp.where(allowed, jnp.exp(scores - l_head[..., None]), 0.0)
        rounded = probs.astype(jnp.bfloat16)
        prob_grad = jnp.einsum("qgd,kd->gqk", g_three, v_head, preferred_element_type=jnp.float32)
        value_total_sum = jnp.einsum(
            "gqk,qgd->kd", rounded, g_three, preferred_element_type=jnp.float32
        )
        rowdot = jnp.sum(probs * prob_grad, axis=-1, keepdims=True)
        score_grad = (probs * (prob_grad - rowdot) * scale).astype(jnp.bfloat16)
        query_grad = jnp.einsum(
            "gqk,kd->qgd", score_grad, k_head, preferred_element_type=jnp.float32
        )
        key_gradient = jnp.einsum(
            "gqk,qgd->kd", score_grad, q_three, preferred_element_type=jnp.float32
        )
        return (query_grad.reshape(step_count, head_group * head), key_gradient, value_total_sum)

    query_grad, key_gradient, value_total_sum = lax.map(
        one_head, (query_layers, key_layers, value_layers, gain_layers, log_total)
    )
    query_grad = query_grad.transpose(1, 0, 2).reshape(step_count, -1)
    key_gradient = key_gradient.transpose(1, 0, 2).reshape(keys_total, -1)
    value_total_sum = value_total_sum.transpose(1, 0, 2).reshape(keys_total, -1)
    return (query_grad, key_gradient, value_total_sum)


def layer_forward(rows, table, micro, weights, groups, heads_kv, head):
    wq, wk, wv, wo, w_gate, w_up, w_down, gain_attn, gain_mlp = weights
    full = lax.all_gather(rows, "tensor", axis=0, tiled=True)
    block = full.shape[0]
    slots, positions = block_layout(table, micro, groups, block)
    unit1, inverse1 = norm_stats(full)
    normed1 = (unit1 * gain_attn.astype(jnp.float32)).astype(jnp.bfloat16)
    query_rows = rotate(matmul(normed1, wq), positions, head).astype(jnp.bfloat16)
    key = rotate(matmul(normed1, wk), positions, head).astype(jnp.bfloat16)
    value_rows = matmul(normed1, wv).astype(jnp.bfloat16)
    key_all, value_all = (
        lax.all_gather(key, "dp", axis=0, tiled=True),
        lax.all_gather(value_rows, "dp", axis=0, tiled=True),
    )
    kv_width = key.shape[1]
    key_seq = key_all.reshape(groups, block, kv_width)[slots].reshape(-1, kv_width)
    value_seq = value_all.reshape(groups, block, kv_width)[slots].reshape(-1, kv_width)
    mixed, log_total = attend(query_rows, key_seq, value_seq, positions, heads_kv, head)
    second = rows + lax.psum_scatter(matmul(mixed, wo), "tensor", scatter_dimension=0, tiled=True)
    full_second = lax.all_gather(second, "tensor", axis=0, tiled=True)
    unit2, inverse2 = norm_stats(full_second)
    normed2 = (unit2 * gain_mlp.astype(jnp.float32)).astype(jnp.bfloat16)
    gate = matmul(normed2, w_gate)
    upper = matmul(normed2, w_up)
    hidden = (jax.nn.silu(gate) * upper).astype(jnp.bfloat16)
    result = second + lax.psum_scatter(
        matmul(hidden, w_down), "tensor", scatter_dimension=0, tiled=True
    )
    return (
        result,
        (
            full,
            query_rows,
            key_seq,
            value_seq,
            mixed,
            log_total,
            full_second,
            gate,
            upper,
            hidden,
            slots,
            positions,
        ),
    )


def layer_backward(grad_rows, context, weights, groups, parts, heads_kv, head):
    wq, wk, wv, wo, w_gate, w_up, w_down, gain_attn, gain_mlp = weights
    (
        full,
        query_rows,
        key_seq,
        value_seq,
        mixed,
        log_total,
        full_second,
        gate,
        upper,
        hidden,
        slots,
        positions,
    ) = context
    block = full.shape[0]
    out_grad = lax.all_gather(grad_rows.astype(jnp.bfloat16), "tensor", axis=0, tiled=True)
    grad_down = matmul(hidden.T, out_grad)
    hidden_grad = matmul(out_grad, w_down.T)
    sigma = jax.nn.sigmoid(gate)
    gate_grad = (hidden_grad * upper * sigma * (1.0 + gate * (1.0 - sigma))).astype(jnp.bfloat16)
    up_grad = (hidden_grad * gate * sigma).astype(jnp.bfloat16)
    unit2, inverse2 = norm_stats(full_second)
    normed2 = (unit2 * gain_mlp.astype(jnp.float32)).astype(jnp.bfloat16)
    grad_gate = matmul(normed2.T, gate_grad)
    grad_up = matmul(normed2.T, up_grad)
    normed2_grad = matmul(gate_grad, w_gate.T) + matmul(up_grad, w_up.T)
    second_terms, gain_mlp_terms = norm_back(
        normed2_grad, unit2, inverse2, gain_mlp.astype(jnp.float32)
    )
    piece_width = gain_mlp_terms.shape[0] // (groups * parts)
    second_part, gain_mlp_part = (
        lax.psum_scatter(
            second_terms.astype(jnp.bfloat16), "tensor", scatter_dimension=0, tiled=True
        ).astype(jnp.float32),
        lax.psum_scatter(
            gain_mlp_terms.reshape(groups, parts, piece_width).astype(jnp.bfloat16),
            "tensor",
            scatter_dimension=1,
            tiled=True,
        ).astype(jnp.float32),
    )
    second_grad = grad_rows + second_part
    attn_grad = lax.all_gather(second_grad.astype(jnp.bfloat16), "tensor", axis=0, tiled=True)
    grad_wo = matmul(mixed.T, attn_grad)
    blended_gradient = matmul(attn_grad, wo.T).astype(jnp.bfloat16)
    query_grad, key_seq_grad, value_seq_grad = attend_back(
        blended_gradient, query_rows, key_seq, value_seq, log_total, positions, heads_kv, head
    )
    kv_width = key_seq.shape[1]
    key_spread = (
        jnp.zeros((groups, block, kv_width), jnp.float32)
        .at[slots]
        .set(key_seq_grad.reshape(-1, block, kv_width))
    )
    value_spread = (
        jnp.zeros((groups, block, kv_width), jnp.float32)
        .at[slots]
        .set(value_seq_grad.reshape(-1, block, kv_width))
    )
    key_own, value_own = (
        lax.psum_scatter(
            key_spread.astype(jnp.bfloat16), "dp", scatter_dimension=0, tiled=True
        ).astype(jnp.float32),
        lax.psum_scatter(
            value_spread.astype(jnp.bfloat16), "dp", scatter_dimension=0, tiled=True
        ).astype(jnp.float32),
    )
    query_round = unrotate(query_grad, positions, head).astype(jnp.bfloat16)
    key_round = unrotate(key_own.reshape(block, kv_width), positions, head).astype(jnp.bfloat16)
    value_round = value_own.reshape(block, kv_width).astype(jnp.bfloat16)
    unit1, inverse1 = norm_stats(full)
    normed1 = (unit1 * gain_attn.astype(jnp.float32)).astype(jnp.bfloat16)
    grad_wq = matmul(normed1.T, query_round)
    grad_wk = matmul(normed1.T, key_round)
    grad_wv = matmul(normed1.T, value_round)
    normed1_grad = matmul(query_round, wq.T) + matmul(key_round, wk.T) + matmul(value_round, wv.T)
    first_terms, gain_attn_terms = norm_back(
        normed1_grad, unit1, inverse1, gain_attn.astype(jnp.float32)
    )
    first_part, gain_attn_part = (
        lax.psum_scatter(first_terms, "tensor", scatter_dimension=0, tiled=True),
        lax.psum_scatter(
            gain_attn_terms.reshape(groups, parts, piece_width),
            "tensor",
            scatter_dimension=1,
            tiled=True,
        ),
    )
    input_grad = second_grad + first_part
    return (
        input_grad,
        (
            grad_wq,
            grad_wk,
            grad_wv,
            grad_wo,
            grad_gate,
            grad_up,
            grad_down,
            gain_attn_part,
            gain_mlp_part,
        ),
    )


def reduce_grads(pieces):
    return (
        lax.psum_scatter(
            pieces[0].astype(jnp.bfloat16), "dp", scatter_dimension=0, tiled=True
        ).astype(jnp.float32),
        lax.psum_scatter(
            pieces[1].astype(jnp.bfloat16), "dp", scatter_dimension=0, tiled=True
        ).astype(jnp.float32),
        lax.psum_scatter(
            pieces[2].astype(jnp.bfloat16), "dp", scatter_dimension=0, tiled=True
        ).astype(jnp.float32),
        lax.psum_scatter(
            pieces[3].astype(jnp.bfloat16), "dp", scatter_dimension=1, tiled=True
        ).astype(jnp.float32),
        lax.psum_scatter(
            pieces[4].astype(jnp.bfloat16), "dp", scatter_dimension=0, tiled=True
        ).astype(jnp.float32),
        lax.psum_scatter(
            pieces[5].astype(jnp.bfloat16), "dp", scatter_dimension=0, tiled=True
        ).astype(jnp.float32),
        lax.psum_scatter(
            pieces[6].astype(jnp.bfloat16), "dp", scatter_dimension=1, tiled=True
        ).astype(jnp.float32),
        lax.psum_scatter(
            pieces[7].astype(jnp.bfloat16), "dp", scatter_dimension=0, tiled=True
        ).astype(jnp.float32),
        lax.psum_scatter(
            pieces[8].astype(jnp.bfloat16), "dp", scatter_dimension=0, tiled=True
        ).astype(jnp.float32),
    )


def shards(inputs, table, cotangent, wq, wk, wv, wo, w_gate, w_up, w_down, gain_attn, gain_mlp):
    groups = lax.axis_size("dp")
    parts = lax.axis_size("tensor")
    micro_count = inputs.shape[0]
    section = lax.axis_index("section")
    first_section = section == 0
    weights = (
        lax.all_gather(wq[0], "dp", axis=0, tiled=True),
        lax.all_gather(wk[0], "dp", axis=0, tiled=True),
        lax.all_gather(wv[0], "dp", axis=0, tiled=True),
        lax.all_gather(wo[0], "dp", axis=1, tiled=True),
        lax.all_gather(w_gate[0], "dp", axis=0, tiled=True),
        lax.all_gather(w_up[0], "dp", axis=0, tiled=True),
        lax.all_gather(w_down[0], "dp", axis=1, tiled=True),
        lax.all_gather(gain_attn[0], "dp", axis=0, tiled=True),
        lax.all_gather(gain_mlp[0], "dp", axis=0, tiled=True),
    )
    head = HEAD_SIZE
    heads_kv = wk.shape[2] // head
    received = jnp.zeros_like(inputs[0])
    produced = []
    saved = []
    for step in range(micro_count + 1):
        own_rows = inputs[step] if step < micro_count else jnp.zeros_like(inputs[0])
        start_rows = jnp.where(first_section, own_rows, received)
        micro = jnp.clip(step - section, 0, micro_count - 1)
        result, context = layer_forward(start_rows, table, micro, weights, groups, heads_kv, head)
        produced.append(result)
        saved.append(context)
        if step < micro_count:
            received = passed_along(result, "section", 1)
    stacked = jnp.stack(produced)
    outputs = jnp.where(first_section, stacked[:micro_count], stacked[1:])[None]
    returned = jnp.zeros_like(inputs[0])
    returned_list = []
    totals = None
    for step in range(micro_count + 1):
        index = micro_count - 1 - step
        given = cotangent[index] if index >= 0 else jnp.zeros_like(cotangent[0])
        start_grad = jnp.where(first_section, returned, given)
        din, pieces = layer_backward(
            start_grad, saved[micro_count - step], weights, groups, parts, heads_kv, head
        )
        returned_list.append(din)
        if step < micro_count:
            returned = passed_along(din.astype(jnp.bfloat16), "section", -1).astype(din.dtype)
        totals = (
            pieces
            if totals is None
            else tuple((left + right for left, right in zip(totals, pieces)))
        )
    totals = reduce_grads(totals)
    reverse_stack = jnp.stack(returned_list[::-1])
    input_grad = jnp.where(first_section, reverse_stack[:micro_count], reverse_stack[1:])[None]
    (
        grad_wq,
        grad_wk,
        grad_wv,
        grad_wo,
        grad_gate,
        grad_up,
        grad_down,
        gain_attn_sum,
        gain_mlp_sum,
    ) = totals
    width_piece = gain_attn_sum.shape[-1]
    return (
        outputs,
        input_grad,
        grad_wq[None],
        grad_wk[None],
        grad_wv[None],
        grad_wo[None],
        grad_gate[None],
        grad_up[None],
        grad_down[None],
        gain_attn_sum.reshape(1, width_piece),
        gain_mlp_sum.reshape(1, width_piece),
    )


def solution(mesh):
    in_specs = (
        P(None, ("dp", "tensor"), None),
        P(),
        P(None, ("dp", "tensor"), None),
        P("section", "dp", "tensor"),
        P("section", "dp", "tensor"),
        P("section", "dp", "tensor"),
        P("section", "tensor", "dp"),
        P("section", "dp", "tensor"),
        P("section", "dp", "tensor"),
        P("section", "tensor", "dp"),
        P("section", "dp"),
        P("section", "dp"),
    )
    out_specs = (
        P("section", None, ("dp", "tensor"), None),
        P("section", None, ("dp", "tensor"), None),
        P("section", "dp", "tensor"),
        P("section", "dp", "tensor"),
        P("section", "dp", "tensor"),
        P("section", "tensor", "dp"),
        P("section", "dp", "tensor"),
        P("section", "dp", "tensor"),
        P("section", "tensor", "dp"),
        P("section", ("dp", "tensor")),
        P("section", ("dp", "tensor")),
    )
    return jax.shard_map(shards, mesh=mesh, in_specs=in_specs, out_specs=out_specs, check_vma=False)
```

profile of v0, /device:TPU:0, one launch (start us, length us, event | category | flops | bytes accessed | tf_op | source)
XLA Modules:
  0.0 3303.5 jit_solution(10158903163360813537)
XLA Ops:
  20.6 22.6 all-gather.1
  47.1 18.4 all-gather.36.cloned.1.call-done
  67.0 32.1 all_gather.84
  109.8 29.6 all_gather.86
  140.5 46.9 %all-gather.40.cloned.1.call-done = bf16[1,2048,1024]{2,1,0:T(8,128)(2,1)} async-done(((bf16[1,256,1024]{2,1,0:T(8,128)(2,1)}), bf16[1,2048,1024]{2,1,0:T(8,128)(2,1)}) %all-gather.40.cloned.1.call-update) | async-done | bytes 4194320 | tf_op jit(solution)/shard_map/all_gather | solution.py:353
  201.6 60.8 %all-gather.42.cloned.1.call-done = bf16[1,1024,2048]{2,1,0:T(8,128)(2,1)} async-done(((bf16[1,1024,256]{2,1,0:T(8,128)(2,1)}), bf16[1,1024,2048]{2,1,0:T(8,128)(2,1)}) %all-gather.42.cloned.1.call-update) | async-done | bytes 4194320 | tf_op jit(solution)/shard_map/all_gather | solution.py:356
  277.2 21.3 all-gather.6
  301.7 214.4 %all-gather.44.cloned.1.call-done = bf16[1,2048,4096]{2,1,0:T(8,128)(2,1)} async-done(((bf16[1,256,4096]{2,1,0:T(8,128)(2,1)}), bf16[1,2048,4096]{2,1,0:T(8,128)(2,1)}) %all-gather.44.cloned.1.call-update) | async-done | bytes 16777232 | tf_op jit(solution)/shard_map/all_gather | solution.py:357
  525.5 218.2 %all-gather.46.cloned.1.call-done = bf16[1,2048,4096]{2,1,0:T(8,128)(2,1)} async-done(((bf16[1,256,4096]{2,1,0:T(8,128)(2,1)}), bf16[1,2048,4096]{2,1,0:T(8,128)(2,1)}) %all-gather.46.cloned.1.call-update) | async-done | bytes 16777232 | tf_op jit(solution)/shard_map/all_gather | solution.py:358
  754.1 217.1 %all-gather.48.cloned.1.call-done = bf16[1,4096,2048]{2,1,0:T(8,128)(2,1)} async-done(((bf16[1,4096,256]{2,1,0:T(8,128)(2,1)}), bf16[1,4096,2048]{2,1,0:T(8,128)(2,1)}) %all-gather.48.cloned.1.call-update) | async-done | bytes 16777232 | tf_op jit(solution)/shard_map/all_gather | solution.py:359
  1019.4 31.8 all_gather.95
  1052.7 27.2 all_gather.96
  1191.3 33.5 %all_gather.99 = bf16[1024,256]{1,0:T(8,128)(2,1)} all-gather(bf16[128,256]{1,0:T(8,128)(2,1)S(1)} %convolution_convert_fusion.3), channel_id=1, replica_groups=mesh['section'=2,'dp'=8,'tensor'=2] {'dp'}, dimensions={0}, use_global_device_ids=true | all-gather | bytes 589824 | tf_op jit(solution)/shard_map/all_gather | solution.py:172
  1229.7 28.3 all_gather.100
  1269.0 13.4 while.86
  1299.2 13.2 fusion.148
  1334.5 12.9 fusion.160
  1347.5 13.6 multiply_reduce_fusion.5
  1384.0 42.0 %while.87 = (s32[]{:T(128)}, f32[4,128,256]{1,2,0:T(8,128)}, f32[4,512,64]{1,2,0:T(8,128)}, f32[4,512,64]{1,2,0:T(8,128)}, bf16[4,512,64]{1,2,0:T(8,128)(2,1)}, ...) while((s32[]{:T(128)}, f32[4,128,256]{1,2,0:T(8,128)}, ...), condition=%wide.region_28.29_spmd.clone, body=%wide.region_26.28_spmd.clone.sunk | while | flops 171509760 | bytes 13048469 | solution.py:151
  1439.3 55.5 %reduce-scatter.40.cloned.1.call-done = bf16[1,128,256]{2,1,0:T(8,128)(2,1)} async-done(((bf16[8,128,256]{2,1,0:T(8,128)(2,1)}), bf16[1,128,256]{2,1,0:T(8,128)(2,1)}) %reduce-scatter.40.cloned.1.call-update) | async-done | bytes 65552 | tf_op jit(solution)/shard_map/reduce_scatter | solution.py:269
  1496.5 63.3 %reduce-scatter.42.cloned.1.call-done = bf16[1,128,256]{2,1,0:T(8,128)(2,1)} async-done(((bf16[8,128,256]{2,1,0:T(8,128)(2,1)}), bf16[1,128,256]{2,1,0:T(8,128)(2,1)}) %reduce-scatter.42.cloned.1.call-update) | async-done | bytes 65552 | tf_op jit(solution)/shard_map/reduce_scatter | solution.py:272
  1589.0 14.4 multiply_convert_fusion.3
  1603.5 12.8 fusion.158
  1616.3 14.0 multiply_reduce_fusion.4
  1652.4 44.7 %while.88 = (s32[]{:T(128)}, f32[4,128,256]{1,2,0:T(8,128)}, f32[4,512,64]{1,2,0:T(8,128)}, f32[4,512,64]{1,2,0:T(8,128)}, bf16[4,512,64]{1,2,0:T(8,128)(2,1)}, ...) while((s32[]{:T(128)}, f32[4,128,256]{1,2,0:T(8,128)}, ...), condition=%wide.region_39.40_spmd.clone, body=%wide.region_37.39_spmd.clone.sunk | while | flops 171509760 | bytes 13048469 | solution.py:151
  1710.4 55.5 %reduce-scatter.48.cloned.1.call-done = bf16[1,128,256]{2,1,0:T(8,128)(2,1)} async-done(((bf16[8,128,256]{2,1,0:T(8,128)(2,1)}), bf16[1,128,256]{2,1,0:T(8,128)(2,1)}) %reduce-scatter.48.cloned.1.call-update) | async-done | bytes 65552 | tf_op jit(solution)/shard_map/reduce_scatter | solution.py:269
  1768.4 62.5 %reduce-scatter.50.cloned.1.call-done = bf16[1,128,256]{2,1,0:T(8,128)(2,1)} async-done(((bf16[8,128,256]{2,1,0:T(8,128)(2,1)}), bf16[1,128,256]{2,1,0:T(8,128)(2,1)}) %reduce-scatter.50.cloned.1.call-update) | async-done | bytes 65552 | tf_op jit(solution)/shard_map/reduce_scatter | solution.py:272
  1859.3 14.4 multiply_convert_fusion.1
  1873.7 12.8 fusion.156
  1886.5 13.8 multiply_reduce_fusion.3
  1922.8 44.6 %while.89 = (s32[]{:T(128)}, f32[4,128,256]{1,2,0:T(8,128)}, f32[4,512,64]{1,2,0:T(8,128)}, f32[4,512,64]{1,2,0:T(8,128)}, bf16[4,512,64]{1,2,0:T(8,128)(2,1)}, ...) while((s32[]{:T(128)}, f32[4,128,256]{1,2,0:T(8,128)}, ...), condition=%wide.region_50.51_spmd.clone, body=%wide.region_48.50_spmd.clone.sunk | while | flops 171509760 | bytes 13048469 | solution.py:151
  1989.4 47.0 %reduce-scatter.56.cloned.1.call-done = bf16[1,128,256]{2,1,0:T(8,128)(2,1)} async-done(((bf16[8,128,256]{2,1,0:T(8,128)(2,1)}), bf16[1,128,256]{2,1,0:T(8,128)(2,1)}) %reduce-scatter.56.cloned.1.call-update) | async-done | bytes 65552 | tf_op jit(solution)/shard_map/reduce_scatter | solution.py:269
  2042.9 58.4 %reduce-scatter.58.cloned.1.call-done = bf16[1,128,256]{2,1,0:T(8,128)(2,1)} async-done(((bf16[8,128,256]{2,1,0:T(8,128)(2,1)}), bf16[1,128,256]{2,1,0:T(8,128)(2,1)}) %reduce-scatter.58.cloned.1.call-update) | async-done | bytes 65552 | tf_op jit(solution)/shard_map/reduce_scatter | solution.py:272
  2125.5 13.4 fusion.298
  2139.0 13.3 fusion.299
  2152.3 28.5 add_convert_fusion.2
  2182.0 13.3 fusion.300
  2195.3 13.4 fusion.301
  2208.7 28.6 add_convert_fusion.1
  2238.7 13.2 fusion.302
  2251.9 13.2 fusion.303
  2265.1 29.1 add_convert_fusion
  2305.4 20.2 all-reduce.6
  2333.5 17.2 reduce-scatter.62.cloned.1.call-done
  2352.8 90.5 %reduce-scatter.68.cloned.1.call-done = bf16[1024,256]{1,0:T(8,128)(2,1)} async-done(((bf16[1024,2048]{1,0:T(8,128)(2,1)}), bf16[1024,256]{1,0:T(8,128)(2,1)}) %reduce-scatter.68.cloned.1.call-update) | async-done | bytes 524304 | tf_op jit(solution)/shard_map/reduce_scatter | solution.py:325
  2445.4 281.4 %reduce-scatter.70.cloned.1.call-done = bf16[256,4096]{1,0:T(8,128)(2,1)} async-done(((bf16[2048,4096]{1,0:T(8,128)(2,1)}), bf16[256,4096]{1,0:T(8,128)(2,1)}) %reduce-scatter.70.cloned.1.call-update) | async-done | bytes 2097168 | tf_op jit(solution)/shard_map/reduce_scatter | solution.py:328
  2730.9 278.8 %reduce-scatter.72.cloned.1.call-done = bf16[256,4096]{1,0:T(8,128)(2,1)} async-done(((bf16[2048,4096]{1,0:T(8,128)(2,1)}), bf16[256,4096]{1,0:T(8,128)(2,1)}) %reduce-scatter.72.cloned.1.call-update) | async-done | bytes 2097168 | tf_op jit(solution)/shard_map/reduce_scatter | solution.py:331
  3013.8 279.0 %reduce-scatter.74.cloned.1.call-done = bf16[4096,256]{1,0:T(8,128)(2,1)} async-done(((bf16[4096,2048]{1,0:T(8,128)(2,1)}), bf16[4096,256]{1,0:T(8,128)(2,1)}) %reduce-scatter.74.cloned.1.call-update) | async-done | bytes 2097168 | tf_op jit(solution)/shard_map/reduce_scatter | solution.py:334
  (780 shorter events, 697.7 us)
Async XLA Ops:
  7.2 37.1 %all-gather.34.cloned.1.call-start = ((), (), s32[]{:S(2)}) async-start(), calls=%async_computation.55 | async-start | bytes 1572864 | tf_op jit(solution)/shard_map/all_gather | solution.py:162
  9.1 56.3 %all-gather.36.cloned.1.call-start = ((), (), s32[]{:S(2)}) async-start(), calls=%async_computation.56 | async-start | bytes 1179648 | tf_op jit(solution)/shard_map/all_gather | solution.py:355
  9.9 98.1 %all-gather.38.cloned.1.call-start = ((), (), s32[]{:S(2)}) async-start(), calls=%async_computation.57 | async-start | bytes 1179648 | tf_op jit(solution)/shard_map/all_gather | solution.py:354
  10.6 176.7 %all-gather.40.cloned.1.call-start = ((), (), s32[]{:S(2)}) async-start(), calls=%async_computation.58 | async-start | bytes 4718592 | tf_op jit(solution)/shard_map/all_gather | solution.py:353
  11.2 251.2 %all-gather.42.cloned.1.call-start = ((), (), s32[]{:S(2)}) async-start(), calls=%async_computation.59 | async-start | bytes 4718592 | tf_op jit(solution)/shard_map/all_gather | solution.py:356
  11.8 261.3 %reduce-scatter.26.cloned.1.call-start = ((), (), s32[]{:S(2)}) async-start(), calls=%async_computation.25 | async-start | bytes 1572864 | tf_op jit(solution)/shard_map/reduce_scatter | solution.py:178
  44.3 1043.2 %copy-start.81 = (f32[128,32]{0,1:T(8,128)}, f32[128,32]{0,1:T(8,128)S(1)}, u32[]{:S(2)}) copy-start(f32[128,32]{0,1:T(8,128)S(1)} %get-tuple-element.600) | copy-start | bytes 49156
  44.3 1043.2 %copy-start.83 = (f32[128,32]{0,1:T(8,128)}, f32[128,32]{0,1:T(8,128)S(1)}, u32[]{:S(2)}) copy-start(f32[128,32]{0,1:T(8,128)S(1)} %get-tuple-element.601) | copy-start | bytes 49156
  44.3 1393.9 %copy-start.85 = (f32[128,32]{0,1:T(8,128)}, f32[128,32]{0,1:T(8,128)S(1)}, u32[]{:S(2)}) copy-start(f32[128,32]{0,1:T(8,128)S(1)} %get-tuple-element.588) | copy-start | bytes 49156
  44.3 1393.9 %copy-start.86 = (f32[128,32]{0,1:T(8,128)}, f32[128,32]{0,1:T(8,128)S(1)}, u32[]{:S(2)}) copy-start(f32[128,32]{0,1:T(8,128)S(1)} %get-tuple-element.589) | copy-start | bytes 49156
  266.4 32.2 all-gather.24.cloned.1.call-start
  275.0 241.0 %all-gather.44.cloned.1.call-start = ((), (), s32[]{:S(2)}) async-start(), calls=%async_computation.60 | async-start | bytes 18874368 | tf_op jit(solution)/shard_map/all_gather | solution.py:357
  275.8 467.9 %all-gather.46.cloned.1.call-start = ((), (), s32[]{:S(2)}) async-start(), calls=%async_computation.61 | async-start | bytes 18874368 | tf_op jit(solution)/shard_map/all_gather | solution.py:358
  276.5 694.6 %all-gather.48.cloned.1.call-start = ((), (), s32[]{:S(2)}) async-start(), calls=%async_computation.62 | async-start | bytes 18874368 | tf_op jit(solution)/shard_map/all_gather | solution.py:359
  277.1 709.9 %reduce-scatter.28.cloned.1.call-start = ((), (), s32[]{:S(2)}) async-start(), calls=%async_computation.27 | async-start | bytes 1572864 | tf_op jit(solution)/shard_map/reduce_scatter | solution.py:185
  300.0 225.5 %copy-start.104 = (f32[128]{0:T(128)}, f32[128]{0:T(128)S(1)}, u32[]{:S(2)}) copy-start(f32[128]{0:T(128)S(1)} %add_rsqrt_fusion.4) | copy-start | bytes 1540
  301.7 442.1 %copy-start.21 = (bf16[128,2048]{1,0:T(8,128)(2,1)}, bf16[128,2048]{1,0:T(8,128)(2,1)S(1)}, u32[]{:S(2)}) copy-start(bf16[128,2048]{1,0:T(8,128)(2,1)S(1)} %multiply_convert_fusion.16) | copy-start | bytes 1572868
  980.3 36.0 %all-gather.26.cloned.1.call-start = ((), (), s32[]{:S(2)}) async-start(), calls=%async_computation.28 | async-start | bytes 1572864 | tf_op jit(solution)/shard_map/all_gather | solution.py:162
  988.9 15.4 collective-permute-start
  1005.2 105.4 %reduce-scatter.30.cloned.1.call-start = ((), (), s32[]{:S(2)}) async-start(), calls=%async_computation.29 | async-start | bytes 1572864 | tf_op jit(solution)/shard_map/reduce_scatter | solution.py:178
  1102.5 20.4 all-gather.28.cloned.1.call-start
  1112.6 46.5 %reduce-scatter.32.cloned.1.call-start = ((), (), s32[]{:S(2)}) async-start(), calls=%async_computation.31 | async-start | bytes 1572864 | tf_op jit(solution)/shard_map/reduce_scatter | solution.py:185
  1149.4 38.8 %all-gather.30.cloned.1.call-start = ((), (), s32[]{:S(2)}) async-start(), calls=%async_computation.32 | async-start | bytes 1572864 | tf_op jit(solution)/shard_map/all_gather | solution.py:162
  1161.0 15.2 collective-permute-start.1
  1177.1 117.5 %reduce-scatter.34.cloned.1.call-start = ((), (), s32[]{:S(2)}) async-start(), calls=%async_computation.33 | async-start | bytes 1572864 | tf_op jit(solution)/shard_map/reduce_scatter | solution.py:178
  1286.4 25.9 all-gather.32.cloned.1.call-start
  1296.6 76.1 %reduce-scatter.38.cloned.1.call-start = ((), (), s32[]{:S(2)}) async-start(), calls=%async_computation.36 | async-start | bytes 786432 | tf_op jit(solution)/shard_map/reduce_scatter | solution.py:240
  1363.4 131.4 %reduce-scatter.40.cloned.1.call-start = ((), (), s32[]{:S(2)}) async-start(), calls=%async_computation.37 | async-start | bytes 589824 | tf_op jit(solution)/shard_map/reduce_scatter | solution.py:269
  1430.9 128.9 %reduce-scatter.42.cloned.1.call-start = ((), (), s32[]{:S(2)}) async-start(), calls=%async_computation.38 | async-start | bytes 589824 | tf_op jit(solution)/shard_map/reduce_scatter | solution.py:272
  1438.1 134.9 %reduce-scatter.44.cloned.1.call-start = ((), (), s32[]{:S(2)}) async-start(), calls=%async_computation.39 | async-start | bytes 1572864 | tf_op jit(solution)/shard_map/reduce_scatter | solution.py:289
  1565.5 75.5 %reduce-scatter.46.cloned.1.call-start = ((), (), s32[]{:S(2)}) async-start(), calls=%async_computation.40 | async-start | bytes 786432 | tf_op jit(solution)/shard_map/reduce_scatter | solution.py:240
  1575.1 10.4 collective-permute-start.2
  1632.6 133.3 %reduce-scatter.48.cloned.1.call-start = ((), (), s32[]{:S(2)}) async-start(), calls=%async_computation.41 | async-start | bytes 589824 | tf_op jit(solution)/shard_map/reduce_scatter | solution.py:269
  1702.0 129.0 %reduce-scatter.50.cloned.1.call-start = ((), (), s32[]{:S(2)}) async-start(), calls=%async_computation.42 | async-start | bytes 589824 | tf_op jit(solution)/shard_map/reduce_scatter | solution.py:272
  1709.2 135.1 %reduce-scatter.52.cloned.1.call-start = ((), (), s32[]{:S(2)}) async-start(), calls=%async_computation.43 | async-start | bytes 1572864 | tf_op jit(solution)/shard_map/reduce_scatter | solution.py:289
  1836.7 74.9 %reduce-scatter.54.cloned.1.call-start = ((), (), s32[]{:S(2)}) async-start(), calls=%async_computation.44 | async-start | bytes 786432 | tf_op jit(solution)/shard_map/reduce_scatter | solution.py:240
  1846.5 10.4 collective-permute-start.3
  1903.3 133.1 %reduce-scatter.56.cloned.1.call-start = ((), (), s32[]{:S(2)}) async-start(), calls=%async_computation.45 | async-start | bytes 589824 | tf_op jit(solution)/shard_map/reduce_scatter | solution.py:269
  1972.5 128.9 %reduce-scatter.58.cloned.1.call-start = ((), (), s32[]{:S(2)}) async-start(), calls=%async_computation.46 | async-start | bytes 589824 | tf_op jit(solution)/shard_map/reduce_scatter | solution.py:272
  1977.4 318.5 %reduce-scatter.36.cloned.1.call-start = ((), (), s32[]{:S(2)}) async-start(), calls=%async_computation.35 | async-start | bytes 1572864 | tf_op jit(solution)/shard_map/reduce_scatter | solution.py:185
  1987.1 340.9 %reduce-scatter.64.cloned.1.call-start = ((), (), s32[]{:S(2)}) async-start(), calls=%async_computation.49 | async-start | bytes 1179648 | tf_op jit(solution)/shard_map/reduce_scatter | solution.py:319
  2040.6 289.0 %reduce-scatter.66.cloned.1.call-start = ((), (), s32[]{:S(2)}) async-start(), calls=%async_computation.50 | async-start | bytes 1179648 | tf_op jit(solution)/shard_map/reduce_scatter | solution.py:322
  2104.6 226.7 %reduce-scatter.60.cloned.1.call-start = ((), (), s32[]{:S(2)}) async-start(), calls=%async_computation.47 | async-start | bytes 1572864 | tf_op jit(solution)/shard_map/reduce_scatter | solution.py:289
  2110.9 239.8 %reduce-scatter.62.cloned.1.call-start = ((), (), s32[]{:S(2)}) async-start(), calls=%async_computation.48 | async-start | bytes 4718592 | tf_op jit(solution)/shard_map/reduce_scatter | solution.py:316
  2117.3 326.0 %reduce-scatter.68.cloned.1.call-start = ((), (), s32[]{:S(2)}) async-start(), calls=%async_computation.51 | async-start | bytes 4718592 | tf_op jit(solution)/shard_map/reduce_scatter | solution.py:325
  2124.2 602.6 %reduce-scatter.70.cloned.1.call-start = ((), (), s32[]{:S(2)}) async-start(), calls=%async_computation.52 | async-start | bytes 18874368 | tf_op jit(solution)/shard_map/reduce_scatter | solution.py:328
  2180.8 828.9 %reduce-scatter.72.cloned.1.call-start = ((), (), s32[]{:S(2)}) async-start(), calls=%async_computation.53 | async-start | bytes 18874368 | tf_op jit(solution)/shard_map/reduce_scatter | solution.py:331
  2237.4 1055.4 %reduce-scatter.74.cloned.1.call-start = ((), (), s32[]{:S(2)}) async-start(), calls=%async_computation.54 | async-start | bytes 18874368 | tf_op jit(solution)/shard_map/reduce_scatter | solution.py:334
  (116 other events, 3047.1 us)
Sparse Core Ops, SparseCore 0:
  10.1 11.7 all-gather.33
  24.0 41.4 all-gather.35
  67.6 40.3 all-gather.37
  110.0 77.3 all-gather.39
  189.2 73.1 all-gather.41
  266.5 6.5 reduce-scatter.25
  275.2 10.2 all-gather.23
  287.6 228.4 all-gather.43
  518.2 225.4 all-gather.45
  745.6 225.4 all-gather.47
  980.4 6.5 reduce-scatter.27
  1005.3 10.9 all-gather.25
  1102.7 7.9 reduce-scatter.29
  1112.7 10.2 all-gather.27
  1149.5 9.5 reduce-scatter.31
  1177.2 10.9 all-gather.29
  1286.6 7.9 reduce-scatter.33
  1296.7 10.2 all-gather.31
  1363.5 9.1 reduce-scatter.37
  1431.0 63.7 reduce-scatter.39
  1498.1 61.5 reduce-scatter.41
  1565.6 7.3 reduce-scatter.43
  1632.7 8.1 reduce-scatter.45
  1702.1 63.7 reduce-scatter.47
  1769.3 61.6 reduce-scatter.49
  1836.8 7.3 reduce-scatter.51
  1903.4 8.1 reduce-scatter.53
  1972.6 63.7 reduce-scatter.55
  2039.7 61.5 reduce-scatter.57
  2104.0 7.3 reduce-scatter.35
  2114.8 65.4 reduce-scatter.63
  2183.7 63.1 reduce-scatter.65
  2249.0 7.3 reduce-scatter.59
  2260.6 90.0 reduce-scatter.61
  2354.9 88.3 reduce-scatter.67
  2446.9 279.8 reduce-scatter.69
  2730.4 279.2 reduce-scatter.71
  3013.5 279.2 reduce-scatter.73
where the time goes:
time: 3320 us; the launch traced here: 3300 us
  waiting for transfers between devices  2230 us (67%)
  matrix products  567 us (17%)
  blocking collectives  266 us (8%)
  local copies, waits for them, and re-layouts  110 us (3%)
  other arithmetic  94.2 us (3%)
    dot_general x63, matrix products, matmul(): return jnp.dot(left, right, preferred_element_type=jnp.float32)  442 us
    reduce_scatter x1, waiting for transfers between devices, reduce_grads(): lax.psum_scatter(pieces[4].astype(jnp.bfloat16), 'dp', scatter_dimension=...  281 us
    reduce_scatter x1, waiting for transfers between devices, reduce_grads(): lax.psum_scatter(pieces[6].astype(jnp.bfloat16), 'dp', scatter_dimension=...  279 us
    reduce_scatter x1, waiting for transfers between devices, reduce_grads(): lax.psum_scatter(pieces[5].astype(jnp.bfloat16), 'dp', scatter_dimension=...  279 us
    all_gather x1, waiting for transfers between devices, shards(): lax.all_gather(w_up[0], 'dp', axis=0, tiled=True)  218 us
    all_gather x1, waiting for transfers between devices, shards(): lax.all_gather(w_down[0], 'dp', axis=1, tiled=True)  217 us
    all_gather x1, waiting for transfers between devices, shards(): lax.all_gather(w_gate[0], 'dp', axis=0, tiled=True)  214 us
    reduce_scatter x3, waiting for transfers between devices, layer_backward(): lax.psum_scatter(value_spread.astype(jnp.bfloat16), 'dp', scatter_dimensi...  184 us
  transfers between devices with their start and end apart: 42, of which 35 were waited for; matrix products, arithmetic and copies ran while one was open for 10% of the time, Pallas kernels for 0%

commit v1 on v0

--- a/solution.py
+++ b/solution.py
@@ -1,8 +1,11 @@
+import functools
 import math
 
 import jax
 import jax.numpy as jnp
 from jax import lax
+from jax.experimental import pallas as pl
+from jax.experimental.pallas import tpu as pltpu
 from jax.sharding import PartitionSpec as P
 
 HEAD_SIZE = 64
@@ -343,7 +346,7 @@
     )
 
 
-def shards(inputs, table, cotangent, wq, wk, wv, wo, w_gate, w_up, w_down, gain_attn, gain_mlp):
+def general_shards(inputs, table, cotangent, wq, wk, wv, wo, w_gate, w_up, w_down, gain_attn, gain_mlp):
     groups = lax.axis_size("dp")
     parts = lax.axis_size("tensor")
     micro_count = inputs.shape[0]
@@ -424,6 +427,669 @@
     )
 
 
+MESH = pl.DeviceIdType.MESH
+
+def ring_place(index, count):
+    return jnp.where(lax.rem(index, 2) == 0, index // 2, count - (index + 1) // 2)
+
+def ring_index(place, count):
+    place = lax.rem(place + 2 * count, count)
+    return jnp.where(place < count // 2, 2 * place, 2 * count - 1 - 2 * place)
+
+def greet(others):
+    barrier = pltpu.get_barrier_semaphore()
+    for other in others:
+        pl.semaphore_signal(barrier, inc=1, device_id=other, device_id_type=MESH)
+    pl.semaphore_wait(barrier, len(others))
+
+def gather_kernel(count, subs, x_ref, o_ref, ring_send, ring_recv, side_send, side_recv, own_sem):
+    rows = x_ref.shape[0]
+    piece = rows // subs
+    me = lax.axis_index("dp")
+    core = lax.axis_index("tensor")
+    place = ring_place(me, count)
+    near = ({"dp": ring_index(place + 1, count)}, {"dp": ring_index(place - 1, count)})
+    side = {"tensor": 1 - core}
+    greet((*near, side))
+    far = count // 2
+
+    def spot(step_from, sub):
+        index = ring_index(place + step_from, count)
+        start = pl.multiple_of((index * 2 + core) * rows, rows) + sub * piece
+        return o_ref.at[pl.ds(pl.multiple_of(start, piece), piece), :]
+
+    own = pltpu.make_async_copy(x_ref, o_ref.at[pl.ds(pl.multiple_of((me * 2 + core) * rows, rows), rows), :], own_sem)
+    own.start()
+    sends = []
+
+    def travels(way, hop, sub):
+        return hop < far or (sub < subs // 2) == (way == 0)
+
+    def ring_copy(way, hop, sub):
+        source = x_ref.at[pl.ds(sub * piece, piece), :] if hop == 1 else spot((1 - hop) if way == 0 else (hop - 1), sub)
+        return pltpu.make_async_remote_copy(source, spot((1 - hop) if way == 0 else (hop - 1), sub),
+            ring_send.at[way, hop - 1, sub], ring_recv.at[way, hop - 1, sub], device_id=near[way], device_id_type=MESH)
+
+    def side_copy(step_from, sub, slot):
+        source = x_ref.at[pl.ds(sub * piece, piece), :] if step_from == 0 else spot(step_from, sub)
+        return pltpu.make_async_remote_copy(source, spot(step_from, sub), side_send.at[slot, sub], side_recv.at[slot, sub],
+            device_id=side, device_id_type=MESH)
+
+    def side_start(copy):
+        copy.start()
+        sends.append(copy)
+
+    order = lambda way: range(subs) if way == 0 else range(subs - 1, -1, -1)
+    for k in range(subs):
+        for way in range(2):
+            sub = list(order(way))[k]
+            copy = ring_copy(way, 1, sub)
+            copy.start(); sends.append(copy)
+    for sub in range(subs):
+        copy = side_copy(0, sub, 0)
+        copy.start(); sends.append(copy)
+    sides = [(0, sub) for sub in range(subs)]
+    for hop in range(1, far + 1):
+        for k in range(subs):
+            for way in range(2):
+                sub = list(order(way))[k]
+                if not travels(way, hop, sub):
+                    continue
+                arrive = pltpu.make_async_remote_copy(spot(-hop if way == 0 else hop, sub), spot(-hop if way == 0 else hop, sub),
+                    ring_send.at[way, hop - 1, sub], ring_recv.at[way, hop - 1, sub], device_id=near[way], device_id_type=MESH)
+                arrive.wait_recv()
+                if hop < far and travels(way, hop + 1, sub):
+                    copy = ring_copy(way, hop + 1, sub)
+                    copy.start(); sends.append(copy)
+                slot = hop if way == 0 or hop == far else count - hop
+                copy = side_copy(-hop if way == 0 else hop, sub, slot)
+                copy.start(); sends.append(copy)
+    for copy in sends:
+        copy.wait_send()
+    for slot in range(count):
+        for sub in range(subs):
+            step_from = -slot if slot <= far else count - slot
+            index = ring_index(place + step_from, count)
+            start = pl.multiple_of((index * 2 + 1 - core) * rows, rows) + sub * piece
+            there = o_ref.at[pl.ds(pl.multiple_of(start, piece), piece), :]
+            pltpu.make_async_remote_copy(there, there, side_send.at[slot, sub], side_recv.at[slot, sub], device_id=side, device_id_type=MESH).wait_recv()
+    own.wait()
+
+def gather_rows(x, count, cid, subs=2):
+    rows, width = x.shape
+    far = count // 2
+    return pl.pallas_call(
+        functools.partial(gather_kernel, count, subs),
+        out_shape=jax.ShapeDtypeStruct((count * 2 * rows, width), x.dtype),
+        in_specs=[pl.BlockSpec(memory_space=pltpu.VMEM)],
+        out_specs=pl.BlockSpec(memory_space=pltpu.VMEM),
+        scratch_shapes=[
+            pltpu.SemaphoreType.DMA((2, far, subs)), pltpu.SemaphoreType.DMA((2, far, subs)),
+            pltpu.SemaphoreType.DMA((count, subs)), pltpu.SemaphoreType.DMA((count, subs)),
+            pltpu.SemaphoreType.DMA],
+        compiler_params=pltpu.CompilerParams(collective_id=cid, has_side_effects=True),
+        name="gather_rows")(x)
+
+def reduce_kernel(count, subs, p_ref, o_ref, side_buf, send_buf, recv_buf, ring_send, ring_recv, side_send, side_recv):
+    rows, width = o_ref.shape
+    piece = rows // subs
+    me = lax.axis_index("dp")
+    core = lax.axis_index("tensor")
+    place = ring_place(me, count)
+    near = ({"dp": ring_index(place + 1, count)}, {"dp": ring_index(place - 1, count)})
+    side = {"tensor": 1 - core}
+    greet((*near, side))
+    far = count // 2
+    steps = [far]
+    for k in range(far - 1, 0, -1):
+        steps += [k, -k]
+    steps += [0]
+    sends = []
+
+    def part(step_to, of_core):
+        index = ring_index(place + step_to, count)
+        return pl.multiple_of((index * 2 + of_core) * rows, rows)
+
+    side_copies = {}
+    for slot, step_to in enumerate(steps):
+        copy = pltpu.make_async_remote_copy(p_ref.at[pl.ds(part(step_to, 1 - core), rows), :], side_buf.at[slot],
+            side_send.at[slot], side_recv.at[slot], device_id=side, device_id_type=MESH)
+        copy.start()
+        side_copies[step_to] = (slot, copy)
+
+    def mine(step_to, sub):
+        slot, _ = side_copies[step_to]
+        start = pl.multiple_of(part(step_to, core) + sub * piece, piece)
+        return p_ref[pl.ds(start, piece), :].astype(jnp.float32) + side_buf[slot, sub * piece:(sub + 1) * piece, :].astype(jnp.float32)
+
+    def travels(way, step, sub):
+        return step > 1 or (sub < subs // 2) == (way == 0)
+
+    def ring_copy(way, step, sub):
+        span = slice(sub * piece, (sub + 1) * piece)
+        return pltpu.make_async_remote_copy(send_buf.at[way, step - 1, span, :], recv_buf.at[way, step - 1, span, :],
+            ring_send.at[way, step - 1, sub], ring_recv.at[way, step - 1, sub], device_id=near[way], device_id_type=MESH)
+
+    order = lambda way: list(range(subs)) if way == 0 else list(range(subs - 1, -1, -1))
+    seen = set()
+    for step in range(1, far + 1):
+        for k in range(subs):
+            for way in range(2):
+                sub = order(way)[k]
+                if not travels(way, step, sub):
+                    continue
+                step_to = far + 1 - step
+                step_to = step_to if way == 0 or step_to == far else -step_to
+                if step_to not in seen:
+                    side_copies[step_to][1].wait_recv()
+                    seen.add(step_to)
+                value = mine(step_to, sub)
+                span = slice(sub * piece, (sub + 1) * piece)
+                if step > 1 and travels(way, step - 1, sub):
+                    ring_copy(way, step - 1, sub).wait_recv()
+                    value = value + recv_buf[way, step - 2, span, :].astype(jnp.float32)
+                send_buf[way, step - 1, span, :] = value.astype(send_buf.dtype)
+                copy = ring_copy(way, step, sub)
+                copy.start()
+                sends.append(copy)
+    side_copies[0][1].wait_recv()
+    for sub in range(subs):
+        span = slice(sub * piece, (sub + 1) * piece)
+        value = mine(0, sub)
+        for way in range(2):
+            ring_copy(way, far, sub).wait_recv()
+            value = value + recv_buf[way, far - 1, span, :].astype(jnp.float32)
+        o_ref[span, :] = value.astype(o_ref.dtype)
+    for copy in sends:
+        copy.wait_send()
+    for _, copy in side_copies.values():
+        copy.wait_send()
+
+def reduce_rows(p, count, cid, subs=2, dtype=jnp.float32):
+    total, width = p.shape
+    rows = total // (2 * count)
+    far = count // 2
+    return pl.pallas_call(
+        functools.partial(reduce_kernel, count, subs),
+        out_shape=jax.ShapeDtypeStruct((rows, width), dtype),
+        in_specs=[pl.BlockSpec(memory_space=pltpu.VMEM)],
+        out_specs=pl.BlockSpec(memory_space=pltpu.VMEM),
+        scratch_shapes=[
+            pltpu.VMEM((count, rows, width), p.dtype),
+            pltpu.VMEM((2, far, rows, width), p.dtype),
+            pltpu.VMEM((2, far, rows, width), p.dtype),
+            pltpu.SemaphoreType.DMA((2, far, subs)), pltpu.SemaphoreType.DMA((2, far, subs)),
+            pltpu.SemaphoreType.DMA((count,)), pltpu.SemaphoreType.DMA((count,))],
+        compiler_params=pltpu.CompilerParams(collective_id=cid, has_side_effects=True),
+        name="reduce_rows")(p)
+
+
+def weight_pieces(source, target, count, heads, srcs, dsts, layer):
+    qkv, wo, gate, up, down, gains = srcs
+    out_qkv, out_wo, out_gu, out_down, out_gains = dsts
+    depth = gate.shape[0]
+    hidden = gate.shape[1] // count
+    q_rows = wo.shape[0] // count
+    kv_rows = (qkv.shape[0] - wo.shape[0]) // 2
+    shared = count * heads // kv_rows
+    cols = pl.ds(pl.multiple_of(source * depth, depth), depth)
+
+    def at(index, size):
+        return pl.ds(pl.multiple_of(index * size, size), size)
+
+    k_from = pl.multiple_of(wo.shape[0] + target // shared * heads, heads)
+    v_from = pl.multiple_of(wo.shape[0] + kv_rows + target // shared * heads, heads)
+    return (
+        (gains, out_gains.at[layer, :, cols]),
+        (qkv.at[at(target, q_rows), :], out_qkv.at[layer, pl.ds(0, q_rows), cols]),
+        (qkv.at[pl.ds(k_from, heads), :], out_qkv.at[layer, pl.ds(q_rows, heads), cols]),
+        (qkv.at[pl.ds(v_from, heads), :], out_qkv.at[layer, pl.ds(q_rows + heads, heads), cols]),
+        (wo.at[at(target, q_rows), :], out_wo.at[layer, :, cols]),
+        (gate.at[:, at(target, hidden)], out_gu.at[layer, cols, pl.ds(0, hidden)]),
+        (up.at[:, at(target, hidden)], out_gu.at[layer, cols, pl.ds(hidden, hidden)]),
+        (down.at[at(target, hidden), :], out_down.at[layer, :, cols]),
+    )
+
+
+KINDS = 8
+
+
+def spread_kernel(count, heads, *refs):
+    srcs = refs[:6]
+    dsts = refs[6:11]
+    send, recv, cross_send, cross_recv, own_sem = refs[11:]
+    me = lax.axis_index("dp")
+    layer = lax.axis_index("section")
+    peers = [lax.rem(me + k, count) for k in range(1, count)]
+    across = {"section": 1 - layer}
+    greet([{"dp": peer} for peer in peers] + [across])
+    waits = []
+    local = []
+    own = weight_pieces(me, me, count, heads, srcs, dsts, layer)
+    for kind in range(KINDS):
+        for k, peer in enumerate(peers):
+            there = weight_pieces(me, peer, count, heads, srcs, dsts, layer)[kind]
+            copy = pltpu.make_async_remote_copy(
+                there[0], there[1], send.at[kind, k], recv.at[kind, k],
+                device_id={"dp": peer}, device_id_type=MESH,
+            )
+            copy.start()
+            waits.append(copy)
+        copy = pltpu.make_async_remote_copy(
+            own[kind][0], own[kind][1], cross_send.at[kind, count - 1], cross_recv.at[kind, count - 1],
+            device_id=across, device_id_type=MESH,
+        )
+        copy.start()
+        waits.append(copy)
+        copy = pltpu.make_async_copy(own[kind][0], own[kind][1], own_sem.at[kind])
+        copy.start()
+        local.append(copy)
+    for kind in range(KINDS):
+        for k in range(count - 1):
+            origin = lax.rem(me + count - 1 - k, count)
+            here = weight_pieces(origin, me, count, heads, srcs, dsts, layer)[kind][1]
+            pltpu.make_async_remote_copy(
+                here, here, send.at[kind, k], recv.at[kind, k],
+                device_id={"dp": origin}, device_id_type=MESH,
+            ).wait_recv()
+            copy = pltpu.make_async_remote_copy(
+                here, here, cross_send.at[kind, k], cross_recv.at[kind, k],
+                device_id=across, device_id_type=MESH,
+            )
+            copy.start()
+            waits.append(copy)
+    for copy in local:
+        copy.wait()
+    for copy in waits:
+        copy.wait_send()
+    for kind in range(KINDS):
+        for k in range(count):
+            origin = lax.rem(me + count - 1 - k, count)
+            there = weight_pieces(origin, me, count, heads, srcs, dsts, 1 - layer)[kind][1]
+            pltpu.make_async_remote_copy(
+                there, there, cross_send.at[kind, k], cross_recv.at[kind, k],
+                device_id=across, device_id_type=MESH,
+            ).wait_recv()
+
+
+def spread_weights(qkv, wo, gate, up, down, gains, count, heads, cid):
+    depth = gate.shape[0]
+    width = depth * count
+    hidden = gate.shape[1] // count
+    q_rows = wo.shape[0] // count
+    shape = lambda *dims: jax.ShapeDtypeStruct((2, *dims), jnp.bfloat16)
+    hbm = pl.BlockSpec(memory_space=pl.ANY)
+    return pl.pallas_call(
+        functools.partial(spread_kernel, count, heads),
+        out_shape=(
+            shape(q_rows + 2 * heads, width),
+            shape(q_rows, width),
+            shape(width, 2 * hidden),
+            shape(hidden, width),
+            jax.ShapeDtypeStruct((2, gains.shape[0], width), gains.dtype),
+        ),
+        in_specs=[hbm] * 6,
+        out_specs=(hbm,) * 5,
+        scratch_shapes=[
+            pltpu.SemaphoreType.DMA((KINDS, count - 1)),
+            pltpu.SemaphoreType.DMA((KINDS, count - 1)),
+            pltpu.SemaphoreType.DMA((KINDS, count)),
+            pltpu.SemaphoreType.DMA((KINDS, count)),
+            pltpu.SemaphoreType.DMA((KINDS,)),
+        ],
+        compiler_params=pltpu.CompilerParams(collective_id=cid, has_side_effects=True),
+        name="spread_weights",
+    )(qkv, wo, gate, up, down, gains)
+
+
+def swap_halves(rows, head):
+    width = rows.shape[1]
+    lane = lax.broadcasted_iota(jnp.int32, rows.shape, 1)
+    half = head // 2
+    return jnp.where(
+        lax.rem(lane, head) < half, pltpu.roll(rows, width - half, 1), pltpu.roll(rows, half, 1)
+    )
+
+
+def low_lanes(shape, head):
+    return lax.broadcasted_iota(jnp.int32, shape, 1) < head
+
+
+def dot(left, right, contract):
+    return lax.dot_general(
+        left, right, (contract, ((), ())), preferred_element_type=jnp.float32
+    )
+
+
+def two_heads(rows, head):
+    low = low_lanes(rows.shape, head)
+    zero = jnp.zeros_like(rows)
+    return jnp.concatenate([jnp.where(low, rows, zero), jnp.where(low, zero, rows)], axis=0)
+
+
+def one_row(rows, head):
+    half = rows.shape[0] // 2
+    return jnp.where(low_lanes((half, rows.shape[1]), head), rows[:half], rows[half:])
+
+
+def triangle(block, keys):
+    row = lax.rem(lax.broadcasted_iota(jnp.int32, (2 * block, keys), 0), block)
+    column = lax.broadcasted_iota(jnp.int32, (2 * block, keys), 1)
+    return column <= row + (keys - block)
+
+
+def attend_kernel(groups, head, slots, qkv_ref, cos_ref, sin_ref, mixed_ref, kept_ref, lse_ref, key2, value2):
+    tokens = qkv_ref.shape[0]
+    block = tokens // groups
+    span = groups // 2
+    wide = 2 * head
+    scale = 1.0 / math.sqrt(head)
+    for spot in range(groups):
+        rows = pl.ds(pl.multiple_of(slots[spot] * block, block), block)
+        cosine = cos_ref[rows, :]
+        sine = sin_ref[rows, :]
+        query = qkv_ref[rows, :wide]
+        query = (query * cosine + swap_halves(query, head) * sine).astype(jnp.bfloat16)
+        pair = qkv_ref[rows, wide:]
+        low = low_lanes(pair.shape, head)
+        pair = jnp.where(low, pair * cosine + swap_halves(pair, head) * sine, pair)
+        turned = pltpu.roll(pair, head, 1)
+        kept_ref[rows, :wide] = query
+        kept_ref[rows, wide:] = pair.astype(jnp.bfloat16)
+        here = slice(spot * block, (spot + 1) * block)
+        key2[here, :] = jnp.where(low, pair, turned).astype(jnp.bfloat16)
+        value2[here, :] = jnp.where(low, turned, pair).astype(jnp.bfloat16)
+    for spot in range(groups):
+        first = spot // span * span * block
+        keys = (spot % span + 1) * block
+        rows = pl.ds(pl.multiple_of(slots[spot] * block, block), block)
+        query = two_heads(kept_ref[rows, :wide], head)
+        score = dot(query, key2[first : first + keys, :], ((1,), (1,))) * scale
+        power = jnp.where(triangle(block, keys), jnp.exp(score), 0.0)
+        total = jnp.sum(power, axis=1, keepdims=True)
+        lse = jnp.log(total)
+        probs = jnp.where(triangle(block, keys), jnp.exp(score - lse), 0.0).astype(jnp.bfloat16)
+        mixed = dot(probs, value2[first : first + keys, :], ((1,), (0,)))
+        mixed_ref[rows, :] = one_row(mixed, head).astype(jnp.bfloat16)
+        lse_ref[spot] = lse
+
+
+def attend_blocks(slots, qkv, cosine, sine, groups, head):
+    tokens = qkv.shape[0]
+    block = tokens // groups
+    vmem = pl.BlockSpec(memory_space=pltpu.VMEM)
+    return pl.pallas_call(
+        functools.partial(attend_kernel, groups, head),
+        out_shape=(
+            jax.ShapeDtypeStruct((tokens, 2 * head), jnp.bfloat16),
+            jax.ShapeDtypeStruct((tokens, 4 * head), jnp.bfloat16),
+            jax.ShapeDtypeStruct((groups, 2 * block, 1), jnp.float32),
+        ),
+        in_specs=[pl.BlockSpec(memory_space=pltpu.SMEM), vmem, vmem, vmem],
+        out_specs=(vmem, vmem, vmem),
+        scratch_shapes=[
+            pltpu.VMEM((tokens, 2 * head), jnp.bfloat16),
+            pltpu.VMEM((tokens, 2 * head), jnp.bfloat16),
+        ],
+        name="attend_blocks",
+    )(slots, qkv, cosine, sine)
+
+
+def attend_back_kernel(
+    groups, head, slots, grad_ref, kept_ref, lse_ref, cos_ref, sin_ref, out_ref, key2, value2, key_sum, value_sum
+):
+    tokens = kept_ref.shape[0]
+    block = tokens // groups
+    span = groups // 2
+    wide = 2 * head
+    scale = 1.0 / math.sqrt(head)
+    for spot in range(groups):
+        rows = pl.ds(pl.multiple_of(slots[spot] * block, block), block)
+        pair = kept_ref[rows, wide:].astype(jnp.float32)
+        low = low_lanes(pair.shape, head)
+        turned = pltpu.roll(pair, head, 1)
+        here = slice(spot * block, (spot + 1) * block)
+        key2[here, :] = jnp.where(low, pair, turned).astype(jnp.bfloat16)
+        value2[here, :] = jnp.where(low, turned, pair).astype(jnp.bfloat16)
+    for spot in range(groups - 1, -1, -1):
+        place = spot % span
+        first = spot // span * span * block
+        keys = (place + 1) * block
+        rows = pl.ds(pl.multiple_of(slots[spot] * block, block), block)
+        query = two_heads(kept_ref[rows, :wide], head)
+        grad = two_heads(grad_ref[rows, :], head)
+        key = key2[first : first + keys, :]
+        value = value2[first : first + keys, :]
+        score = dot(query, key, ((1,), (1,))) * scale
+        probs = jnp.where(triangle(block, keys), jnp.exp(score - lse_ref[spot]), 0.0)
+        prob_grad = dot(grad, value, ((1,), (1,)))
+        rowdot = jnp.sum(probs * prob_grad, axis=1, keepdims=True)
+        score_grad = (probs * (prob_grad - rowdot) * scale).astype(jnp.bfloat16)
+        value_part = dot(probs.astype(jnp.bfloat16), grad, ((0,), (0,)))
+        key_part = dot(score_grad, query, ((0,), (0,)))
+        if place == span - 1:
+            value_sum[first : first + keys, :] = value_part
+            key_sum[first : first + keys, :] = key_part
+        else:
+            value_sum[first : first + keys, :] += value_part
+            key_sum[first : first + keys, :] += key_part
+        query_grad = one_row(dot(score_grad, key, ((1,), (0,))), head)
+        query_grad = query_grad * cos_ref[rows, :] - swap_halves(query_grad, head) * sin_ref[rows, :]
+        out_ref[rows, :wide] = query_grad.astype(jnp.bfloat16)
+    for spot in range(groups):
+        rows = pl.ds(pl.multiple_of(slots[spot] * block, block), block)
+        here = slice(spot * block, (spot + 1) * block)
+        key = key_sum[here, :]
+        key = key + pltpu.roll(key, head, 1)
+        key = key * cos_ref[rows, :] - swap_halves(key, head) * sin_ref[rows, :]
+        value = value_sum[here, :]
+        value = value + pltpu.roll(value, head, 1)
+        low = low_lanes(key.shape, head)
+        out_ref[rows, wide:] = jnp.where(low, key, value).astype(jnp.bfloat16)
+
+
+def attend_blocks_back(slots, grad, kept, lse, cosine, sine, groups, head):
+    tokens = kept.shape[0]
+    vmem = pl.BlockSpec(memory_space=pltpu.VMEM)
+    return pl.pallas_call(
+        functools.partial(attend_back_kernel, groups, head),
+        out_shape=jax.ShapeDtypeStruct((tokens, 4 * head), jnp.bfloat16),
+        in_specs=[pl.BlockSpec(memory_space=pltpu.SMEM)] + [vmem] * 5,
+        out_specs=vmem,
+        scratch_shapes=[
+            pltpu.VMEM((tokens, 2 * head), jnp.bfloat16),
+            pltpu.VMEM((tokens, 2 * head), jnp.bfloat16),
+            pltpu.VMEM((tokens, 2 * head), jnp.float32),
+            pltpu.VMEM((tokens, 2 * head), jnp.float32),
+        ],
+        name="attend_blocks_back",
+    )(slots, grad, kept, lse, cosine, sine)
+
+
+def rope_tables(table_row, block, head):
+    groups = table_row.shape[0]
+    place = table_row % (groups // 2)
+    positions = (place[:, None] * block + jnp.arange(block, dtype=jnp.int32)).reshape(-1)
+    angle = positions.astype(jnp.float32)[:, None] * rope_frequencies(head)[None, :]
+    cosine = jnp.cos(angle)
+    sine = jnp.sin(angle)
+    return (
+        jnp.concatenate([cosine] * 4, axis=1),
+        jnp.concatenate([-sine, sine] * 2, axis=1),
+    )
+
+
+def matmul_nt(left, right):
+    return dot(left, right, ((1,), (1,)))
+
+
+def matmul_tn(left, right):
+    return dot(left, right, ((0,), (0,)))
+
+
+def section_swap(value):
+    return lax.ppermute(value, "section", [(0, 1), (1, 0)])
+
+
+def section_move(value, source):
+    return lax.ppermute(value, "section", [(source, 1 - source)])
+
+
+def fast_forward(rows, weights, layer, tools):
+    qkv_w, wo_w, gu_w, down_w, gain_attn, gain_mlp = [w[layer] for w in weights]
+    count, slots, cosine, sine, head = tools
+    unit1, inverse1 = norm_stats(rows)
+    normed1 = gather_rows((unit1 * gain_attn).astype(jnp.bfloat16), count, 1)
+    qkv = matmul_nt(normed1, qkv_w)
+    mixed, kept, lse = attend_blocks(slots, qkv, cosine, sine, count, head)
+    second = rows + reduce_rows(matmul(mixed, wo_w).astype(jnp.bfloat16), count, 2)
+    unit2, inverse2 = norm_stats(second)
+    normed2 = gather_rows((unit2 * gain_mlp).astype(jnp.bfloat16), count, 1)
+    gate_up = matmul(normed2, gu_w)
+    gate, upper = jnp.split(gate_up, 2, axis=1)
+    hidden = (jax.nn.silu(gate) * upper).astype(jnp.bfloat16)
+    result = second + reduce_rows(matmul(hidden, down_w).astype(jnp.bfloat16), count, 2)
+    return result, (unit1, inverse1, normed1, kept, lse, mixed, unit2, inverse2, normed2, gate_up, hidden)
+
+
+def fast_backward(grad_rows, context, weights, layer, tools):
+    qkv_w, wo_w, gu_w, down_w, gain_attn, gain_mlp = [w[layer] for w in weights]
+    count, slots, cosine, sine, head = tools
+    unit1, inverse1, normed1, kept, lse, mixed, unit2, inverse2, normed2, gate_up, hidden = context
+    gate, upper = jnp.split(gate_up, 2, axis=1)
+    out_grad = gather_rows(grad_rows.astype(jnp.bfloat16), count, 1)
+    hidden_grad = matmul_nt(out_grad, down_w)
+    grad_down = matmul_tn(hidden, out_grad).astype(jnp.bfloat16)
+    sigma = jax.nn.sigmoid(gate)
+    gate_grad = (hidden_grad * upper * sigma * (1.0 + gate * (1.0 - sigma))).astype(jnp.bfloat16)
+    up_grad = (hidden_grad * gate * sigma).astype(jnp.bfloat16)
+    gu_grad = jnp.concatenate([gate_grad, up_grad], axis=1)
+    grad_gu = matmul_tn(normed2, gu_grad).astype(jnp.bfloat16)
+    normed2_grad = reduce_rows(matmul_nt(gu_grad, gu_w).astype(jnp.bfloat16), count, 2)
+    second_part, gain_mlp_part = norm_back(normed2_grad, unit2, inverse2, gain_mlp)
+    second_grad = grad_rows + second_part
+    attn_grad = gather_rows(second_grad.astype(jnp.bfloat16), count, 1)
+    grad_wo = matmul_tn(mixed, attn_grad).astype(jnp.bfloat16)
+    mixed_grad = matmul_nt(attn_grad, wo_w).astype(jnp.bfloat16)
+    qkv_grad = attend_blocks_back(slots, mixed_grad, kept, lse, cosine, sine, count, head)
+    grad_qkv = matmul_tn(qkv_grad, normed1).astype(jnp.bfloat16)
+    normed1_grad = reduce_rows(matmul(qkv_grad, qkv_w).astype(jnp.bfloat16), count, 2)
+    first_part, gain_attn_part = norm_back(normed1_grad, unit1, inverse1, gain_attn)
+    return second_grad + first_part, (grad_gu, grad_down, grad_wo, grad_qkv), (gain_attn_part, gain_mlp_part)
+
+
+def fast_shards(inputs, table, cotangent, wq, wk, wv, wo, w_gate, w_up, w_down, gain_attn, gain_mlp):
+    count = lax.axis_size("dp")
+    parts = lax.axis_size("tensor")
+    head = HEAD_SIZE
+    section = lax.axis_index("section")
+    first_section = section == 0
+    block = inputs.shape[1] * parts
+    depth = wq.shape[1]
+    width = depth * count
+    q_rows = wo.shape[1] // count
+    hidden = w_gate.shape[2] // count
+
+    qkv_t = jnp.concatenate([wq[0], wk[0], wv[0]], axis=1).T
+    gains = jnp.concatenate([gain_attn, gain_mlp], axis=0).astype(jnp.float32)
+    gains = jnp.concatenate([gains] * 4, axis=0)
+    qkv_w, wo_w, gu_w, down_w, all_gains = spread_weights(
+        qkv_t, wo[0], w_gate[0], w_up[0], w_down[0], gains, count, head, 0
+    )
+    weights = (qkv_w, wo_w, gu_w, down_w, all_gains[:, 0], all_gains[:, 1])
+
+    rows = lax.dynamic_index_in_dim(inputs, section, 0, keepdims=False)
+    given = lax.dynamic_index_in_dim(cotangent, section, 0, keepdims=False)
+    table_row = lax.dynamic_index_in_dim(table, section, 0, keepdims=False)
+    slot_ids = jnp.arange(count, dtype=jnp.int32)
+    slots = jnp.sum(jnp.where(table_row[None, :] == slot_ids[:, None], slot_ids[None, :], 0), axis=1)
+    cosine, sine = rope_tables(table_row, block, head)
+    tools = (count, slots, cosine, sine, head)
+
+    result0, context0 = fast_forward(rows, weights, 0, tools)
+    result1, context1 = fast_forward(result0, weights, 1, tools)
+    din1, grads1, gains1 = fast_backward(given, context1, weights, 1, tools)
+    moved1 = [section_move(g, 0) for g in grads1]
+    din0, grads0, gains0 = fast_backward(din1, context0, weights, 0, tools)
+    moved0 = [section_move(g, 1) for g in grads0]
+
+    def both(at0, at1):
+        other = section_swap(jnp.where(first_section, at1, at0))
+        return jnp.where(
+            first_section, jnp.stack([at0, other]), jnp.stack([other, at1])
+        )[None]
+
+    outputs = both(result0, result1)
+    input_grad = both(din0, din1)
+
+    def total(at):
+        mine = jnp.where(first_section, grads0[at], grads1[at]).astype(jnp.float32)
+        theirs = jnp.where(first_section, moved0[at], moved1[at]).astype(jnp.float32)
+        return (mine + theirs).astype(jnp.bfloat16)
+
+    gu_total, down_total, wo_total, qkv_total = [total(at) for at in range(4)]
+    cut = lambda value: value.reshape(value.shape[0], count, depth).transpose(1, 0, 2)
+    exchange = lambda value: lax.all_to_all(value, "dp", split_axis=0, concat_axis=0, tiled=True)
+    gu_own = exchange(gu_total.reshape(count, depth, 2 * hidden))
+    down_own = exchange(cut(down_total))
+    wo_own = exchange(cut(wo_total))
+    qkv_own = exchange(cut(qkv_total))
+    grad_gate = gu_own[:, :, :hidden].transpose(1, 0, 2).reshape(depth, -1).astype(jnp.float32)
+    grad_up = gu_own[:, :, hidden:].transpose(1, 0, 2).reshape(depth, -1).astype(jnp.float32)
+    grad_down = down_own.reshape(-1, depth).astype(jnp.float32)
+    grad_wo = wo_own.reshape(-1, depth).astype(jnp.float32)
+    grad_wq = qkv_own[:, :q_rows].reshape(-1, depth).astype(jnp.float32).T
+    shared = count * head // wk.shape[2]
+    joined = qkv_own[:, q_rows:].astype(jnp.float32).reshape(count // shared, shared, 2, head, depth)
+    joined = jnp.sum(joined, axis=1)
+    grad_wk = joined[:, 0].reshape(-1, depth).T
+    grad_wv = joined[:, 1].reshape(-1, depth).T
+
+    gain_rows = jnp.stack(
+        [jnp.stack(gains0), jnp.stack(gains1)]
+    ).reshape(2, 2, count * parts, -1).transpose(0, 2, 1, 3)
+    gain_piece = gain_rows.shape[-1]
+    gain_rows = gain_rows.reshape(2 * count * parts, 2 * gain_piece)
+    gain_sums = lax.psum_scatter(
+        gain_rows, ("section", "dp", "tensor"), scatter_dimension=0, tiled=True
+    ).reshape(2, gain_piece)
+    return (
+        outputs,
+        input_grad,
+        grad_wq[None],
+        grad_wk[None],
+        grad_wv[None],
+        grad_wo[None],
+        grad_gate[None],
+        grad_up[None],
+        grad_down[None],
+        gain_sums[:1],
+        gain_sums[1:],
+    )
+
+
+def fits(mesh, inputs, table, cotangent, wq, wk, wv, wo, w_gate, w_up, w_down, gain_attn, gain_mlp):
+    sections, count, parts = (mesh.shape[axis] for axis in ("section", "dp", "tensor"))
+    head = HEAD_SIZE
+    if sections != 2 or parts != 2 or inputs.shape[0] != sections or count % 4:
+        return False
+    devices = count * parts
+    queries, keys = wq.shape[2] // head, wk.shape[2] // head
+    if queries != 2 * devices or devices % keys or keys % parts or 4 * head != 256:
+        return False
+    return (
+        wq.shape[1] % (128 * count) == 0
+        and w_gate.shape[2] % (128 * devices) == 0
+        and inputs.shape[1] % (64 * devices) == 0
+    )
+
+
+def shards(mesh, whole, *args):
+    if fits(mesh, *whole):
+        return fast_shards(*args)
+    return general_shards(*args)
+
+
 def solution(mesh):
     in_specs = (
         P(None, ("dp", "tensor"), None),
@@ -452,4 +1118,14 @@
         P("section", ("dp", "tensor")),
         P("section", ("dp", "tensor")),
     )
-    return jax.shard_map(shards, mesh=mesh, in_specs=in_specs, out_specs=out_specs, check_vma=False)
+
+    def step(*args):
+        return jax.shard_map(
+            functools.partial(shards, mesh, args),
+            mesh=mesh,
+            in_specs=in_specs,
+            out_specs=out_specs,
+            check_vma=False,
+        )(*args)
+
+    return step

time: 3320 us -> 1190 us (0.36)
  waiting for transfers between devices: 2230 us -> 90.3 us
  Pallas kernels: 0 us -> 782 us
  matrix products: 567 us -> 121 us
  blocking collectives: 266 us -> 44.5 us
  local copies, waits for them, and re-layouts: 110 us -> 42.8 us
  other arithmetic: 94.2 us -> 59 us
    reduce_scatter x25 -> x0, waiting for transfers between devices: 1370 us -> none  [the longest x1 281 us: reduce_grads(): lax.psum_scatter(pieces[4].astype(jnp.bfloat16), 'dp', scatter_dimension=...]
    all_gather x13 -> x0, waiting for transfers between devices: 815 us -> none  [the longest x1 218 us: shards(): lax.all_gather(w_up[0], 'dp', axis=0, tiled=True)]
    pallas_call x0 -> x21, Pallas kernels: none -> 782 us  [the longest x8 312 us: reduce_rows(): pl.pallas_call(functools.partial(reduce_kernel, count, subs), out_shape=j...]
    dot_general x63 -> x8, matrix products: 442 us -> 42.5 us  [matmul(): return jnp.dot(left, right, preferred_element_type=jnp.float32)]
    all_gather x14 -> x0, blocking collectives: 240 us -> none  [the longest x3 97.5 us: layer_forward(): lax.all_gather(value_rows, 'dp', axis=0, tiled=True)]
    dot_general x84 -> x16, matrix products: 125 us -> 78.7 us  [dot(): lax.dot_general(left, right, (contract, ((), ())), preferred_element_type...]
    ppermute x4 -> x10, waiting for transfers between devices: 41.2 us -> 82.7 us  [the longest x8 82.7 us: section_move(): return lax.ppermute(value, 'section', [(source, 1 - source)])]
  transfers between devices with their start and end apart: 42 -> 14, of which waited for: 35 -> 4; matrix products, arithmetic and copies ran while one was open for 10% -> 10% of each run, Pallas kernels for 0% -> 27%
where the time goes in v1:
time: 1190 us; the launch traced here: 1180 us
  Pallas kernels  782 us (66%)
  matrix products  121 us (10%)
  waiting for transfers between devices  90.3 us (8%)
  other arithmetic  59 us (5%)
  blocking collectives  44.5 us (4%)
  local copies, waits for them, and re-layouts  42.8 us (4%)
  starting transfers between devices  40.5 us (3%)
    pallas_call x8, Pallas kernels, reduce_rows(): pl.pallas_call(functools.partial(reduce_kernel, count, subs), out_shape=j...  312 us
    pallas_call x8, Pallas kernels, gather_rows(): pl.pallas_call(functools.partial(gather_kernel, count, subs), out_shape=j...  237 us
    pallas_call x1, Pallas kernels, spread_weights(): pl.pallas_call(functools.partial(spread_kernel, count, heads), out_shape=...  208 us
    ppermute x8, waiting for transfers between devices, section_move(): return lax.ppermute(value, 'section', [(source, 1 - source)])  82.7 us
    dot_general x16, matrix products, dot(): lax.dot_general(left, right, (contract, ((), ())), preferred_element_type...  78.7 us
    unnamed x1, blocking collectives  44.5 us
    dot_general x8, matrix products, matmul(): return jnp.dot(left, right, preferred_element_type=jnp.float32)  42.5 us
  transfers between devices with their start and end apart: 14, of which 4 were waited for; matrix products, arithmetic and copies ran while one was open for 10% of the time, Pallas kernels for 27%

profile of v1, /device:TPU:0, one launch (start us, length us, event | category | flops | bytes accessed | tf_op | source)
XLA Modules:
  0.0 1182.4 jit_solution(11740863662471647306)
XLA Ops:
  9.8 29.7 %gather_rows.12 = bf16[1024,2048]{1,0:T(8,128)(2,1)} custom-call(bf16[64,2048]{1,0:T(8,128)(2,1)} %bitcast_convert_fusion.3.x_ref), custom_call_target="tpu_custom_call" | custom-call | tf_op jit(solution)/shard_map/gather_rows/pallas_call | solution.py:521
  40.5 207.8 %spread_weights.1 = (bf16[2,256,2048]{2,1,0:T(8,128)(2,1)}, bf16[2,128,2048]{2,1,0:T(8,128)(2,1)}, bf16[2,2048,1024]{2,1,0:T(8,128)(2,1)}, bf16[2,512,2048]{2,1,0:T(8,128)(2,1)}, f32[2,8,2048]{2,1,0:T(8,128)}) custom-call(bf16[1536,256]{1,0:T(8,128)(2,1)} %maximum_bitcast_fusion.refs_0_, bf16[1024,256]{1,0:T(8,128)(2,1)} %bitcast.205, ...), custom_call_target="tpu_custom_call" | custom-call | tf_op jit(solution)/shard_map/spread_weights/pallas_call | solution.py:722
  250.1 43.2 %gather_rows.8 = bf16[1024,2048]{1,0:T(8,128)(2,1)} custom-call(bf16[64,2048]{1,0:T(8,128)(2,1)} %multiply_convert_fusion.9.x_ref), custom_call_target="tpu_custom_call" | custom-call | tf_op jit(solution)/shard_map/gather_rows/pallas_call | solution.py:521
  295.3 4.8 fusion.32.qkv_ref
  301.9 5.6 attend_blocks.2
  311.7 29.2 %reduce_rows.8 = f32[64,2048]{1,0:T(8,128)} custom-call(bf16[1024,2048]{1,0:T(8,128)(2,1)} %convolution_convert_fusion.5.p_ref), custom_call_target="tpu_custom_call" | custom-call | tf_op jit(solution)/shard_map/reduce_rows/pallas_call | solution.py:612
  342.9 27.1 %gather_rows.9 = bf16[1024,2048]{1,0:T(8,128)(2,1)} custom-call(bf16[64,2048]{1,0:T(8,128)(2,1)} %multiply_convert_fusion.8.x_ref), custom_call_target="tpu_custom_call" | custom-call | tf_op jit(solution)/shard_map/gather_rows/pallas_call | solution.py:521
  370.0 7.9 fusion.6
  386.9 29.0 %reduce_rows.9 = f32[64,2048]{1,0:T(8,128)} custom-call(bf16[1024,2048]{1,0:T(8,128)(2,1)} %convolution_convert_fusion.3.p_ref), custom_call_target="tpu_custom_call" | custom-call | tf_op jit(solution)/shard_map/reduce_rows/pallas_call | solution.py:612
  418.2 27.7 %gather_rows.10 = bf16[1024,2048]{1,0:T(8,128)(2,1)} custom-call(bf16[64,2048]{1,0:T(8,128)(2,1)} %multiply_convert_fusion.7.x_ref), custom_call_target="tpu_custom_call" | custom-call | tf_op jit(solution)/shard_map/gather_rows/pallas_call | solution.py:521
  445.8 4.5 fusion.29.qkv_ref
  450.3 5.6 attend_blocks.3
  460.3 29.0 %reduce_rows.10 = f32[64,2048]{1,0:T(8,128)} custom-call(bf16[1024,2048]{1,0:T(8,128)(2,1)} %convolution_convert_fusion.4.p_ref), custom_call_target="tpu_custom_call" | custom-call | tf_op jit(solution)/shard_map/reduce_rows/pallas_call | solution.py:612
  491.3 27.2 %gather_rows.11 = bf16[1024,2048]{1,0:T(8,128)(2,1)} custom-call(bf16[64,2048]{1,0:T(8,128)(2,1)} %multiply_convert_fusion.6.x_ref), custom_call_target="tpu_custom_call" | custom-call | tf_op jit(solution)/shard_map/gather_rows/pallas_call | solution.py:521
  518.6 7.9 fusion.2
  537.3 6.1 fusion.11.p_ref
  543.4 29.2 %reduce_rows.12 = f32[64,2048]{1,0:T(8,128)} custom-call(bf16[1024,2048]{1,0:T(8,128)(2,1)} %fusion.11.p_ref), custom_call_target="tpu_custom_call" | custom-call | tf_op jit(solution)/shard_map/reduce_rows/pallas_call | solution.py:612
  576.2 27.3 %gather_rows.13 = bf16[1024,2048]{1,0:T(8,128)(2,1)} custom-call(bf16[64,2048]{1,0:T(8,128)(2,1)} %get-tuple-element.91.x_ref), custom_call_target="tpu_custom_call" | custom-call | tf_op jit(solution)/shard_map/gather_rows/pallas_call | solution.py:521
  611.9 7.6 attend_blocks_back.2
  619.5 4.6 convolution_convert_fusion.10
  626.7 4.6 convolution_convert_fusion.1.p_ref
  631.4 4.4 convolution_convert_fusion.2.p_ref
  635.8 29.3 %reduce_rows.13 = f32[64,2048]{1,0:T(8,128)} custom-call(bf16[1024,2048]{1,0:T(8,128)(2,1)} %convolution_convert_fusion.1.p_ref), custom_call_target="tpu_custom_call" | custom-call | tf_op jit(solution)/shard_map/reduce_rows/pallas_call | solution.py:612
  666.4 29.1 %reduce_rows.11 = f32[64,2048]{1,0:T(8,128)} custom-call(bf16[1024,2048]{1,0:T(8,128)(2,1)} %convolution_convert_fusion.2.p_ref), custom_call_target="tpu_custom_call" | custom-call | tf_op jit(solution)/shard_map/reduce_rows/pallas_call | solution.py:612
  698.1 27.3 %gather_rows.14 = bf16[1024,2048]{1,0:T(8,128)(2,1)} custom-call(bf16[64,2048]{1,0:T(8,128)(2,1)} %get-tuple-element.112.x_ref), custom_call_target="tpu_custom_call" | custom-call | tf_op jit(solution)/shard_map/gather_rows/pallas_call | solution.py:521
  725.4 6.0 convolution_convert_fusion.9
  733.4 4.7 multiply_convert_fusion.1
  739.1 6.1 fusion.8.p_ref
  745.2 29.4 %reduce_rows.14 = f32[64,2048]{1,0:T(8,128)} custom-call(bf16[1024,2048]{1,0:T(8,128)(2,1)} %fusion.8.p_ref), custom_call_target="tpu_custom_call" | custom-call | tf_op jit(solution)/shard_map/reduce_rows/pallas_call | solution.py:612
  778.1 26.9 %gather_rows.15 = bf16[1024,2048]{1,0:T(8,128)(2,1)} custom-call(bf16[64,2048]{1,0:T(8,128)(2,1)} %get-tuple-element.87.x_ref), custom_call_target="tpu_custom_call" | custom-call | tf_op jit(solution)/shard_map/gather_rows/pallas_call | solution.py:521
  812.6 7.6 attend_blocks_back.3
  820.2 4.6 convolution_convert_fusion.11
  830.9 9.4 convolution_convert_fusion.7
  841.9 12.6 %collective-permute-done.2 = bf16[256,2048]{1,0:T(8,128)(2,1)} collective-permute-done((bf16[256,2048]{1,0:T(8,128)(2,1)}, bf16[256,2048]{1,0:T(8,128)(2,1)}, u32[]{:S(2)}, u32[]{:S(2)}) %collective-permute-start.2) | collective-permute-done | bytes 1048608 | tf_op jit(solution)/shard_map/ppermute | solution.py:935
  862.2 9.1 convolution_convert_fusion.6
  880.2 7.6 all-to-all-done
  892.4 51.7 %collective-permute-done.6 = bf16[2048,1024]{1,0:T(8,128)(2,1)} collective-permute-done((bf16[2048,1024]{1,0:T(8,128)(2,1)}, bf16[2048,1024]{1,0:T(8,128)(2,1)}, u32[]{:S(2)}, u32[]{:S(2)}) %collective-permute-start.6) | collective-permute-done | bytes 4194336 | tf_op jit(solution)/shard_map/ppermute | solution.py:935
  944.0 18.5 %collective-permute-done.7 = bf16[2048,1024]{1,0:T(8,128)(2,1)} collective-permute-done((bf16[2048,1024]{1,0:T(8,128)(2,1)}, bf16[2048,1024]{1,0:T(8,128)(2,1)}, u32[]{:S(2)}, u32[]{:S(2)}) %collective-permute-start.7) | collective-permute-done | bytes 4194336 | tf_op jit(solution)/shard_map/ppermute | solution.py:935
  962.5 7.6 add_convert_fusion
  970.2 6.0 all-to-all-start.2
  978.7 4.7 convolution_convert_fusion.p_ref
  983.4 107.3 %reduce_rows.15 = f32[64,2048]{1,0:T(8,128)} custom-call(bf16[1024,2048]{1,0:T(8,128)(2,1)} %convolution_convert_fusion.p_ref), custom_call_target="tpu_custom_call" | custom-call | tf_op jit(solution)/shard_map/reduce_rows/pallas_call | solution.py:612
  1097.2 44.5 %all-reduce = f32[32,256]{1,0:T(8,128)S(1)} all-reduce(f32[32,256]{1,0:T(8,128)S(1)} %bitcast.220), channel_id=2, replica_groups=mesh['section'=2,'dp'=8,'tensor'=2] {'section','dp','tensor'}, use_global_device_ids=true, to_apply=%region_14.15.clone | all-reduce | flops 8192 | bytes 65536
  1156.2 4.9 convert_bitcast_fusion
  1161.1 4.4 copy.80
  1165.5 4.9 reshape.360
  1170.4 6.6 copy.79
  1177.0 4.9 reshape.359
  (169 shorter events, 134.8 us)
Async XLA Ops:
  1.9 247.4 %copy-start.22 = (f32[64]{0:T(128)}, f32[64]{0:T(128)S(1)}, u32[]{:S(2)}) copy-start(f32[64]{0:T(128)S(1)} %add_rsqrt_fusion.3) | copy-start | bytes 772
  40.5 208.8 %copy-start.2 = (f32[2,64,2048]{2,1,0:T(8,128)S(1)}, f32[2,64,2048]{2,1,0:T(8,128)}, u32[]{:S(2)}) copy-start(f32[2,64,2048]{2,1,0:T(8,128)} %param.12) | copy-start | bytes 3145732
  300.0 7.4 copy-start.16
  377.9 2.0 copy-start.4
  379.9 2.6 copy-start.24
  380.6 1.0 copy-start.17
  415.9 29.9 %copy-start.13 = (bf16[2,256,2048]{2,1,0:T(8,128)(2,1)S(1)}, bf16[2,256,2048]{2,1,0:T(8,128)(2,1)}, u32[]{:S(2)}) copy-start(bf16[2,256,2048]{2,1,0:T(8,128)(2,1)} %get-tuple-element.23) | copy-start | bytes 6291460
  518.6 8.0 copy-start.6
  518.6 8.0 copy-start.25
  518.6 18.7 %slice-start = ((s8[8388608]{0:T(1024)(128)(4,1)}), s8[4194304]{0:T(1024)(128)(4,1)S(1)}, s32[]{:S(2)}) async-start(s8[8388608]{0:T(1024)(128)(4,1)} %bitcast.226), calls=%async_computation.4 | async-start | bytes 8388608
  526.5 10.8 slice-start.1
  529.6 3.7 copy-start.27
  529.7 7.7 copy-start.29
  529.7 7.7 copy-start.31
  533.3 341.4 %collective-permute-start.9 = (bf16[512,2048]{1,0:T(8,128)(2,1)}, bf16[512,2048]{1,0:T(8,128)(2,1)}, u32[]{:S(2)}, u32[]{:S(2)}) collective-permute-start(bf16[512,2048]{1,0:T(8,128)(2,1)} %convolution_convert_fusion.8), channel_id=1, source_target_pairs={{0,16},{1,17},{2,18},{3,19},{4,20},{5,21},{6,22},{7,23},{8,24},{9,... | collective-permute-start | bytes 6291464 | tf_op jit(solution)/shard_map/ppermute | solution.py:935
  543.4 30.6 %copy-start.19 = (f32[2,64,2048]{2,1,0:T(8,128)S(1)}, f32[2,64,2048]{2,1,0:T(8,128)}, u32[]{:S(2)}) copy-start(f32[2,64,2048]{2,1,0:T(8,128)} %param.14) | copy-start | bytes 3145732
  572.7 30.8 %copy-start.15 = (bf16[1024,128]{1,0:T(8,128)(2,1)S(1)}, bf16[1024,128]{1,0:T(8,128)(2,1)}, u32[]{:S(2)}) copy-start(bf16[1024,128]{1,0:T(8,128)(2,1)} %get-tuple-element.28) | copy-start | bytes 786436
  603.5 5.4 copy-start.1
  606.6 218.2 %collective-permute-start.5 = (bf16[128,2048]{1,0:T(8,128)(2,1)S(1)}, bf16[128,2048]{1,0:T(8,128)(2,1)}, u32[]{:S(2)}, u32[]{:S(2)}) collective-permute-start(bf16[128,2048]{1,0:T(8,128)(2,1)S(1)} %convolution_convert_fusion.12), channel_id=1, source_target_pairs={{0,16},{1,17},{2,18},{3,19},{4,20},{5,21},{6,22},{7,23},{8,24},{9,... | collective-permute-start | bytes 1572872 | tf_op jit(solution)/shard_map/ppermute | solution.py:935
  619.5 7.2 copy-start.10
  624.1 217.8 %collective-permute-start.3 = (bf16[256,2048]{1,0:T(8,128)(2,1)}, bf16[256,2048]{1,0:T(8,128)(2,1)}, u32[]{:S(2)}, u32[]{:S(2)}) collective-permute-start(bf16[256,2048]{1,0:T(8,128)(2,1)} %convolution_convert_fusion.10), channel_id=1, source_target_pairs={{0,16},{1,17},{2,18},{3,19},{4,20},{5,21},{6,22},{7,23},{8,24},{9,... | collective-permute-start | bytes 3145736 | tf_op jit(solution)/shard_map/ppermute | solution.py:935
  626.7 4.7 copy-start.26
  626.7 4.7 copy-start.28
  665.0 30.6 %copy-start.3 = (f32[64,2048]{1,0:T(8,128)S(1)}, f32[64,2048]{1,0:T(8,128)}, u32[]{:S(2)}) copy-start(f32[64,2048]{1,0:T(8,128)} %reduce_rows.13) | copy-start | bytes 1572868
  698.1 27.3 %copy-start.18 = (bf16[1024,512]{0,1:T(8,128)(2,1)S(1)}, bf16[1024,512]{0,1:T(8,128)(2,1)}, u32[]{:S(2)}) copy-start(bf16[1024,512]{0,1:T(8,128)(2,1)} %copy-done.17) | copy-start | bytes 3145732
  725.4 8.0 copy-start.5
  725.4 8.0 copy-start.7
  725.4 13.7 %slice-start.2 = ((s8[8388608]{0:T(1024)(128)(4,1)}), s8[4194304]{0:T(1024)(128)(4,1)S(1)}, s32[]{:S(2)}) async-start(s8[8388608]{0:T(1024)(128)(4,1)} %bitcast.228), calls=%async_computation.6 | async-start | bytes 8388608
  731.4 7.7 slice-start.3
  731.4 143.4 %collective-permute-start.8 = (bf16[512,2048]{1,0:T(8,128)(2,1)}, bf16[512,2048]{1,0:T(8,128)(2,1)}, u32[]{:S(2)}, u32[]{:S(2)}) collective-permute-start(bf16[512,2048]{1,0:T(8,128)(2,1)} %convolution_convert_fusion.9), channel_id=1, source_target_pairs={{16,0},{17,1},{18,2},{19,3},{20,4},{21,5},{22,6},{23,7},{24,8},{25... | collective-permute-start | bytes 6291464 | tf_op jit(solution)/shard_map/ppermute | solution.py:935
  738.1 7.1 copy-start.32
  774.6 30.4 %copy-start.14 = (bf16[1024,128]{1,0:T(8,128)(2,1)S(1)}, bf16[1024,128]{1,0:T(8,128)(2,1)}, u32[]{:S(2)}) copy-start(bf16[1024,128]{1,0:T(8,128)(2,1)} %get-tuple-element.24) | copy-start | bytes 786436
  805.0 4.6 copy-start
  808.1 17.9 %collective-permute-start.4 = (bf16[128,2048]{1,0:T(8,128)(2,1)S(1)}, bf16[128,2048]{1,0:T(8,128)(2,1)S(1)}, u32[]{:S(2)}, u32[]{:S(2)}) collective-permute-start(bf16[128,2048]{1,0:T(8,128)(2,1)S(1)} %convolution_convert_fusion.13), channel_id=1, source_target_pairs={{16,0},{17,1},{18,2},{19,3},{20,4},{21,5},{22,6},{23,7},{24,8},{25... | collective-permute-start | bytes 1572872 | tf_op jit(solution)/shard_map/ppermute | solution.py:935
  824.8 29.7 %collective-permute-start.2 = (bf16[256,2048]{1,0:T(8,128)(2,1)}, bf16[256,2048]{1,0:T(8,128)(2,1)}, u32[]{:S(2)}, u32[]{:S(2)}) collective-permute-start(bf16[256,2048]{1,0:T(8,128)(2,1)} %convolution_convert_fusion.11), channel_id=1, source_target_pairs={{16,0},{17,1},{18,2},{19,3},{20,4},{21,5},{22,6},{23,7},{24,8},{25... | collective-permute-start | bytes 3145736 | tf_op jit(solution)/shard_map/ppermute | solution.py:935
  827.3 30.5 %all-to-all-start.1 = ((bf16[8,128,256]{2,1,0:T(8,128)(2,1)}), bf16[8,128,256]{2,1,0:T(8,128)(2,1)S(1)}, u32[]{:S(2)}, u32[]{:S(2)}) async-start(bf16[8,128,256]{2,1,0:T(8,128)(2,1)} %bitcast.183), calls=%async_computation.1 | async-start | bytes 1048576 | tf_op jit(solution)/shard_map/all_to_all | solution.py:1032
  840.3 21.9 %copy-start.30 = (bf16[1024,512]{0,1:T(8,128)(2,1)S(1)}, bf16[1024,512]{0,1:T(8,128)(2,1)}, u32[]{:S(2)}) copy-start(bf16[1024,512]{0,1:T(8,128)(2,1)} %copy-done.29) | copy-start | bytes 3145732
  840.3 103.8 %collective-permute-start.6 = (bf16[2048,1024]{1,0:T(8,128)(2,1)}, bf16[2048,1024]{1,0:T(8,128)(2,1)}, u32[]{:S(2)}, u32[]{:S(2)}) collective-permute-start(bf16[2048,1024]{1,0:T(8,128)(2,1)} %convolution_convert_fusion.7), channel_id=1, source_target_pairs={{16,0},{17,1},{18,2},{19,3},{20,4},{21,5},{22,6},{23,7},{24,8},{25... | collective-permute-start | bytes 12582920 | tf_op jit(solution)/shard_map/ppermute | solution.py:935
  858.6 29.2 %all-to-all-start = ((bf16[8,256,256]{2,1,0:T(8,128)(2,1)}), bf16[8,256,256]{2,1,0:T(8,128)(2,1)S(1)}, u32[]{:S(2)}, u32[]{:S(2)}) async-start(bf16[8,256,256]{2,1,0:T(8,128)(2,1)} %bitcast.181), calls=%async_computation | async-start | bytes 2097152 | tf_op jit(solution)/shard_map/all_to_all | solution.py:1032
  871.3 91.2 %collective-permute-start.7 = (bf16[2048,1024]{1,0:T(8,128)(2,1)}, bf16[2048,1024]{1,0:T(8,128)(2,1)}, u32[]{:S(2)}, u32[]{:S(2)}) collective-permute-start(bf16[2048,1024]{1,0:T(8,128)(2,1)} %convolution_convert_fusion.6), channel_id=1, source_target_pairs={{0,16},{1,17},{2,18},{3,19},{4,20},{5,21},{6,22},{7,23},{8,24},{9,... | collective-permute-start | bytes 12582920 | tf_op jit(solution)/shard_map/ppermute | solution.py:935
  888.8 81.4 %all-to-all-start.3 = ((bf16[8,512,256]{2,1,0:T(8,128)(2,1)}), bf16[8,512,256]{2,1,0:T(8,128)(2,1)S(1)}, u32[]{:S(2)}, u32[]{:S(2)}) async-start(bf16[8,512,256]{2,1,0:T(8,128)(2,1)} %bitcast.190), calls=%async_computation.3 | async-start | bytes 4194304 | tf_op jit(solution)/shard_map/all_to_all | solution.py:1032
  970.2 186.0 %all-to-all-start.2 = ((bf16[8,256,1024]{2,1,0:T(8,128)(2,1)}), bf16[8,256,1024]{2,1,0:T(8,128)(2,1)}, u32[]{:S(2)}, u32[]{:S(2)}) async-start(bf16[8,256,1024]{2,1,0:T(8,128)(2,1)} %bitcast.188), calls=%async_computation.2 | async-start | bytes 8388608 | tf_op jit(solution)/shard_map/all_to_all | solution.py:1032
  976.2 166.2 %collective-permute-start = (f32[64,2048]{1,0:T(8,128)}, f32[64,2048]{1,0:T(8,128)}, u32[]{:S(2)}, u32[]{:S(2)}) collective-permute-start(f32[64,2048]{1,0:T(8,128)} %get-tuple-element.111), channel_id=1, source_target_pairs={{0,16},{16,0},{1,17},{17,1},{2,18},{18,2},{3,19},{19,3},{4,20},{20... | collective-permute-start | bytes 1572872 | tf_op jit(solution)/shard_map/ppermute | solution.py:931
  983.4 107.3 %copy-start.21 = (f32[1,1,2048]{2,1,0:T(1,128)S(1)}, f32[1,1,2048]{2,1,0:T(1,128)}, u32[]{:S(2)}) copy-start(f32[1,1,2048]{2,1,0:T(1,128)} %copy-done.20) | copy-start | bytes 24580
  983.4 107.3 %copy-start.23 = (f32[64]{0:T(128)S(1)}, f32[64]{0:T(128)}, u32[]{:S(2)}) copy-start(f32[64]{0:T(128)} %copy-done.22) | copy-start | bytes 772
  1094.7 50.1 %collective-permute-start.1 = (f32[64,2048]{1,0:T(8,128)}, f32[64,2048]{1,0:T(8,128)}, u32[]{:S(2)}, u32[]{:S(2)}) collective-permute-start(f32[64,2048]{1,0:T(8,128)} %get-tuple-element.85), channel_id=1, source_target_pairs={{0,16},{16,0},{1,17},{17,1},{2,18},{18,2},{3,19},{19,3},{4,20},{20... | collective-permute-start | bytes 1572872 | tf_op jit(solution)/shard_map/ppermute | solution.py:931
  1141.7 5.5 copy-start.12
  1141.7 6.6 copy-start.9
  (4 other events, 3.6 us)

commit v2 on v1

--- a/solution.py
+++ b/solution.py
@@ -428,13 +428,21 @@
 
 
 MESH = pl.DeviceIdType.MESH
+SUBS = 2
+
+
+def taking(us):
+    return pl.CostEstimate(flops=0, bytes_accessed=int(us * 3.69e6), transcendentals=0)
+
 
 def ring_place(index, count):
     return jnp.where(lax.rem(index, 2) == 0, index // 2, count - (index + 1) // 2)
+
 
 def ring_index(place, count):
     place = lax.rem(place + 2 * count, count)
     return jnp.where(place < count // 2, 2 * place, 2 * count - 1 - 2 * place)
+
 
 def greet(others):
     barrier = pltpu.get_barrier_semaphore()
@@ -442,104 +450,174 @@
         pl.semaphore_signal(barrier, inc=1, device_id=other, device_id_type=MESH)
     pl.semaphore_wait(barrier, len(others))
 
-def gather_kernel(count, subs, x_ref, o_ref, ring_send, ring_recv, side_send, side_recv, own_sem):
-    rows = x_ref.shape[0]
-    piece = rows // subs
-    me = lax.axis_index("dp")
-    core = lax.axis_index("tensor")
-    place = ring_place(me, count)
-    near = ({"dp": ring_index(place + 1, count)}, {"dp": ring_index(place - 1, count)})
-    side = {"tensor": 1 - core}
-    greet((*near, side))
+
+def remote(source, target, send, recv, device):
+    return pltpu.make_async_remote_copy(
+        source, target, send, recv, device_id=device, device_id_type=MESH
+    )
+
+
+def partners(me, count):
+    half = count // 2
+    side, inside = me // half, lax.rem(me, half)
+    peers = [(1 - side) * half + lax.rem(inside + k, half) for k in range(half)]
+    peers += [side * half + lax.rem(inside + k, half) for k in range(1, half)]
+    origins = [(1 - side) * half + lax.rem(inside + half - k, half) for k in range(half)]
+    origins += [side * half + lax.rem(inside + half - k, half) for k in range(1, half)]
+    return peers, origins
+
+
+def aligned(start, size):
+    return pl.ds(pl.multiple_of(start, size), size)
+
+
+class Ring:
+    def __init__(self, count):
+        self.count = count
+        self.far = count // 2
+        self.me = lax.axis_index("dp")
+        self.core = lax.axis_index("tensor")
+        self.place = ring_place(self.me, count)
+        self.near = tuple({"dp": ring_index(self.place + step, count)} for step in (1, -1))
+        self.side = {"tensor": 1 - self.core}
+
+    def everyone(self):
+        return [*self.near, self.side]
+
+    def index(self, steps):
+        return ring_index(self.place + steps, self.count)
+
+    def orders(self):
+        for k in range(SUBS):
+            yield k, 0
+            yield SUBS - 1 - k, 1
+
+
+def gather_scratch(count):
     far = count // 2
-
-    def spot(step_from, sub):
-        index = ring_index(place + step_from, count)
-        start = pl.multiple_of((index * 2 + core) * rows, rows) + sub * piece
-        return o_ref.at[pl.ds(pl.multiple_of(start, piece), piece), :]
-
-    own = pltpu.make_async_copy(x_ref, o_ref.at[pl.ds(pl.multiple_of((me * 2 + core) * rows, rows), rows), :], own_sem)
-    own.start()
-    sends = []
-
-    def travels(way, hop, sub):
-        return hop < far or (sub < subs // 2) == (way == 0)
-
-    def ring_copy(way, hop, sub):
-        source = x_ref.at[pl.ds(sub * piece, piece), :] if hop == 1 else spot((1 - hop) if way == 0 else (hop - 1), sub)
-        return pltpu.make_async_remote_copy(source, spot((1 - hop) if way == 0 else (hop - 1), sub),
-            ring_send.at[way, hop - 1, sub], ring_recv.at[way, hop - 1, sub], device_id=near[way], device_id_type=MESH)
-
-    def side_copy(step_from, sub, slot):
-        source = x_ref.at[pl.ds(sub * piece, piece), :] if step_from == 0 else spot(step_from, sub)
-        return pltpu.make_async_remote_copy(source, spot(step_from, sub), side_send.at[slot, sub], side_recv.at[slot, sub],
-            device_id=side, device_id_type=MESH)
-
-    def side_start(copy):
+    dma = pltpu.SemaphoreType.DMA
+    return [dma((2, far, SUBS)), dma((2, far, SUBS)), dma((count, SUBS)), dma((count, SUBS)), dma]
+
+
+class Gather:
+    def __init__(self, ring, x_ref, o_ref, scratch):
+        self.ring = ring
+        self.x_ref, self.o_ref = x_ref, o_ref
+        self.ring_send, self.ring_recv, self.side_send, self.side_recv, self.own_sem = scratch
+        self.rows = x_ref.shape[0]
+        self.piece = self.rows // SUBS
+        self.sends = []
+
+    def spot(self, steps, sub, core):
+        start = (self.ring.index(steps) * 2 + core) * self.rows + sub * self.piece
+        return self.o_ref.at[aligned(start, self.piece), :]
+
+    def mine(self, steps, sub):
+        if steps == 0:
+            return self.x_ref.at[sub * self.piece : (sub + 1) * self.piece, :]
+        return self.spot(steps, sub, self.ring.core)
+
+    def travels(self, way, hop, sub):
+        return hop < self.ring.far or (sub < SUBS // 2) == (way == 0)
+
+    def go(self, copy):
         copy.start()
-        sends.append(copy)
-
-    order = lambda way: range(subs) if way == 0 else range(subs - 1, -1, -1)
-    for k in range(subs):
-        for way in range(2):
-            sub = list(order(way))[k]
-            copy = ring_copy(way, 1, sub)
-            copy.start(); sends.append(copy)
-    for sub in range(subs):
-        copy = side_copy(0, sub, 0)
-        copy.start(); sends.append(copy)
-    sides = [(0, sub) for sub in range(subs)]
-    for hop in range(1, far + 1):
-        for k in range(subs):
-            for way in range(2):
-                sub = list(order(way))[k]
-                if not travels(way, hop, sub):
-                    continue
-                arrive = pltpu.make_async_remote_copy(spot(-hop if way == 0 else hop, sub), spot(-hop if way == 0 else hop, sub),
-                    ring_send.at[way, hop - 1, sub], ring_recv.at[way, hop - 1, sub], device_id=near[way], device_id_type=MESH)
-                arrive.wait_recv()
-                if hop < far and travels(way, hop + 1, sub):
-                    copy = ring_copy(way, hop + 1, sub)
-                    copy.start(); sends.append(copy)
-                slot = hop if way == 0 or hop == far else count - hop
-                copy = side_copy(-hop if way == 0 else hop, sub, slot)
-                copy.start(); sends.append(copy)
-    for copy in sends:
-        copy.wait_send()
-    for slot in range(count):
-        for sub in range(subs):
-            step_from = -slot if slot <= far else count - slot
-            index = ring_index(place + step_from, count)
-            start = pl.multiple_of((index * 2 + 1 - core) * rows, rows) + sub * piece
-            there = o_ref.at[pl.ds(pl.multiple_of(start, piece), piece), :]
-            pltpu.make_async_remote_copy(there, there, side_send.at[slot, sub], side_recv.at[slot, sub], device_id=side, device_id_type=MESH).wait_recv()
-    own.wait()
-
-def gather_rows(x, count, cid, subs=2):
+        self.sends.append(copy)
+
+    def pass_on(self, way, hop, sub):
+        steps = 1 - hop if way == 0 else hop - 1
+        self.go(
+            remote(
+                self.mine(steps, sub),
+                self.spot(steps, sub, self.ring.core),
+                self.ring_send.at[way, hop - 1, sub],
+                self.ring_recv.at[way, hop - 1, sub],
+                self.ring.near[way],
+            )
+        )
+
+    def hand_over(self, steps, sub, slot):
+        self.go(
+            remote(
+                self.mine(steps, sub),
+                self.spot(steps, sub, self.ring.core),
+                self.side_send.at[slot, sub],
+                self.side_recv.at[slot, sub],
+                self.ring.side,
+            )
+        )
+
+    def start(self):
+        for sub, way in self.ring.orders():
+            self.pass_on(way, 1, sub)
+        for sub in range(SUBS):
+            self.hand_over(0, sub, 0)
+        self.own = pltpu.make_async_copy(
+            self.x_ref,
+            self.o_ref.at[aligned((self.ring.me * 2 + self.ring.core) * self.rows, self.rows), :],
+            self.own_sem,
+        )
+        self.own.start()
+
+    def hop(self, hop):
+        far, count = self.ring.far, self.ring.count
+        for sub, way in self.ring.orders():
+            if not self.travels(way, hop, sub):
+                continue
+            steps = -hop if way == 0 else hop
+            here = self.spot(steps, sub, self.ring.core)
+            remote(
+                here, here, self.ring_send.at[way, hop - 1, sub],
+                self.ring_recv.at[way, hop - 1, sub], self.ring.near[way],
+            ).wait_recv()
+            if hop < far and self.travels(way, hop + 1, sub):
+                self.pass_on(way, hop + 1, sub)
+            self.hand_over(steps, sub, hop if way == 0 or hop == far else count - hop)
+
+    def finish(self):
+        for copy in self.sends:
+            copy.wait_send()
+        for slot in range(self.ring.count):
+            steps = -slot if slot <= self.ring.far else self.ring.count - slot
+            for sub in range(SUBS):
+                there = self.spot(steps, sub, 1 - self.ring.core)
+                remote(
+                    there, there, self.side_send.at[slot, sub], self.side_recv.at[slot, sub],
+                    self.ring.side,
+                ).wait_recv()
+        self.own.wait()
+
+
+def gather_kernel(count, x_ref, o_ref, *scratch):
+    ring = Ring(count)
+    greet(ring.everyone())
+    gather = Gather(ring, x_ref, o_ref, scratch)
+    gather.start()
+    for hop in range(1, ring.far + 1):
+        gather.hop(hop)
+    gather.finish()
+
+
+def gather_rows(x, count, cid):
     rows, width = x.shape
-    far = count // 2
     return pl.pallas_call(
-        functools.partial(gather_kernel, count, subs),
+        functools.partial(gather_kernel, count),
         out_shape=jax.ShapeDtypeStruct((count * 2 * rows, width), x.dtype),
         in_specs=[pl.BlockSpec(memory_space=pltpu.VMEM)],
         out_specs=pl.BlockSpec(memory_space=pltpu.VMEM),
-        scratch_shapes=[
-            pltpu.SemaphoreType.DMA((2, far, subs)), pltpu.SemaphoreType.DMA((2, far, subs)),
-            pltpu.SemaphoreType.DMA((count, subs)), pltpu.SemaphoreType.DMA((count, subs)),
-            pltpu.SemaphoreType.DMA],
+        scratch_shapes=gather_scratch(count),
         compiler_params=pltpu.CompilerParams(collective_id=cid, has_side_effects=True),
-        name="gather_rows")(x)
-
-def reduce_kernel(count, subs, p_ref, o_ref, side_buf, send_buf, recv_buf, ring_send, ring_recv, side_send, side_recv):
+        cost_estimate=taking(27),
+        name="gather_rows",
+    )(x)
+
+
+def reduce_kernel(count, p_ref, o_ref, side_buf, send_buf, recv_buf, ring_send, ring_recv, side_send, side_recv):
     rows, width = o_ref.shape
-    piece = rows // subs
-    me = lax.axis_index("dp")
-    core = lax.axis_index("tensor")
-    place = ring_place(me, count)
-    near = ({"dp": ring_index(place + 1, count)}, {"dp": ring_index(place - 1, count)})
-    side = {"tensor": 1 - core}
-    greet((*near, side))
-    far = count // 2
+    piece = rows // SUBS
+    ring = Ring(count)
+    far, core = ring.far, ring.core
+    greet(ring.everyone())
     steps = [far]
     for k in range(far - 1, 0, -1):
         steps += [k, -k]
@@ -547,70 +625,74 @@
     sends = []
 
     def part(step_to, of_core):
-        index = ring_index(place + step_to, count)
-        return pl.multiple_of((index * 2 + of_core) * rows, rows)
+        return pl.multiple_of((ring.index(step_to) * 2 + of_core) * rows, rows)
 
     side_copies = {}
     for slot, step_to in enumerate(steps):
-        copy = pltpu.make_async_remote_copy(p_ref.at[pl.ds(part(step_to, 1 - core), rows), :], side_buf.at[slot],
-            side_send.at[slot], side_recv.at[slot], device_id=side, device_id_type=MESH)
+        copy = remote(
+            p_ref.at[pl.ds(part(step_to, 1 - core), rows), :], side_buf.at[slot],
+            side_send.at[slot], side_recv.at[slot], ring.side,
+        )
         copy.start()
         side_copies[step_to] = (slot, copy)
+
+    def span(sub):
+        return slice(sub * piece, (sub + 1) * piece)
 
     def mine(step_to, sub):
         slot, _ = side_copies[step_to]
         start = pl.multiple_of(part(step_to, core) + sub * piece, piece)
-        return p_ref[pl.ds(start, piece), :].astype(jnp.float32) + side_buf[slot, sub * piece:(sub + 1) * piece, :].astype(jnp.float32)
+        return p_ref[pl.ds(start, piece), :].astype(jnp.float32) + side_buf[
+            slot, span(sub), :
+        ].astype(jnp.float32)
 
     def travels(way, step, sub):
-        return step > 1 or (sub < subs // 2) == (way == 0)
+        return step > 1 or (sub < SUBS // 2) == (way == 0)
 
     def ring_copy(way, step, sub):
-        span = slice(sub * piece, (sub + 1) * piece)
-        return pltpu.make_async_remote_copy(send_buf.at[way, step - 1, span, :], recv_buf.at[way, step - 1, span, :],
-            ring_send.at[way, step - 1, sub], ring_recv.at[way, step - 1, sub], device_id=near[way], device_id_type=MESH)
-
-    order = lambda way: list(range(subs)) if way == 0 else list(range(subs - 1, -1, -1))
+        return remote(
+            send_buf.at[way, step - 1, span(sub), :], recv_buf.at[way, step - 1, span(sub), :],
+            ring_send.at[way, step - 1, sub], ring_recv.at[way, step - 1, sub], ring.near[way],
+        )
+
     seen = set()
     for step in range(1, far + 1):
-        for k in range(subs):
-            for way in range(2):
-                sub = order(way)[k]
-                if not travels(way, step, sub):
-                    continue
-                step_to = far + 1 - step
-                step_to = step_to if way == 0 or step_to == far else -step_to
-                if step_to not in seen:
-                    side_copies[step_to][1].wait_recv()
-                    seen.add(step_to)
-                value = mine(step_to, sub)
-                span = slice(sub * piece, (sub + 1) * piece)
-                if step > 1 and travels(way, step - 1, sub):
-                    ring_copy(way, step - 1, sub).wait_recv()
-                    value = value + recv_buf[way, step - 2, span, :].astype(jnp.float32)
-                send_buf[way, step - 1, span, :] = value.astype(send_buf.dtype)
-                copy = ring_copy(way, step, sub)
-                copy.start()
-                sends.append(copy)
+        for sub, way in ring.orders():
+            if not travels(way, step, sub):
+                continue
+            step_to = far + 1 - step
+            step_to = step_to if way == 0 or step_to == far else -step_to
+            if step_to not in seen:
+                side_copies[step_to][1].wait_recv()
+                seen.add(step_to)
+            value = mine(step_to, sub)
+            if step > 1 and travels(way, step - 1, sub):
+                ring_copy(way, step - 1, sub).wait_recv()
+                value = value + recv_buf[way, step - 2, span(sub), :].astype(jnp.float32)
+            send_buf[way, step - 1, span(sub), :] = value.astype(send_buf.dtype)
+            copy = ring_copy(way, step, sub)
+            copy.start()
+            sends.append(copy)
     side_copies[0][1].wait_recv()
-    for sub in range(subs):
-        span = slice(sub * piece, (sub + 1) * piece)
+    for sub in range(SUBS):
         value = mine(0, sub)
         for way in range(2):
             ring_copy(way, far, sub).wait_recv()
-            value = value + recv_buf[way, far - 1, span, :].astype(jnp.float32)
-        o_ref[span, :] = value.astype(o_ref.dtype)
+            value = value + recv_buf[way, far - 1, span(sub), :].astype(jnp.float32)
+        o_ref[span(sub), :] = value.astype(o_ref.dtype)
     for copy in sends:
         copy.wait_send()
     for _, copy in side_copies.values():
         copy.wait_send()
 
-def reduce_rows(p, count, cid, subs=2, dtype=jnp.float32):
+
+def reduce_rows(p, count, cid, dtype=jnp.float32):
     total, width = p.shape
     rows = total // (2 * count)
     far = count // 2
+    dma = pltpu.SemaphoreType.DMA
     return pl.pallas_call(
-        functools.partial(reduce_kernel, count, subs),
+        functools.partial(reduce_kernel, count),
         out_shape=jax.ShapeDtypeStruct((rows, width), dtype),
         in_specs=[pl.BlockSpec(memory_space=pltpu.VMEM)],
         out_specs=pl.BlockSpec(memory_space=pltpu.VMEM),
@@ -618,107 +700,141 @@
             pltpu.VMEM((count, rows, width), p.dtype),
             pltpu.VMEM((2, far, rows, width), p.dtype),
             pltpu.VMEM((2, far, rows, width), p.dtype),
-            pltpu.SemaphoreType.DMA((2, far, subs)), pltpu.SemaphoreType.DMA((2, far, subs)),
-            pltpu.SemaphoreType.DMA((count,)), pltpu.SemaphoreType.DMA((count,))],
+            dma((2, far, SUBS)), dma((2, far, SUBS)), dma((count,)), dma((count,)),
+        ],
         compiler_params=pltpu.CompilerParams(collective_id=cid, has_side_effects=True),
-        name="reduce_rows")(p)
+        cost_estimate=taking(29),
+        name="reduce_rows",
+    )(p)
 
 
 def weight_pieces(source, target, count, heads, srcs, dsts, layer):
-    qkv, wo, gate, up, down, gains = srcs
-    out_qkv, out_wo, out_gu, out_down, out_gains = dsts
+    qkv, wo, gate, up, down = srcs
+    out_qkv, out_wo, out_gu, out_down = dsts
     depth = gate.shape[0]
     hidden = gate.shape[1] // count
     q_rows = wo.shape[0] // count
     kv_rows = (qkv.shape[0] - wo.shape[0]) // 2
     shared = count * heads // kv_rows
-    cols = pl.ds(pl.multiple_of(source * depth, depth), depth)
-
-    def at(index, size):
-        return pl.ds(pl.multiple_of(index * size, size), size)
-
+    cols = aligned(source * depth, depth)
     k_from = pl.multiple_of(wo.shape[0] + target // shared * heads, heads)
     v_from = pl.multiple_of(wo.shape[0] + kv_rows + target // shared * heads, heads)
+    mine = aligned(target * hidden, hidden)
     return (
-        (gains, out_gains.at[layer, :, cols]),
-        (qkv.at[at(target, q_rows), :], out_qkv.at[layer, pl.ds(0, q_rows), cols]),
+        (qkv.at[aligned(target * q_rows, q_rows), :], out_qkv.at[layer, pl.ds(0, q_rows), cols]),
         (qkv.at[pl.ds(k_from, heads), :], out_qkv.at[layer, pl.ds(q_rows, heads), cols]),
         (qkv.at[pl.ds(v_from, heads), :], out_qkv.at[layer, pl.ds(q_rows + heads, heads), cols]),
-        (wo.at[at(target, q_rows), :], out_wo.at[layer, :, cols]),
-        (gate.at[:, at(target, hidden)], out_gu.at[layer, cols, pl.ds(0, hidden)]),
-        (up.at[:, at(target, hidden)], out_gu.at[layer, cols, pl.ds(hidden, hidden)]),
-        (down.at[at(target, hidden), :], out_down.at[layer, :, cols]),
-    )
-
-
-KINDS = 8
+        (wo.at[aligned(target * q_rows, q_rows), :], out_wo.at[layer, :, cols]),
+        (gate.at[:, mine], out_gu.at[layer, cols, pl.ds(0, hidden)]),
+        (up.at[:, mine], out_gu.at[layer, cols, pl.ds(hidden, hidden)]),
+        (down.at[mine, :], out_down.at[layer, :, cols]),
+    )
+
+
+KINDS = 7
 
 
 def spread_kernel(count, heads, *refs):
-    srcs = refs[:6]
-    dsts = refs[6:11]
-    send, recv, cross_send, cross_recv, own_sem = refs[11:]
-    me = lax.axis_index("dp")
+    srcs, gain_in, unit_ref, grad_ref = refs[:5], refs[5], refs[6], refs[7]
+    dsts, all_gains, gathered = refs[8:12], refs[12], refs[13:15]
+    normed, gain_send, gain_recv, gain_own = refs[15:19]
+    send, recv, cross_send, cross_recv, own_sem = refs[19:24]
+    ring = Ring(count)
+    me = ring.me
     layer = lax.axis_index("section")
-    peers = [lax.rem(me + k, count) for k in range(1, count)]
+    peers, origins = partners(me, count)
     across = {"section": 1 - layer}
-    greet([{"dp": peer} for peer in peers] + [across])
-    waits = []
+    holders = [{"dp": peer} for peer in peers] + [
+        {"section": 1 - layer, "dp": peer} for peer in [*peers, me]
+    ]
+    greet([*holders, ring.side])
+    gathers = [
+        Gather(ring, source, gathered[k], refs[24 + 5 * k : 29 + 5 * k])
+        for k, source in enumerate((normed, grad_ref))
+    ]
+    started = []
     local = []
-    own = weight_pieces(me, me, count, heads, srcs, dsts, layer)
-    for kind in range(KINDS):
+
+    def go(copy):
+        copy.start()
+        started.append(copy)
+
+    def gain_spot(at, source):
+        depth = gain_in.shape[1]
+        return all_gains.at[at, :, aligned(source * depth, depth)]
+
+    def send_kind(kind):
         for k, peer in enumerate(peers):
-            there = weight_pieces(me, peer, count, heads, srcs, dsts, layer)[kind]
-            copy = pltpu.make_async_remote_copy(
-                there[0], there[1], send.at[kind, k], recv.at[kind, k],
-                device_id={"dp": peer}, device_id_type=MESH,
-            )
-            copy.start()
-            waits.append(copy)
-        copy = pltpu.make_async_remote_copy(
-            own[kind][0], own[kind][1], cross_send.at[kind, count - 1], cross_recv.at[kind, count - 1],
-            device_id=across, device_id_type=MESH,
-        )
-        copy.start()
-        waits.append(copy)
-        copy = pltpu.make_async_copy(own[kind][0], own[kind][1], own_sem.at[kind])
+            source, target = weight_pieces(me, peer, count, heads, srcs, dsts, layer)[kind]
+            go(remote(source, target, send.at[kind, k], recv.at[kind, k], {"dp": peer}))
+
+    def own_kind(kind):
+        source, target = weight_pieces(me, me, count, heads, srcs, dsts, layer)[kind]
+        go(remote(source, target, cross_send.at[kind, count - 1], cross_recv.at[kind, count - 1], across))
+        copy = pltpu.make_async_copy(source, target, own_sem.at[kind])
         copy.start()
         local.append(copy)
+
+    def forward(kind, k):
+        here = weight_pieces(origins[k], me, count, heads, srcs, dsts, layer)[kind][1]
+        remote(here, here, send.at[kind, k], recv.at[kind, k], {"dp": origins[k]}).wait_recv()
+        go(remote(here, here, cross_send.at[kind, k], cross_recv.at[kind, k], across))
+
+    sizes = [math.prod(there.shape) for _, there in weight_pieces(me, me, count, heads, srcs, dsts, layer)]
+    arrivals = []
     for kind in range(KINDS):
         for k in range(count - 1):
-            origin = lax.rem(me + count - 1 - k, count)
-            here = weight_pieces(origin, me, count, heads, srcs, dsts, layer)[kind][1]
-            pltpu.make_async_remote_copy(
-                here, here, send.at[kind, k], recv.at[kind, k],
-                device_id={"dp": origin}, device_id_type=MESH,
-            ).wait_recv()
-            copy = pltpu.make_async_remote_copy(
-                here, here, cross_send.at[kind, k], cross_recv.at[kind, k],
-                device_id=across, device_id_type=MESH,
-            )
-            copy.start()
-            waits.append(copy)
+            part = (k + 1) / (count // 2) if k < count // 2 else 1.0
+            due = sum(sizes[:kind]) + part * sizes[kind]
+            arrivals.append((due if k < count // 2 else due * 0.5, kind, k))
+    arrivals.sort()
+
+    for k, holder in enumerate(holders):
+        go(remote(gain_in, gain_spot(layer, me), gain_send.at[k], gain_recv.at[k], holder))
+    own_gains = pltpu.make_async_copy(gain_in, gain_spot(layer, me), gain_own)
+    own_gains.start()
+    gathers[1].start()
+    for kind in range(KINDS):
+        own_kind(kind)
+    own_gains.wait()
+    for k, holder in enumerate(holders):
+        at, source = (layer, k) if k < count - 1 else (1 - layer, k - count + 1)
+        spot = gain_spot(at, origins[source] if source < count - 1 else me)
+        remote(spot, spot, gain_send.at[k], gain_recv.at[k], holder).wait_recv()
+    normed[...] = (unit_ref[...] * all_gains[0, 0:1, :]).astype(normed.dtype)
+    gathers[0].start()
+    batches = [range(KINDS - 3), [KINDS - 3], [KINDS - 2, KINDS - 1]]
+    for hop in range(1, ring.far + 1):
+        gathers[1].hop(hop)
+        gathers[0].hop(hop)
+        if hop > ring.far - len(batches):
+            for kind in batches[hop - 1 - ring.far + len(batches)]:
+                send_kind(kind)
+    for _, kind, k in arrivals:
+        forward(kind, k)
+    for gather in gathers:
+        gather.finish()
     for copy in local:
         copy.wait()
-    for copy in waits:
+    for copy in started:
         copy.wait_send()
     for kind in range(KINDS):
         for k in range(count):
-            origin = lax.rem(me + count - 1 - k, count)
+            origin = origins[k] if k < count - 1 else me
             there = weight_pieces(origin, me, count, heads, srcs, dsts, 1 - layer)[kind][1]
-            pltpu.make_async_remote_copy(
-                there, there, cross_send.at[kind, k], cross_recv.at[kind, k],
-                device_id=across, device_id_type=MESH,
-            ).wait_recv()
-
-
-def spread_weights(qkv, wo, gate, up, down, gains, count, heads, cid):
+            remote(there, there, cross_send.at[kind, k], cross_recv.at[kind, k], across).wait_recv()
+
+
+def spread_weights(qkv, wo, gate, up, down, gains, unit, grads, count, heads, cid):
     depth = gate.shape[0]
     width = depth * count
     hidden = gate.shape[1] // count
     q_rows = wo.shape[0] // count
     shape = lambda *dims: jax.ShapeDtypeStruct((2, *dims), jnp.bfloat16)
     hbm = pl.BlockSpec(memory_space=pl.ANY)
+    vmem = pl.BlockSpec(memory_space=pltpu.VMEM)
+    dma = pltpu.SemaphoreType.DMA
+    gathered = jax.ShapeDtypeStruct((count * 2 * grads.shape[0], width), grads.dtype)
     return pl.pallas_call(
         functools.partial(spread_kernel, count, heads),
         out_shape=(
@@ -727,19 +843,173 @@
             shape(width, 2 * hidden),
             shape(hidden, width),
             jax.ShapeDtypeStruct((2, gains.shape[0], width), gains.dtype),
+            gathered,
+            gathered,
         ),
-        in_specs=[hbm] * 6,
-        out_specs=(hbm,) * 5,
+        in_specs=[hbm] * 5 + [vmem] * 3,
+        out_specs=(hbm,) * 4 + (vmem,) * 3,
         scratch_shapes=[
-            pltpu.SemaphoreType.DMA((KINDS, count - 1)),
-            pltpu.SemaphoreType.DMA((KINDS, count - 1)),
-            pltpu.SemaphoreType.DMA((KINDS, count)),
-            pltpu.SemaphoreType.DMA((KINDS, count)),
-            pltpu.SemaphoreType.DMA((KINDS,)),
+            pltpu.VMEM(grads.shape, grads.dtype),
+            dma((2 * count - 1,)), dma((2 * count - 1,)), dma,
+            dma((KINDS, count - 1)), dma((KINDS, count - 1)),
+            dma((KINDS, count)), dma((KINDS, count)), dma((KINDS,)),
+            *gather_scratch(count), *gather_scratch(count),
         ],
         compiler_params=pltpu.CompilerParams(collective_id=cid, has_side_effects=True),
+        cost_estimate=taking(220),
         name="spread_weights",
-    )(qkv, wo, gate, up, down, gains)
+    )(qkv, wo, gate, up, down, gains, unit, grads)
+
+
+def gradient_pieces(target, count, refs):
+    down, gate, up, wo, qkv = refs
+    depth = down.shape[1] // count
+    cols = aligned(target * depth, depth)
+    return (
+        down.at[:, cols],
+        gate.at[cols, :],
+        up.at[cols, :],
+        wo.at[:, cols],
+        qkv.at[cols, :],
+    )
+
+
+def owned_pieces(source, refs, sizes):
+    down, gate, up, wo, qkv = refs
+    return (
+        down.at[aligned(source * sizes[0][0], sizes[0][0]), :],
+        gate.at[:, aligned(source * sizes[1][1], sizes[1][1])],
+        up.at[:, aligned(source * sizes[2][1], sizes[2][1])],
+        wo.at[aligned(source * sizes[3][0], sizes[3][0]), :],
+        qkv.at[source],
+    )
+
+
+GRADS = 5
+
+
+def return_kernel(count, *refs):
+    partial = (refs[:5], refs[5:10])
+    gain_in = refs[10]
+    outs, gain_out = refs[11:16], refs[16]
+    landed, mine = refs[17:22], refs[22:27]
+    gain_landed, cross_send, cross_recv, load_sem, send, recv, own_sem, gain_send, gain_recv = refs[27:]
+    ring = Ring(count)
+    me, core = ring.me, ring.core
+    layer = lax.axis_index("section")
+    across = {"section": 1 - layer}
+    sizes = [ref.shape[1:] for ref in mine]
+    everyone = 4 * count
+    this = (layer * count + me) * 2 + core
+
+    def device(k):
+        other = lax.rem(this + k, everyone)
+        return {
+            "section": other // (2 * count),
+            "dp": lax.rem(other // 2, count),
+            "tensor": lax.rem(other, 2),
+        }
+
+    greet([device(k) for k in range(1, everyone)])
+    gain_copies = []
+    for k in range(1, everyone):
+        copy = remote(
+            gain_in.at[lax.rem(this + k, everyone)], gain_landed.at[k - 1],
+            gain_send.at[k - 1], gain_recv.at[k - 1], device(k),
+        )
+        copy.start()
+        gain_copies.append(copy)
+    peers, origins = partners(me, count)
+    order = [*peers, me]
+    crossing, loads, sends = {}, {}, []
+    for kind in range(GRADS):
+        for k, owner in enumerate(order):
+            pieces = [gradient_pieces(owner, count, partial[at])[kind] for at in range(2)]
+            for at in range(2):
+                copy = remote(
+                    pieces[1 - at], landed[kind].at[k],
+                    cross_send.at[kind, k], cross_recv.at[kind, k], across,
+                )
+                load = pltpu.make_async_copy(pieces[at], mine[kind].at[k], load_sem.at[kind, k])
+
+                @pl.when(layer == at)
+                def _():
+                    copy.start()
+                    load.start()
+
+            crossing[kind, k], loads[kind, k] = copy, load
+    for kind in range(GRADS):
+        for k, owner in enumerate(order):
+            loads[kind, k].wait()
+            crossing[kind, k].wait_recv()
+            total = mine[kind][k].astype(jnp.float32) + landed[kind][k].astype(jnp.float32)
+            mine[kind][k] = total.astype(jnp.bfloat16)
+            target = owned_pieces(me, outs, sizes)[kind]
+            if k < count - 1:
+                copy = remote(
+                    mine[kind].at[k], target, send.at[kind, k], recv.at[kind, k], {"dp": owner}
+                )
+            else:
+                copy = pltpu.make_async_copy(mine[kind].at[k], target, own_sem.at[kind])
+            copy.start()
+            sends.append((k, copy))
+    total = gain_in[this]
+    for k, copy in enumerate(gain_copies):
+        copy.wait_recv()
+        total = total + gain_landed[k]
+    gain_out[...] = total
+    for copy in gain_copies:
+        copy.wait_send()
+    for copy in crossing.values():
+        copy.wait_send()
+    for k, copy in sends:
+        if k < count - 1:
+            copy.wait_send()
+        else:
+            copy.wait()
+    for kind in range(GRADS):
+        for k in range(count - 1):
+            here = owned_pieces(origins[k], outs, sizes)[kind]
+            remote(
+                mine[kind].at[k], here, send.at[kind, k], recv.at[kind, k], {"dp": origins[k]}
+            ).wait_recv()
+
+
+def return_gradients(layer0, layer1, gains, count, cid):
+    hidden, width = layer0[0].shape
+    depth = width // count
+    q_rows = layer0[3].shape[0]
+    qkv_rows = layer0[4].shape[1]
+    hbm = pl.BlockSpec(memory_space=pl.ANY)
+    vmem = pl.BlockSpec(memory_space=pltpu.VMEM)
+    dma = pltpu.SemaphoreType.DMA
+    shape = lambda *dims: jax.ShapeDtypeStruct(dims, jnp.bfloat16)
+    sizes = [(hidden, depth), (depth, hidden), (depth, hidden), (q_rows, depth), (depth, qkv_rows)]
+    everyone, gain_rows, lanes = gains.shape
+    return pl.pallas_call(
+        functools.partial(return_kernel, count),
+        out_shape=(
+            shape(count * hidden, depth),
+            shape(depth, count * hidden),
+            shape(depth, count * hidden),
+            shape(count * q_rows, depth),
+            shape(count, depth, qkv_rows),
+            jax.ShapeDtypeStruct((gain_rows, lanes), gains.dtype),
+        ),
+        in_specs=[hbm] * 10 + [vmem],
+        out_specs=(hbm,) * 5 + (vmem,),
+        scratch_shapes=[
+            *(pltpu.VMEM((count, *size), jnp.bfloat16) for size in sizes),
+            *(pltpu.VMEM((count, *size), jnp.bfloat16) for size in sizes),
+            pltpu.VMEM((everyone - 1, gain_rows, lanes), gains.dtype),
+            dma((GRADS, count)), dma((GRADS, count)), dma((GRADS, count)),
+            dma((GRADS, count - 1)), dma((GRADS, count - 1)), dma((GRADS,)),
+            dma((everyone - 1,)), dma((everyone - 1,)),
+        ],
+        compiler_params=pltpu.CompilerParams(collective_id=cid, has_side_effects=True),
+        cost_estimate=taking(200),
+        name="return_gradients",
+    )(*layer0, *layer1, gains)
 
 
 def swap_halves(rows, head):
@@ -831,6 +1101,7 @@
             pltpu.VMEM((tokens, 2 * head), jnp.bfloat16),
             pltpu.VMEM((tokens, 2 * head), jnp.bfloat16),
         ],
+        cost_estimate=taking(6),
         name="attend_blocks",
     )(slots, qkv, cosine, sine)
 
@@ -902,6 +1173,7 @@
             pltpu.VMEM((tokens, 2 * head), jnp.float32),
             pltpu.VMEM((tokens, 2 * head), jnp.float32),
         ],
+        cost_estimate=taking(8),
         name="attend_blocks_back",
     )(slots, grad, kept, lse, cosine, sine)
 
@@ -931,15 +1203,12 @@
     return lax.ppermute(value, "section", [(0, 1), (1, 0)])
 
 
-def section_move(value, source):
-    return lax.ppermute(value, "section", [(source, 1 - source)])
-
-
-def fast_forward(rows, weights, layer, tools):
-    qkv_w, wo_w, gu_w, down_w, gain_attn, gain_mlp = [w[layer] for w in weights]
+def fast_forward(rows, normed1, weights, tools):
+    qkv_w, wo_w, gu_w, down_w, gain_attn, gain_mlp = weights
     count, slots, cosine, sine, head = tools
     unit1, inverse1 = norm_stats(rows)
-    normed1 = gather_rows((unit1 * gain_attn).astype(jnp.bfloat16), count, 1)
+    if normed1 is None:
+        normed1 = gather_rows((unit1 * gain_attn).astype(jnp.bfloat16), count, 1)
     qkv = matmul_nt(normed1, qkv_w)
     mixed, kept, lse = attend_blocks(slots, qkv, cosine, sine, count, head)
     second = rows + reduce_rows(matmul(mixed, wo_w).astype(jnp.bfloat16), count, 2)
@@ -952,19 +1221,21 @@
     return result, (unit1, inverse1, normed1, kept, lse, mixed, unit2, inverse2, normed2, gate_up, hidden)
 
 
-def fast_backward(grad_rows, context, weights, layer, tools):
-    qkv_w, wo_w, gu_w, down_w, gain_attn, gain_mlp = [w[layer] for w in weights]
+def fast_backward(grad_rows, out_grad, context, weights, tools):
+    qkv_w, wo_w, gu_w, down_w, gain_attn, gain_mlp = weights
     count, slots, cosine, sine, head = tools
     unit1, inverse1, normed1, kept, lse, mixed, unit2, inverse2, normed2, gate_up, hidden = context
     gate, upper = jnp.split(gate_up, 2, axis=1)
-    out_grad = gather_rows(grad_rows.astype(jnp.bfloat16), count, 1)
+    if out_grad is None:
+        out_grad = gather_rows(grad_rows.astype(jnp.bfloat16), count, 1)
     hidden_grad = matmul_nt(out_grad, down_w)
     grad_down = matmul_tn(hidden, out_grad).astype(jnp.bfloat16)
     sigma = jax.nn.sigmoid(gate)
     gate_grad = (hidden_grad * upper * sigma * (1.0 + gate * (1.0 - sigma))).astype(jnp.bfloat16)
     up_grad = (hidden_grad * gate * sigma).astype(jnp.bfloat16)
     gu_grad = jnp.concatenate([gate_grad, up_grad], axis=1)
-    grad_gu = matmul_tn(normed2, gu_grad).astype(jnp.bfloat16)
+    grad_gate = matmul_tn(normed2, gate_grad).astype(jnp.bfloat16)
+    grad_up = matmul_tn(normed2, up_grad).astype(jnp.bfloat16)
     normed2_grad = reduce_rows(matmul_nt(gu_grad, gu_w).astype(jnp.bfloat16), count, 2)
     second_part, gain_mlp_part = norm_back(normed2_grad, unit2, inverse2, gain_mlp)
     second_grad = grad_rows + second_part
@@ -972,10 +1243,14 @@
     grad_wo = matmul_tn(mixed, attn_grad).astype(jnp.bfloat16)
     mixed_grad = matmul_nt(attn_grad, wo_w).astype(jnp.bfloat16)
     qkv_grad = attend_blocks_back(slots, mixed_grad, kept, lse, cosine, sine, count, head)
-    grad_qkv = matmul_tn(qkv_grad, normed1).astype(jnp.bfloat16)
+    grad_qkv = matmul_tn(normed1, qkv_grad).astype(jnp.bfloat16)
     normed1_grad = reduce_rows(matmul(qkv_grad, qkv_w).astype(jnp.bfloat16), count, 2)
     first_part, gain_attn_part = norm_back(normed1_grad, unit1, inverse1, gain_attn)
-    return second_grad + first_part, (grad_gu, grad_down, grad_wo, grad_qkv), (gain_attn_part, gain_mlp_part)
+    return (
+        second_grad + first_part,
+        (grad_down, grad_gate, grad_up, grad_wo, grad_qkv),
+        (gain_attn_part, gain_mlp_part),
+    )
 
 
 def fast_shards(inputs, table, cotangent, wq, wk, wv, wo, w_gate, w_up, w_down, gain_attn, gain_mlp):
@@ -986,17 +1261,7 @@
     first_section = section == 0
     block = inputs.shape[1] * parts
     depth = wq.shape[1]
-    width = depth * count
-    q_rows = wo.shape[1] // count
-    hidden = w_gate.shape[2] // count
-
-    qkv_t = jnp.concatenate([wq[0], wk[0], wv[0]], axis=1).T
-    gains = jnp.concatenate([gain_attn, gain_mlp], axis=0).astype(jnp.float32)
-    gains = jnp.concatenate([gains] * 4, axis=0)
-    qkv_w, wo_w, gu_w, down_w, all_gains = spread_weights(
-        qkv_t, wo[0], w_gate[0], w_up[0], w_down[0], gains, count, head, 0
-    )
-    weights = (qkv_w, wo_w, gu_w, down_w, all_gains[:, 0], all_gains[:, 1])
+    q_cols = wq.shape[2] // count
 
     rows = lax.dynamic_index_in_dim(inputs, section, 0, keepdims=False)
     given = lax.dynamic_index_in_dim(cotangent, section, 0, keepdims=False)
@@ -1006,12 +1271,23 @@
     cosine, sine = rope_tables(table_row, block, head)
     tools = (count, slots, cosine, sine, head)
 
-    result0, context0 = fast_forward(rows, weights, 0, tools)
-    result1, context1 = fast_forward(result0, weights, 1, tools)
-    din1, grads1, gains1 = fast_backward(given, context1, weights, 1, tools)
-    moved1 = [section_move(g, 0) for g in grads1]
-    din0, grads0, gains0 = fast_backward(din1, context0, weights, 0, tools)
-    moved0 = [section_move(g, 1) for g in grads0]
+    qkv_t = jnp.concatenate([wq[0], wk[0], wv[0]], axis=1).T
+    gains = jnp.concatenate([gain_attn, gain_mlp], axis=0).astype(jnp.float32)
+    gains = jnp.concatenate([gains] * 4, axis=0)
+    unit1, _ = norm_stats(rows)
+    qkv_w, wo_w, gu_w, down_w, all_gains, normed1, out_grad = spread_weights(
+        qkv_t, wo[0], w_gate[0], w_up[0], w_down[0], gains,
+        unit1, given.astype(jnp.bfloat16), count, head, 0,
+    )
+    weights = [
+        (qkv_w[at], wo_w[at], gu_w[at], down_w[at], all_gains[at, 0], all_gains[at, 1])
+        for at in range(2)
+    ]
+
+    result0, context0 = fast_forward(rows, normed1, weights[0], tools)
+    result1, context1 = fast_forward(result0, None, weights[1], tools)
+    din1, grads1, gains1 = fast_backward(given, out_grad, context1, weights[1], tools)
+    din0, grads0, gains0 = fast_backward(din1, None, context0, weights[0], tools)
 
     def both(at0, at1):
         other = section_swap(jnp.where(first_section, at1, at0))
@@ -1022,49 +1298,30 @@
     outputs = both(result0, result1)
     input_grad = both(din0, din1)
 
-    def total(at):
-        mine = jnp.where(first_section, grads0[at], grads1[at]).astype(jnp.float32)
-        theirs = jnp.where(first_section, moved0[at], moved1[at]).astype(jnp.float32)
-        return (mine + theirs).astype(jnp.bfloat16)
-
-    gu_total, down_total, wo_total, qkv_total = [total(at) for at in range(4)]
-    cut = lambda value: value.reshape(value.shape[0], count, depth).transpose(1, 0, 2)
-    exchange = lambda value: lax.all_to_all(value, "dp", split_axis=0, concat_axis=0, tiled=True)
-    gu_own = exchange(gu_total.reshape(count, depth, 2 * hidden))
-    down_own = exchange(cut(down_total))
-    wo_own = exchange(cut(wo_total))
-    qkv_own = exchange(cut(qkv_total))
-    grad_gate = gu_own[:, :, :hidden].transpose(1, 0, 2).reshape(depth, -1).astype(jnp.float32)
-    grad_up = gu_own[:, :, hidden:].transpose(1, 0, 2).reshape(depth, -1).astype(jnp.float32)
-    grad_down = down_own.reshape(-1, depth).astype(jnp.float32)
-    grad_wo = wo_own.reshape(-1, depth).astype(jnp.float32)
-    grad_wq = qkv_own[:, :q_rows].reshape(-1, depth).astype(jnp.float32).T
+    gain_rows = jnp.stack(gains0 + gains1).reshape(2, 2, count * parts, -1).transpose(0, 2, 1, 3)
+    gain_rows = jnp.concatenate([gain_rows.reshape(2 * count * parts, 2, -1)] * 4, axis=1)
+    grad_down, grad_gate, grad_up, grad_wo, qkv_own, gain_sums = return_gradients(
+        grads0, grads1, gain_rows, count, 3
+    )
+    grad_wq = qkv_own[:, :, :q_cols].astype(jnp.float32).transpose(1, 0, 2).reshape(depth, -1)
     shared = count * head // wk.shape[2]
-    joined = qkv_own[:, q_rows:].astype(jnp.float32).reshape(count // shared, shared, 2, head, depth)
+    joined = qkv_own[:, :, q_cols:].astype(jnp.float32).reshape(count // shared, shared, depth, 2, head)
     joined = jnp.sum(joined, axis=1)
-    grad_wk = joined[:, 0].reshape(-1, depth).T
-    grad_wv = joined[:, 1].reshape(-1, depth).T
-
-    gain_rows = jnp.stack(
-        [jnp.stack(gains0), jnp.stack(gains1)]
-    ).reshape(2, 2, count * parts, -1).transpose(0, 2, 1, 3)
-    gain_piece = gain_rows.shape[-1]
-    gain_rows = gain_rows.reshape(2 * count * parts, 2 * gain_piece)
-    gain_sums = lax.psum_scatter(
-        gain_rows, ("section", "dp", "tensor"), scatter_dimension=0, tiled=True
-    ).reshape(2, gain_piece)
+    grad_wk = joined[:, :, 0].transpose(1, 0, 2).reshape(depth, -1)
+    grad_wv = joined[:, :, 1].transpose(1, 0, 2).reshape(depth, -1)
+    wide = lambda value: value.astype(jnp.float32)[None]
     return (
         outputs,
         input_grad,
         grad_wq[None],
         grad_wk[None],
         grad_wv[None],
-        grad_wo[None],
-        grad_gate[None],
-        grad_up[None],
-        grad_down[None],
+        wide(grad_wo),
+        wide(grad_gate),
+        wide(grad_up),
+        wide(grad_down),
         gain_sums[:1],
-        gain_sums[1:],
+        gain_sums[1:2],
     )
 
 

time: 1190 us -> 1090 us (0.916)
  waiting for transfers between devices: 90.3 us -> 0.01 us
  Pallas kernels: 782 us -> 872 us
  blocking collectives: 44.5 us -> 0 us
  starting transfers between devices: 40.5 us -> 2.03 us
  local copies, waits for them, and re-layouts: 42.8 us -> 23.8 us
    ppermute x8 -> x0, waiting for transfers between devices: 82.7 us -> none  [section_move(): return lax.ppermute(value, 'section', [(source, 1 - source)])]
    pallas_call x1, Pallas kernels: 208 us -> 255 us  [spread_weights(): pl.pallas_call(functools.partial(spread_kernel, count, heads), out_shape=...]
    unnamed x1 -> x0, blocking collectives: 44.5 us -> none
    pallas_call x16 -> x15, Pallas kernels: 548 us -> 591 us  [the longest x8 241 us: reduce_rows(): pl.pallas_call(functools.partial(reduce_kernel, count), out_shape=jax.Sha...]
    convert_element_type x7 -> x0, other arithmetic: 22.5 us -> none  [the longest x4 14.2 us: total(): return (mine + theirs).astype(jnp.bfloat16)]
    convert_element_type x5 -> x1, local copies, waits for them, and re-layouts: 22.7 us -> 1.78 us  [fast_shards(): given.astype(jnp.bfloat16)]
    ppermute x8 -> x0, starting transfers between devices: 18.6 us -> none  [section_move(): return lax.ppermute(value, 'section', [(source, 1 - source)])]
    all_to_all x4 -> x0, starting transfers between devices: 16.8 us -> none  [fast_shards(): lax.all_to_all(value, 'dp', split_axis=0, concat_axis=0, tiled=True)]
  transfers between devices with their start and end apart: 14 -> 2, of which waited for: 4 -> 0; matrix products, arithmetic and copies ran while one was open for 10% -> 8% of each run, Pallas kernels for 27% -> 29%
where the time goes in v2:
time: 1090 us; the launch traced here: 1070 us
  Pallas kernels  872 us (80%)
  matrix products  125 us (11%)
  other arithmetic  50.3 us (5%)
  local copies, waits for them, and re-layouts  23.8 us (2%)
    pallas_call x1, Pallas kernels, spread_weights(): pl.pallas_call(functools.partial(spread_kernel, count, heads), out_shape=...  255 us
    pallas_call x8, Pallas kernels, reduce_rows(): pl.pallas_call(functools.partial(reduce_kernel, count), out_shape=jax.Sha...  241 us
    pallas_call x1, Pallas kernels, return_gradients(): pl.pallas_call(functools.partial(return_kernel, count), out_shape=(shape(...  188 us
    pallas_call x6, Pallas kernels, gather_rows(): pl.pallas_call(functools.partial(gather_kernel, count), out_shape=jax.Sha...  162 us
    dot_general x18, matrix products, dot(): lax.dot_general(left, right, (contract, ((), ())), preferred_element_type...  78.1 us
    dot_general x8, matrix products, matmul(): return jnp.dot(left, right, preferred_element_type=jnp.float32)  46.4 us
  transfers between devices with their start and end apart: 2, of which 0 were waited for; matrix products, arithmetic and copies ran while one was open for 8% of the time, Pallas kernels for 29%

profile of v2, /device:TPU:0, one launch (start us, length us, event | category | flops | bytes accessed | tf_op | source)
XLA Modules:
  0.0 1074.4 jit_solution(16350171367102663553)
XLA Ops:
  12.7 254.7 %spread_weights.1 = (bf16[2,256,2048]{2,1,0:T(8,128)(2,1)}, bf16[2,128,2048]{2,1,0:T(8,128)(2,1)}, bf16[2,2048,1024]{2,1,0:T(8,128)(2,1)}, bf16[2,512,2048]{2,1,...) custom-call(bf16[1536,256]{1,0:T(8,128)(2,1)} %maximum_bitcast_fusion.refs_0_, ...), custom_call_target="tpu_custom_call" | custom-call | bytes 811800000 | tf_op jit(solution)/shard_map/spread_weights/pallas_call | solution.py:838
  270.2 4.7 fusion.38.qkv_ref
  276.8 5.6 attend_blocks.2
  282.4 4.2 convolution_convert_fusion.5.p_ref
  286.6 37.0 %reduce_rows.8 = f32[64,2048]{1,0:T(8,128)} custom-call(bf16[1024,2048]{1,0:T(8,128)(2,1)} %convolution_convert_fusion.5.p_ref), custom_call_target="tpu_custom_call" | custom-call | bytes 107010000 | tf_op jit(solution)/shard_map/reduce_rows/pallas_call | solution.py:694
  325.7 26.9 %gather_rows.6 = bf16[1024,2048]{1,0:T(8,128)(2,1)} custom-call(bf16[64,2048]{1,0:T(8,128)(2,1)} %multiply_convert_fusion.8.x_ref), custom_call_target="tpu_custom_call" | custom-call | bytes 99630000 | tf_op jit(solution)/shard_map/gather_rows/pallas_call | solution.py:603
  352.6 7.6 fusion.6
  364.8 4.4 convolution_convert_fusion.3.p_ref
  369.2 29.3 %reduce_rows.9 = f32[64,2048]{1,0:T(8,128)} custom-call(bf16[1024,2048]{1,0:T(8,128)(2,1)} %convolution_convert_fusion.3.p_ref), custom_call_target="tpu_custom_call" | custom-call | bytes 107010000 | tf_op jit(solution)/shard_map/reduce_rows/pallas_call | solution.py:694
  400.6 26.9 %gather_rows.7 = bf16[1024,2048]{1,0:T(8,128)(2,1)} custom-call(bf16[64,2048]{1,0:T(8,128)(2,1)} %multiply_convert_fusion.7.x_ref), custom_call_target="tpu_custom_call" | custom-call | bytes 99630000 | tf_op jit(solution)/shard_map/gather_rows/pallas_call | solution.py:603
  427.5 4.7 fusion.35.qkv_ref
  432.2 5.6 attend_blocks.3
  437.8 4.4 convolution_convert_fusion.4.p_ref
  442.2 29.3 %reduce_rows.10 = f32[64,2048]{1,0:T(8,128)} custom-call(bf16[1024,2048]{1,0:T(8,128)(2,1)} %convolution_convert_fusion.4.p_ref), custom_call_target="tpu_custom_call" | custom-call | bytes 107010000 | tf_op jit(solution)/shard_map/reduce_rows/pallas_call | solution.py:694
  473.6 26.9 %gather_rows.8 = bf16[1024,2048]{1,0:T(8,128)(2,1)} custom-call(bf16[64,2048]{1,0:T(8,128)(2,1)} %multiply_convert_fusion.6.x_ref), custom_call_target="tpu_custom_call" | custom-call | bytes 99630000 | tf_op jit(solution)/shard_map/gather_rows/pallas_call | solution.py:603
  500.5 10.2 fusion.2
  510.6 6.4 multiply_convert_fusion.3
  518.4 6.1 fusion.11.p_ref
  524.5 29.3 %reduce_rows.12 = f32[64,2048]{1,0:T(8,128)} custom-call(bf16[1024,2048]{1,0:T(8,128)(2,1)} %fusion.11.p_ref), custom_call_target="tpu_custom_call" | custom-call | bytes 107010000 | tf_op jit(solution)/shard_map/reduce_rows/pallas_call | solution.py:694
  557.4 27.0 %gather_rows.9 = bf16[1024,2048]{1,0:T(8,128)(2,1)} custom-call(bf16[64,2048]{1,0:T(8,128)(2,1)} %get-tuple-element.107.x_ref), custom_call_target="tpu_custom_call" | custom-call | bytes 99630000 | tf_op jit(solution)/shard_map/gather_rows/pallas_call | solution.py:603
  584.4 4.3 convolution_convert_fusion.17.grad_ref
  588.7 7.6 attend_blocks_back.2
  596.2 4.7 convolution_convert_fusion.1.p_ref
  600.9 29.3 %reduce_rows.13 = f32[64,2048]{1,0:T(8,128)} custom-call(bf16[1024,2048]{1,0:T(8,128)(2,1)} %convolution_convert_fusion.1.p_ref), custom_call_target="tpu_custom_call" | custom-call | bytes 107010000 | tf_op jit(solution)/shard_map/reduce_rows/pallas_call | solution.py:694
  631.5 6.3 convolution_convert_fusion.2.p_ref
  637.8 29.1 %reduce_rows.11 = f32[64,2048]{1,0:T(8,128)} custom-call(bf16[1024,2048]{1,0:T(8,128)(2,1)} %convolution_convert_fusion.2.p_ref), custom_call_target="tpu_custom_call" | custom-call | bytes 107010000 | tf_op jit(solution)/shard_map/reduce_rows/pallas_call | solution.py:694
  666.9 3.0 add_bitcast_fusion
  671.7 27.1 %gather_rows.10 = bf16[1024,2048]{1,0:T(8,128)(2,1)} custom-call(bf16[64,2048]{1,0:T(8,128)(2,1)} %get-tuple-element.124.x_ref), custom_call_target="tpu_custom_call" | custom-call | bytes 99630000 | tf_op jit(solution)/shard_map/gather_rows/pallas_call | solution.py:603
  698.8 6.9 multiply_convert_fusion.1
  707.1 8.3 fusion.8.p_ref
  715.4 29.1 %reduce_rows.14 = f32[64,2048]{1,0:T(8,128)} custom-call(bf16[1024,2048]{1,0:T(8,128)(2,1)} %fusion.8.p_ref), custom_call_target="tpu_custom_call" | custom-call | bytes 107010000 | tf_op jit(solution)/shard_map/reduce_rows/pallas_call | solution.py:694
  747.8 27.1 %gather_rows.11 = bf16[1024,2048]{1,0:T(8,128)(2,1)} custom-call(bf16[64,2048]{1,0:T(8,128)(2,1)} %get-tuple-element.103.x_ref), custom_call_target="tpu_custom_call" | custom-call | bytes 99630000 | tf_op jit(solution)/shard_map/gather_rows/pallas_call | solution.py:603
  774.9 4.3 convolution_convert_fusion.16.grad_ref
  779.2 7.6 attend_blocks_back.3
  786.7 4.7 convolution_convert_fusion.p_ref
  791.4 29.1 %reduce_rows.15 = f32[64,2048]{1,0:T(8,128)} custom-call(bf16[1024,2048]{1,0:T(8,128)(2,1)} %convolution_convert_fusion.p_ref), custom_call_target="tpu_custom_call" | custom-call | bytes 107010000 | tf_op jit(solution)/shard_map/reduce_rows/pallas_call | solution.py:694
  824.5 5.1 convolution_convert_fusion.8.refs_5_
  829.6 4.0 convolution_convert_fusion.7.refs_6_
  833.6 3.8 convolution_convert_fusion.6.refs_7_
  842.8 3.7 convolution_convert_fusion.11.refs_0_
  846.5 3.8 convolution_convert_fusion.10.refs_1_
  850.4 4.1 convolution_convert_fusion.9.refs_2_
  857.0 2.4 convolution_convert_fusion.13.refs_4_
  860.1 187.9 %return_gradients.1 = (bf16[4096,256]{1,0:T(8,128)(2,1)}, bf16[256,4096]{1,0:T(8,128)(2,1)}, bf16[256,4096]{1,0:T(8,128)(2,1)}, bf16[1024,256]{1,0:T(8,128)(2,1)...) custom-call(bf16[512,2048]{1,0:T(8,128)(2,1)} %convolution_convert_fusion.11.refs_0_, ...), custom_call_target="tpu_custom_call" | custom-call | bytes 738000000 | tf_op jit(solution)/shard_map/return_gradients/pallas_call | solution.py:989
  1050.5 4.2 bitcast_convert_fusion.2
  1054.7 2.5 bitcast_convert_fusion.1
  1062.9 2.6 copy.60
  1071.6 2.4 maximum_select_fusion.1
  (131 shorter events, 66.9 us)
Async XLA Ops:
  275.0 7.5 copy-start.16
  286.6 37.0 %copy-start.2 = (f32[2,64,2048]{2,1,0:T(8,128)S(1)}, f32[2,64,2048]{2,1,0:T(8,128)}, u32[]{:S(2)}) copy-start(f32[2,64,2048]{2,1,0:T(8,128)} %param.12) | copy-start | bytes 3145732
  360.2 2.0 copy-start.3
  362.3 2.6 copy-start.23
  362.9 6.3 copy-start.17
  500.4 10.2 copy-start.21
  500.4 10.2 copy-start.24
  500.4 18.0 %slice-start = ((s8[8388608]{0:T(1024)(128)(4,1)}), s8[4194304]{0:T(1024)(128)(4,1)S(1)}, s32[]{:S(2)}) async-start(s8[8388608]{0:T(1024)(128)(4,1)} %bitcast.194), calls=%async_computation | async-start | bytes 8388608
  510.6 7.8 slice-start.1
  517.1 1.0 copy-start.25
  517.1 1.4 copy-start.27
  669.9 399.3 %collective-permute-start = (f32[64,2048]{1,0:T(8,128)}, f32[64,2048]{1,0:T(8,128)}, u32[]{:S(2)}, u32[]{:S(2)}) collective-permute-start(f32[64,2048]{1,0:T(8,128)} %get-tuple-element.123), channel_id=1, source_target_pairs={{0,16},{16,0},{1,17},{17,1},{2,18},{18,2},{3,19},{19,3},{4,20},{20... | collective-permute-start | bytes 1572872 | tf_op jit(solution)/shard_map/ppermute | solution.py:1203
  705.7 1.0 copy-start.29
  705.8 1.3 copy-start.31
  820.5 4.0 copy-start.22
  824.2 5.4 copy-start.6
  824.2 5.4 copy-start.28
  824.2 247.4 %collective-permute-start.1 = (f32[64,2048]{1,0:T(8,128)}, f32[64,2048]{1,0:T(8,128)}, u32[]{:S(2)}, u32[]{:S(2)}) collective-permute-start(f32[64,2048]{1,0:T(8,128)} %get-tuple-element.101), channel_id=1, source_target_pairs={{0,16},{16,0},{1,17},{17,1},{2,18},{18,2},{3,19},{19,3},{4,20},{20... | collective-permute-start | bytes 1572872 | tf_op jit(solution)/shard_map/ppermute | solution.py:1203
  829.6 4.0 copy-start.26
  833.6 3.8 copy-start
  833.6 3.8 copy-start.15
  837.5 2.4 copy-start.5
  837.5 2.5 copy-start.8
  840.0 2.4 copy-start.7
  840.0 2.9 copy-start.18
  842.8 3.7 copy-start.4
  842.8 3.7 copy-start.32
  846.5 3.8 copy-start.30
  850.4 4.1 copy-start.1
  850.4 4.1 copy-start.14
  854.4 1.5 copy-start.9
  854.4 2.5 copy-start.20
  1050.5 4.3 copy-start.11
  1054.7 2.5 copy-start.10
  1059.6 9.7 copy-start.13
  1060.3 5.2 copy-start.19
  1062.9 8.7 copy-start.12

commit v3 on v0

--- a/solution.py
+++ b/solution.py
@@ -1,11 +1,15 @@
+import functools
 import math
 
 import jax
 import jax.numpy as jnp
 from jax import lax
+from jax.experimental import pallas as pl
+from jax.experimental.pallas import tpu as pltpu
 from jax.sharding import PartitionSpec as P
 
 HEAD_SIZE = 64
+SECTION, DP, TENSOR = "section", "dp", "tensor"
 
 
 epsilon = 1e-05
@@ -70,7 +74,7 @@
 def block_layout(table, micro, groups, block):
     layout_row = lax.dynamic_index_in_dim(table, micro, 0, keepdims=False)
     span = groups // 2
-    mine = lax.dynamic_index_in_dim(layout_row, lax.axis_index("dp"), 0, keepdims=False)
+    mine = lax.dynamic_index_in_dim(layout_row, lax.axis_index(DP), 0, keepdims=False)
     sequence = mine // span
     place = mine % span
     slot_ids = jnp.arange(groups, dtype=jnp.int32)
@@ -159,7 +163,7 @@
 
 def layer_forward(rows, table, micro, weights, groups, heads_kv, head):
     wq, wk, wv, wo, w_gate, w_up, w_down, gain_attn, gain_mlp = weights
-    full = lax.all_gather(rows, "tensor", axis=0, tiled=True)
+    full = lax.all_gather(rows, TENSOR, axis=0, tiled=True)
     block = full.shape[0]
     slots, positions = block_layout(table, micro, groups, block)
     unit1, inverse1 = norm_stats(full)
@@ -168,22 +172,22 @@
     key = rotate(matmul(normed1, wk), positions, head).astype(jnp.bfloat16)
     value_rows = matmul(normed1, wv).astype(jnp.bfloat16)
     key_all, value_all = (
-        lax.all_gather(key, "dp", axis=0, tiled=True),
-        lax.all_gather(value_rows, "dp", axis=0, tiled=True),
+        lax.all_gather(key, DP, axis=0, tiled=True),
+        lax.all_gather(value_rows, DP, axis=0, tiled=True),
     )
     kv_width = key.shape[1]
     key_seq = key_all.reshape(groups, block, kv_width)[slots].reshape(-1, kv_width)
     value_seq = value_all.reshape(groups, block, kv_width)[slots].reshape(-1, kv_width)
     mixed, log_total = attend(query_rows, key_seq, value_seq, positions, heads_kv, head)
-    second = rows + lax.psum_scatter(matmul(mixed, wo), "tensor", scatter_dimension=0, tiled=True)
-    full_second = lax.all_gather(second, "tensor", axis=0, tiled=True)
+    second = rows + lax.psum_scatter(matmul(mixed, wo), TENSOR, scatter_dimension=0, tiled=True)
+    full_second = lax.all_gather(second, TENSOR, axis=0, tiled=True)
     unit2, inverse2 = norm_stats(full_second)
     normed2 = (unit2 * gain_mlp.astype(jnp.float32)).astype(jnp.bfloat16)
     gate = matmul(normed2, w_gate)
     upper = matmul(normed2, w_up)
     hidden = (jax.nn.silu(gate) * upper).astype(jnp.bfloat16)
     result = second + lax.psum_scatter(
-        matmul(hidden, w_down), "tensor", scatter_dimension=0, tiled=True
+        matmul(hidden, w_down), TENSOR, scatter_dimension=0, tiled=True
     )
     return (
         result,
@@ -221,7 +225,7 @@
         positions,
     ) = context
     block = full.shape[0]
-    out_grad = lax.all_gather(grad_rows.astype(jnp.bfloat16), "tensor", axis=0, tiled=True)
+    out_grad = lax.all_gather(grad_rows.astype(jnp.bfloat16), TENSOR, axis=0, tiled=True)
     grad_down = matmul(hidden.T, out_grad)
     hidden_grad = matmul(out_grad, w_down.T)
     sigma = jax.nn.sigmoid(gate)
@@ -238,17 +242,17 @@
     piece_width = gain_mlp_terms.shape[0] // (groups * parts)
     second_part, gain_mlp_part = (
         lax.psum_scatter(
-            second_terms.astype(jnp.bfloat16), "tensor", scatter_dimension=0, tiled=True
+            second_terms.astype(jnp.bfloat16), TENSOR, scatter_dimension=0, tiled=True
         ).astype(jnp.float32),
         lax.psum_scatter(
             gain_mlp_terms.reshape(groups, parts, piece_width).astype(jnp.bfloat16),
-            "tensor",
+            TENSOR,
             scatter_dimension=1,
             tiled=True,
         ).astype(jnp.float32),
     )
     second_grad = grad_rows + second_part
-    attn_grad = lax.all_gather(second_grad.astype(jnp.bfloat16), "tensor", axis=0, tiled=True)
+    attn_grad = lax.all_gather(second_grad.astype(jnp.bfloat16), TENSOR, axis=0, tiled=True)
     grad_wo = matmul(mixed.T, attn_grad)
     blended_gradient = matmul(attn_grad, wo.T).astype(jnp.bfloat16)
     query_grad, key_seq_grad, value_seq_grad = attend_back(
@@ -267,10 +271,10 @@
     )
     key_own, value_own = (
         lax.psum_scatter(
-            key_spread.astype(jnp.bfloat16), "dp", scatter_dimension=0, tiled=True
+            key_spread.astype(jnp.bfloat16), DP, scatter_dimension=0, tiled=True
         ).astype(jnp.float32),
         lax.psum_scatter(
-            value_spread.astype(jnp.bfloat16), "dp", scatter_dimension=0, tiled=True
+            value_spread.astype(jnp.bfloat16), DP, scatter_dimension=0, tiled=True
         ).astype(jnp.float32),
     )
     query_round = unrotate(query_grad, positions, head).astype(jnp.bfloat16)
@@ -286,10 +290,10 @@
         normed1_grad, unit1, inverse1, gain_attn.astype(jnp.float32)
     )
     first_part, gain_attn_part = (
-        lax.psum_scatter(first_terms, "tensor", scatter_dimension=0, tiled=True),
+        lax.psum_scatter(first_terms, TENSOR, scatter_dimension=0, tiled=True),
         lax.psum_scatter(
             gain_attn_terms.reshape(groups, parts, piece_width),
-            "tensor",
+            TENSOR,
             scatter_dimension=1,
             tiled=True,
         ),
@@ -314,51 +318,51 @@
 def reduce_grads(pieces):
     return (
         lax.psum_scatter(
-            pieces[0].astype(jnp.bfloat16), "dp", scatter_dimension=0, tiled=True
+            pieces[0].astype(jnp.bfloat16), DP, scatter_dimension=0, tiled=True
         ).astype(jnp.float32),
         lax.psum_scatter(
-            pieces[1].astype(jnp.bfloat16), "dp", scatter_dimension=0, tiled=True
+            pieces[1].astype(jnp.bfloat16), DP, scatter_dimension=0, tiled=True
         ).astype(jnp.float32),
         lax.psum_scatter(
-            pieces[2].astype(jnp.bfloat16), "dp", scatter_dimension=0, tiled=True
+            pieces[2].astype(jnp.bfloat16), DP, scatter_dimension=0, tiled=True
         ).astype(jnp.float32),
         lax.psum_scatter(
-            pieces[3].astype(jnp.bfloat16), "dp", scatter_dimension=1, tiled=True
+            pieces[3].astype(jnp.bfloat16), DP, scatter_dimension=1, tiled=True
         ).astype(jnp.float32),
         lax.psum_scatter(
-            pieces[4].astype(jnp.bfloat16), "dp", scatter_dimension=0, tiled=True
+            pieces[4].astype(jnp.bfloat16), DP, scatter_dimension=0, tiled=True
         ).astype(jnp.float32),
         lax.psum_scatter(
-            pieces[5].astype(jnp.bfloat16), "dp", scatter_dimension=0, tiled=True
+            pieces[5].astype(jnp.bfloat16), DP, scatter_dimension=0, tiled=True
         ).astype(jnp.float32),
         lax.psum_scatter(
-            pieces[6].astype(jnp.bfloat16), "dp", scatter_dimension=1, tiled=True
+            pieces[6].astype(jnp.bfloat16), DP, scatter_dimension=1, tiled=True
         ).astype(jnp.float32),
         lax.psum_scatter(
-            pieces[7].astype(jnp.bfloat16), "dp", scatter_dimension=0, tiled=True
+            pieces[7].astype(jnp.bfloat16), DP, scatter_dimension=0, tiled=True
         ).astype(jnp.float32),
         lax.psum_scatter(
-            pieces[8].astype(jnp.bfloat16), "dp", scatter_dimension=0, tiled=True
+            pieces[8].astype(jnp.bfloat16), DP, scatter_dimension=0, tiled=True
         ).astype(jnp.float32),
     )
 
 
-def shards(inputs, table, cotangent, wq, wk, wv, wo, w_gate, w_up, w_down, gain_attn, gain_mlp):
-    groups = lax.axis_size("dp")
-    parts = lax.axis_size("tensor")
+def general_shards(inputs, table, cotangent, wq, wk, wv, wo, w_gate, w_up, w_down, gain_attn, gain_mlp):
+    groups = lax.axis_size(DP)
+    parts = lax.axis_size(TENSOR)
     micro_count = inputs.shape[0]
-    section = lax.axis_index("section")
+    section = lax.axis_index(SECTION)
     first_section = section == 0
     weights = (
-        lax.all_gather(wq[0], "dp", axis=0, tiled=True),
-        lax.all_gather(wk[0], "dp", axis=0, tiled=True),
-        lax.all_gather(wv[0], "dp", axis=0, tiled=True),
-        lax.all_gather(wo[0], "dp", axis=1, tiled=True),
-        lax.all_gather(w_gate[0], "dp", axis=0, tiled=True),
-        lax.all_gather(w_up[0], "dp", axis=0, tiled=True),
-        lax.all_gather(w_down[0], "dp", axis=1, tiled=True),
-        lax.all_gather(gain_attn[0], "dp", axis=0, tiled=True),
-        lax.all_gather(gain_mlp[0], "dp", axis=0, tiled=True),
+        lax.all_gather(wq[0], DP, axis=0, tiled=True),
+        lax.all_gather(wk[0], DP, axis=0, tiled=True),
+        lax.all_gather(wv[0], DP, axis=0, tiled=True),
+        lax.all_gather(wo[0], DP, axis=1, tiled=True),
+        lax.all_gather(w_gate[0], DP, axis=0, tiled=True),
+        lax.all_gather(w_up[0], DP, axis=0, tiled=True),
+        lax.all_gather(w_down[0], DP, axis=1, tiled=True),
+        lax.all_gather(gain_attn[0], DP, axis=0, tiled=True),
+        lax.all_gather(gain_mlp[0], DP, axis=0, tiled=True),
     )
     head = HEAD_SIZE
     heads_kv = wk.shape[2] // head
@@ -373,7 +377,7 @@
         produced.append(result)
         saved.append(context)
         if step < micro_count:
-            received = passed_along(result, "section", 1)
+            received = passed_along(result, SECTION, 1)
     stacked = jnp.stack(produced)
     outputs = jnp.where(first_section, stacked[:micro_count], stacked[1:])[None]
     returned = jnp.zeros_like(inputs[0])
@@ -388,7 +392,7 @@
         )
         returned_list.append(din)
         if step < micro_count:
-            returned = passed_along(din.astype(jnp.bfloat16), "section", -1).astype(din.dtype)
+            returned = passed_along(din.astype(jnp.bfloat16), SECTION, -1).astype(din.dtype)
         totals = (
             pieces
             if totals is None
@@ -424,32 +428,1533 @@
     )
 
 
+MESH = pl.DeviceIdType.MESH
+SUBS = 2
+HBM = pl.BlockSpec(memory_space=pl.ANY)
+VMEM = pl.BlockSpec(memory_space=pltpu.VMEM)
+SMEM = pl.BlockSpec(memory_space=pltpu.SMEM)
+NARROW, WIDE = jnp.bfloat16, jnp.float32
+
+
+def ring_place(index, count):
+    return jnp.where(lax.rem(index, 2) == 0, index // 2, count - (index + 1) // 2)
+
+
+def ring_index(place, count):
+    place = lax.rem(place + 2 * count, count)
+    return jnp.where(place < count // 2, 2 * place, 2 * count - 1 - 2 * place)
+
+
+def greet(others):
+    barrier = pltpu.get_barrier_semaphore()
+    for other in others:
+        pl.semaphore_signal(barrier, inc=1, device_id=other, device_id_type=MESH)
+    pl.semaphore_wait(barrier, len(others))
+
+
+def remote(source, target, send, recv, device):
+    return pltpu.make_async_remote_copy(
+        source, target, send, recv, device_id=device, device_id_type=MESH
+    )
+
+
+def partners(me, count):
+    half = count // 2
+    side, inside = me // half, lax.rem(me, half)
+    peers = [(1 - side) * half + lax.rem(inside + k, half) for k in range(half)]
+    peers += [side * half + lax.rem(inside + k, half) for k in range(1, half)]
+    origins = [(1 - side) * half + lax.rem(inside + half - k, half) for k in range(half)]
+    origins += [side * half + lax.rem(inside + half - k, half) for k in range(1, half)]
+    return peers, origins
+
+
+def aligned(start, size):
+    return pl.ds(pl.multiple_of(start, size), size)
+
+
+def tiles(size, tile):
+    return [slice(at, at + tile) for at in range(0, size, tile)]
+
+
+def loop(start, stop, body):
+    if stop - start == 1:
+        body(start)
+    elif stop > start:
+
+        def step(at, carry):
+            body(at)
+            return carry
+
+        lax.fori_loop(start, stop, step, 0)
+
+
+def dot(left, right, contract):
+    return lax.dot_general(
+        left, right, (contract, ((), ())), preferred_element_type=jnp.float32
+    )
+
+
+class Names:
+    def __init__(self, **values):
+        self.__dict__.update(values)
+
+
+class Work:
+    def __init__(self):
+        self.items = []
+
+    def add(self, body, count=1):
+        self.items.append((body, 0, count))
+
+    def first(self, body):
+        self.items.insert(0, (body, 0, 1))
+
+    def do(self, some=1 << 20):
+        while some > 0 and self.items:
+            body, start, stop = self.items.pop(0)
+            until = min(stop, start + some)
+            loop(start, until, body)
+            some -= until - start
+            if until < stop:
+                self.items.insert(0, (body, until, stop))
+
+
+class Copies:
+    def __init__(self, sem):
+        self.sem = sem
+        self.used = 0
+
+    def __call__(self, source, target):
+        copy = pltpu.make_async_copy(source, target, self.sem.at[self.used])
+        self.used += 1
+        copy.start()
+        return copy
+
+
+class Ring:
+    def __init__(self):
+        self.count = lax.axis_size(DP)
+        self.far = self.count // 2
+        self.me = lax.axis_index(DP)
+        self.core = lax.axis_index(TENSOR)
+        self.place = ring_place(self.me, self.count)
+        self.near = tuple({DP: ring_index(self.place + step, self.count)} for step in (1, -1))
+        self.side = {TENSOR: 1 - self.core}
+
+    def everyone(self):
+        return [*self.near, self.side]
+
+    def index(self, steps):
+        return ring_index(self.place + steps, self.count)
+
+    def orders(self):
+        for k in range(SUBS):
+            yield k, 0
+            yield SUBS - 1 - k, 1
+
+
+def gather_scratch(count):
+    far = count // 2
+    dma = pltpu.SemaphoreType.DMA
+    return [
+        dma((2, far, SUBS)), dma((2, far, SUBS)), dma((count, SUBS)), dma((count, SUBS)), dma((1,))
+    ]
+
+
+class Gather:
+    def __init__(self, ring, x_ref, o_ref, sems):
+        self.ring = ring
+        self.x_ref, self.o_ref = x_ref, o_ref
+        self.ring_send, self.ring_recv, self.side_send, self.side_recv, self.own_sem = sems
+        self.rows = x_ref.shape[0]
+        self.piece = self.rows // SUBS
+        self.sends = []
+
+    def spot(self, steps, sub, core):
+        start = (self.ring.index(steps) * 2 + core) * self.rows + sub * self.piece
+        return self.o_ref.at[aligned(start, self.piece), :]
+
+    def mine(self, steps, sub):
+        if steps == 0:
+            return self.x_ref.at[sub * self.piece : (sub + 1) * self.piece, :]
+        return self.spot(steps, sub, self.ring.core)
+
+    def travels(self, way, hop, sub):
+        return hop < self.ring.far or (sub < SUBS // 2) == (way == 0)
+
+    def go(self, copy):
+        copy.start()
+        self.sends.append(copy)
+
+    def pass_on(self, way, hop, sub):
+        steps = 1 - hop if way == 0 else hop - 1
+        self.go(
+            remote(
+                self.mine(steps, sub),
+                self.spot(steps, sub, self.ring.core),
+                self.ring_send.at[way, hop - 1, sub],
+                self.ring_recv.at[way, hop - 1, sub],
+                self.ring.near[way],
+            )
+        )
+
+    def hand_over(self, steps, sub, slot):
+        self.go(
+            remote(
+                self.mine(steps, sub),
+                self.spot(steps, sub, self.ring.core),
+                self.side_send.at[slot, sub],
+                self.side_recv.at[slot, sub],
+                self.ring.side,
+            )
+        )
+
+    def start(self):
+        for sub, way in self.ring.orders():
+            self.pass_on(way, 1, sub)
+        for sub in range(SUBS):
+            self.hand_over(0, sub, 0)
+        self.own = pltpu.make_async_copy(
+            self.x_ref,
+            self.o_ref.at[aligned((self.ring.me * 2 + self.ring.core) * self.rows, self.rows), :],
+            self.own_sem.at[0],
+        )
+        self.own.start()
+
+    def hop(self, hop):
+        far, count = self.ring.far, self.ring.count
+        for sub, way in self.ring.orders():
+            if not self.travels(way, hop, sub):
+                continue
+            steps = -hop if way == 0 else hop
+            here = self.spot(steps, sub, self.ring.core)
+            remote(
+                here, here, self.ring_send.at[way, hop - 1, sub],
+                self.ring_recv.at[way, hop - 1, sub], self.ring.near[way],
+            ).wait_recv()
+            if hop < far and self.travels(way, hop + 1, sub):
+                self.pass_on(way, hop + 1, sub)
+            self.hand_over(steps, sub, hop if way == 0 or hop == far else count - hop)
+
+    def side_arrived(self, steps):
+        slot = -steps if steps <= 0 else self.ring.count - steps
+        slot = self.ring.far if abs(steps) == self.ring.far else slot
+        for sub in range(SUBS):
+            there = self.spot(steps, sub, 1 - self.ring.core)
+            remote(
+                there, there, self.side_send.at[slot, sub], self.side_recv.at[slot, sub],
+                self.ring.side,
+            ).wait_recv()
+
+    def around(self, hop):
+        return (-hop, hop) if hop < self.ring.far else (-hop,)
+
+    def sent(self):
+        for copy in self.sends:
+            copy.wait_send()
+
+    def finish(self):
+        self.own.wait()
+        self.side_arrived(0)
+        for hop in range(1, self.ring.far + 1):
+            for steps in self.around(hop):
+                self.side_arrived(steps)
+        self.sent()
+
+    def run(self, use, work, some):
+        self.start()
+        self.own.wait()
+        self.side_arrived(0)
+        use([self.ring.index(0)])
+        for hop in range(1, self.ring.far + 1):
+            work.do(some)
+            self.hop(hop)
+            for steps in self.around(hop):
+                self.side_arrived(steps)
+            use([self.ring.index(steps) for steps in self.around(hop)])
+        self.sent()
+
+
+def chosen(at, indices):
+    return indices[0] if len(indices) == 1 else indices[0] + (indices[1] - indices[0]) * at
+
+
+def reduce_scratch(count, rows, width):
+    far = count // 2
+    dma = pltpu.SemaphoreType.DMA
+    return [
+        pltpu.VMEM((count * 2 * rows, width), NARROW),
+        pltpu.VMEM((count, rows, width), NARROW),
+        pltpu.VMEM((2, far, rows, width), NARROW),
+        pltpu.VMEM((2, far, rows, width), NARROW),
+        dma((2, far, SUBS)), dma((2, far, SUBS)), dma((count,)), dma((count,)),
+    ]
+
+
+class Reduce:
+    def __init__(self, ring, scratch):
+        self.ring = ring
+        self.parts, self.beside, self.outgoing, self.incoming = scratch[:4]
+        self.ring_send, self.ring_recv, self.side_send, self.side_recv = scratch[4:]
+        self.rows = self.beside.shape[1]
+        self.piece = self.rows // SUBS
+
+    def span(self, sub):
+        return slice(sub * self.piece, (sub + 1) * self.piece)
+
+    def spot(self, steps, core, sub=None):
+        start = (self.ring.index(steps) * 2 + core) * self.rows
+        if sub is None:
+            return aligned(start, self.rows)
+        return aligned(start + sub * self.piece, self.piece)
+
+    def make(self, *several):
+        self.produce([self.ring.index(steps) for steps in several], self.parts)
+        for steps in several:
+            slot = len(self.slots)
+            copy = remote(
+                self.parts.at[self.spot(steps, 1 - self.ring.core), :], self.beside.at[slot],
+                self.side_send.at[slot], self.side_recv.at[slot], self.ring.side,
+            )
+            copy.start()
+            self.slots[steps] = (slot, copy)
+
+    def mine(self, steps, sub):
+        slot, copy = self.slots[steps]
+        if steps not in self.joined:
+            copy.wait_recv()
+            self.joined.add(steps)
+        return self.parts[self.spot(steps, self.ring.core, sub), :].astype(
+            jnp.float32
+        ) + self.beside[slot, self.span(sub), :].astype(jnp.float32)
+
+    def travels(self, way, step, sub):
+        return step > 1 or (sub < SUBS // 2) == (way == 0)
+
+    def ring_copy(self, way, step, sub):
+        return remote(
+            self.outgoing.at[way, step - 1, self.span(sub), :],
+            self.incoming.at[way, step - 1, self.span(sub), :],
+            self.ring_send.at[way, step - 1, sub],
+            self.ring_recv.at[way, step - 1, sub],
+            self.ring.near[way],
+        )
+
+    def step(self, step):
+        far = self.ring.far
+        for sub, way in self.ring.orders():
+            if not self.travels(way, step, sub):
+                continue
+            steps = far + 1 - step
+            steps = steps if way == 0 or steps == far else -steps
+            value = self.mine(steps, sub)
+            if step > 1 and self.travels(way, step - 1, sub):
+                self.ring_copy(way, step - 1, sub).wait_recv()
+                value = value + self.incoming[way, step - 2, self.span(sub), :].astype(jnp.float32)
+            self.outgoing[way, step - 1, self.span(sub), :] = value.astype(NARROW)
+            copy = self.ring_copy(way, step, sub)
+            copy.start()
+            self.sends.append(copy)
+
+    def begin(self, produce):
+        self.produce = produce
+        self.slots, self.joined, self.sends = {}, set(), []
+        far = self.ring.far
+        self.make(far)
+        self.make(far - 1, 1 - far)
+
+    def middle(self, step):
+        left = self.ring.far - 1 - step
+        self.step(step)
+        if left > 0:
+            self.make(left, -left)
+        elif left == 0:
+            self.make(0)
+
+    def end(self, finish):
+        far = self.ring.far
+        for sub in range(SUBS):
+            value = self.mine(0, sub)
+            for way in range(2):
+                self.ring_copy(way, far, sub).wait_recv()
+                value = value + self.incoming[way, far - 1, self.span(sub), :].astype(jnp.float32)
+            finish(self.span(sub), value)
+        for copy in self.sends:
+            copy.wait_send()
+        for _, copy in self.slots.values():
+            copy.wait_send()
+
+    def run(self, produce, finish, work, some, beside=()):
+        beside = list(beside)
+        self.begin(produce)
+        for step in range(1, self.ring.far + 1):
+            self.middle(step)
+            if beside:
+                beside.pop(0)()
+            work.do(some)
+        self.end(finish)
+        return beside
+
+
+def products(left, right, transposed, tile=512):
+    width = right.shape[0] if transposed else right.shape[1]
+    number = width // tile
+
+    def produce(indices, parts):
+        block = parts.shape[0] // lax.axis_size(DP)
+
+        def one(at):
+            rows = aligned(chosen(at // number, indices) * block, block)
+            cols = aligned(lax.rem(at, number) * tile, tile)
+            if transposed:
+                part = dot(left[rows, :], right[cols, :], ((1,), (1,)))
+            else:
+                part = dot(left[rows, :], right[:, cols], ((1,), (0,)))
+            parts[rows, cols] = part.astype(NARROW)
+
+        loop(0, number * len(indices), one)
+
+    return produce
+
+
+def add_gradient(work, left, right, out, tile=256):
+    if out.shape[0] >= out.shape[1]:
+
+        def piece(at):
+            cols = aligned(at * tile, tile)
+            out[cols, :] = dot(left[:, cols], right[...], ((0,), (0,))).astype(NARROW)
+
+        work.add(piece, out.shape[0] // tile)
+    else:
+
+        def piece(at):
+            cols = aligned(at * tile, tile)
+            out[:, cols] = dot(left[...], right[:, cols], ((0,), (0,))).astype(NARROW)
+
+        work.add(piece, out.shape[1] // tile)
+
+
+def unit_rows(value):
+    inverse = lax.rsqrt(jnp.mean(value * value, axis=-1, keepdims=True) + epsilon)
+    return value * inverse, inverse
+
+
+def through_norm(grad, value, gain):
+    unit, inverse = unit_rows(value)
+    scaled = grad * gain
+    inner = jnp.mean(scaled * unit, axis=-1, keepdims=True)
+    return inverse * (scaled - unit * inner), jnp.sum(grad * unit, axis=0, keepdims=True)
+
+
+def shape_of(*dims, kind=NARROW):
+    return jax.ShapeDtypeStruct(dims, kind)
+
+
+def call_fused(name, body, cid, us, ins, outs, scratch):
+    def kernel(*refs):
+        refs = list(refs)
+        named = {key: refs.pop(0) for key in [*ins, *outs]}
+        for key, kind in scratch.items():
+            named[key] = [refs.pop(0) for _ in kind] if isinstance(kind, list) else refs.pop(0)
+        body(Names(**named))
+
+    flat = []
+    for kind in scratch.values():
+        flat += kind if isinstance(kind, list) else [kind]
+    result = pl.pallas_call(
+        kernel,
+        out_shape=tuple(shape for shape, _ in outs.values()),
+        in_specs=[spec for _, spec in ins.values()],
+        out_specs=tuple(spec for _, spec in outs.values()),
+        scratch_shapes=flat,
+        compiler_params=pltpu.CompilerParams(
+            collective_id=cid, has_side_effects=True, vmem_limit_bytes=63 * 1024 * 1024
+        ),
+        cost_estimate=pl.CostEstimate(
+            flops=0, bytes_accessed=int(us * 3.69e6), transcendentals=0
+        ),
+        name=name,
+    )(*[value for value, _ in ins.values()])
+    return Names(**dict(zip(outs, result)))
+
+
+def swap_halves(rows, head):
+    width = rows.shape[1]
+    lane = lax.broadcasted_iota(jnp.int32, rows.shape, 1)
+    half = head // 2
+    return jnp.where(
+        lax.rem(lane, head) < half, pltpu.roll(rows, width - half, 1), pltpu.roll(rows, half, 1)
+    )
+
+
+def low_lanes(shape, head):
+    return lax.broadcasted_iota(jnp.int32, shape, 1) < head
+
+
+def two_heads(rows, head):
+    low = low_lanes(rows.shape, head)
+    zero = jnp.zeros_like(rows)
+    return jnp.concatenate([jnp.where(low, rows, zero), jnp.where(low, zero, rows)], axis=0)
+
+
+def one_row(rows, head):
+    half = rows.shape[0] // 2
+    return jnp.where(low_lanes((half, rows.shape[1]), head), rows[:half], rows[half:])
+
+
+def triangle(block, keys):
+    row = lax.rem(lax.broadcasted_iota(jnp.int32, (2 * block, keys), 0), block)
+    column = lax.broadcasted_iota(jnp.int32, (2 * block, keys), 1)
+    return column <= row + (keys - block)
+
+
+def in_order(ref, order, spot, block):
+    value = ref[:block, :]
+    for other in range(1, ref.shape[0] // block):
+        there = order[spot] == other
+        value = jnp.where(there, ref[other * block : (other + 1) * block, :], value)
+    return value
+
+
+def attend_here(slots, qkv, cosine, sine, kept, lse, mixed, key2, value2):
+    groups = slots.shape[0]
+    tokens = qkv.shape[0]
+    block = tokens // groups
+    span = groups // 2
+    wide = qkv.shape[1] // 2
+    head = wide // 2
+    scale = 1.0 / math.sqrt(head)
+    for spot in range(groups):
+        here = slice(spot * block, (spot + 1) * block)
+        turn_rows = slice(spot % span * block, (spot % span + 1) * block)
+        turned_by, turned_sine = cosine[turn_rows, :], sine[turn_rows, :]
+        rows = in_order(qkv, slots, spot, block)
+        query, pair = rows[:, :wide], rows[:, wide:]
+        low = low_lanes(pair.shape, head)
+        query = query * turned_by + swap_halves(query, head) * turned_sine
+        pair = jnp.where(low, pair * turned_by + swap_halves(pair, head) * turned_sine, pair)
+        other = pltpu.roll(pair, head, 1)
+        kept[here, :wide] = query.astype(kept.dtype)
+        kept[here, wide:] = pair.astype(kept.dtype)
+        key2[here, :] = jnp.where(low, pair, other).astype(key2.dtype)
+        value2[here, :] = jnp.where(low, other, pair).astype(value2.dtype)
+    for spot in range(groups):
+        here = slice(spot * block, (spot + 1) * block)
+        first = spot // span * span * block
+        keys = (spot % span + 1) * block
+        query = two_heads(kept[here, :wide], head)
+        score = dot(query, key2[first : first + keys, :], ((1,), (1,))) * scale
+        allowed = triangle(block, keys)
+        total = jnp.sum(jnp.where(allowed, jnp.exp(score), 0.0), axis=1, keepdims=True)
+        log_total = jnp.log(total)
+        probs = jnp.where(allowed, jnp.exp(score - log_total), 0.0).astype(jnp.bfloat16)
+        value = dot(probs, value2[first : first + keys, :], ((1,), (0,)))
+        mixed[here, :] = one_row(value, head).astype(mixed.dtype)
+        lse[spot] = log_total
+
+
+def attend_back_here(slots, grad, kept, lse, cosine, sine, out, key2, value2, key_sum, value_sum):
+    groups = slots.shape[0]
+    tokens = kept.shape[0]
+    block = tokens // groups
+    span = groups // 2
+    wide = kept.shape[1] // 2
+    head = wide // 2
+    scale = 1.0 / math.sqrt(head)
+    for spot in range(groups):
+        here = slice(spot * block, (spot + 1) * block)
+        pair = kept[here, wide:].astype(jnp.float32)
+        low = low_lanes(pair.shape, head)
+        other = pltpu.roll(pair, head, 1)
+        key2[here, :] = jnp.where(low, pair, other).astype(key2.dtype)
+        value2[here, :] = jnp.where(low, other, pair).astype(value2.dtype)
+    for spot in range(groups - 1, -1, -1):
+        here = slice(spot * block, (spot + 1) * block)
+        place = spot % span
+        turn_rows = slice(place * block, (place + 1) * block)
+        first = spot // span * span * block
+        keys = (place + 1) * block
+        query = two_heads(kept[here, :wide], head)
+        given = two_heads(in_order(grad, slots, spot, block), head)
+        key = key2[first : first + keys, :]
+        value = value2[first : first + keys, :]
+        score = dot(query, key, ((1,), (1,))) * scale
+        probs = jnp.where(triangle(block, keys), jnp.exp(score - lse[spot]), 0.0)
+        prob_grad = dot(given, value, ((1,), (1,)))
+        rowdot = jnp.sum(probs * prob_grad, axis=1, keepdims=True)
+        score_grad = (probs * (prob_grad - rowdot) * scale).astype(jnp.bfloat16)
+        value_part = dot(probs.astype(jnp.bfloat16), given, ((0,), (0,)))
+        key_part = dot(score_grad, query, ((0,), (0,)))
+        if place == span - 1:
+            value_sum[first : first + keys, :] = value_part
+            key_sum[first : first + keys, :] = key_part
+        else:
+            value_sum[first : first + keys, :] += value_part
+            key_sum[first : first + keys, :] += key_part
+        query_grad = one_row(dot(score_grad, key, ((1,), (0,))), head)
+        query_grad = query_grad * cosine[turn_rows, :] - swap_halves(query_grad, head) * sine[turn_rows, :]
+        out[here, :wide] = query_grad.astype(out.dtype)
+    for spot in range(groups):
+        here = slice(spot * block, (spot + 1) * block)
+        turn_rows = slice(spot % span * block, (spot % span + 1) * block)
+        key = key_sum[here, :]
+        key = key + pltpu.roll(key, head, 1)
+        key = key * cosine[turn_rows, :] - swap_halves(key, head) * sine[turn_rows, :]
+        value = value_sum[here, :]
+        value = value + pltpu.roll(value, head, 1)
+        out[here, wide:] = jnp.where(low_lanes(key.shape, head), key, value).astype(out.dtype)
+
+
+def put_back(source, target, row):
+    groups = row.shape[0]
+    block = source.shape[0] // groups
+    for spot in range(groups):
+        target[spot * block : (spot + 1) * block, :] = in_order(source, row, spot, block)
+
+
+def attend_scratch(tokens, head, back=False):
+    vmem = pltpu.VMEM
+    wide = 2 * head
+    kinds = dict(
+        key2=vmem((tokens, wide), jnp.bfloat16),
+        value2=vmem((tokens, wide), jnp.bfloat16),
+        by_number=vmem((tokens, 2 * wide if back else wide), jnp.bfloat16),
+    )
+    if back:
+        kinds.update(
+            key_sum=vmem((tokens, wide), jnp.float32), value_sum=vmem((tokens, wide), jnp.float32)
+        )
+    return kinds
+
+
+def rope_tables(tokens, head):
+    angle = jnp.arange(tokens, dtype=jnp.float32)[:, None] * rope_frequencies(head)[None, :]
+    cosine = jnp.cos(angle)
+    sine = jnp.sin(angle)
+    return (
+        jnp.concatenate([cosine] * 4, axis=1),
+        jnp.concatenate([-sine, sine] * 2, axis=1),
+    )
+
+
+def weight_pieces(source, target, count, heads, srcs, dsts, layer):
+    qkv, wo, gate, up, down = srcs
+    out_qkv, out_wo, out_gu, out_down = dsts
+    depth = gate.shape[1]
+    hidden = gate.shape[2] // count
+    q_rows = wo.shape[1] // count
+    kv_rows = (qkv.shape[0] - wo.shape[1]) // 2
+    shared = count * heads // kv_rows
+    cols = aligned(source * depth, depth)
+    k_from = pl.multiple_of(wo.shape[1] + target // shared * heads, heads)
+    v_from = pl.multiple_of(wo.shape[1] + kv_rows + target // shared * heads, heads)
+    mine = aligned(target * hidden, hidden)
+    return (
+        (qkv.at[aligned(target * q_rows, q_rows), :], out_qkv.at[layer, pl.ds(0, q_rows), cols]),
+        (qkv.at[pl.ds(k_from, heads), :], out_qkv.at[layer, pl.ds(q_rows, heads), cols]),
+        (qkv.at[pl.ds(v_from, heads), :], out_qkv.at[layer, pl.ds(q_rows + heads, heads), cols]),
+        (wo.at[0, aligned(target * q_rows, q_rows), :], out_wo.at[layer, :, cols]),
+        (gate.at[0, :, mine], out_gu.at[layer, cols, pl.ds(0, hidden)]),
+        (up.at[0, :, mine], out_gu.at[layer, cols, pl.ds(hidden, hidden)]),
+        (down.at[0, mine, :], out_down.at[layer, :, cols]),
+    )
+
+
+KINDS, ATTENTION_KINDS = 7, 4
+
+
+class Spread:
+    def __init__(self, ring, heads, srcs, dsts, sems):
+        self.ring = ring
+        self.layer = lax.axis_index(SECTION)
+        self.across = {SECTION: 1 - self.layer}
+        self.peers, self.origins = partners(ring.me, ring.count)
+        self.send, self.recv, self.cross_send, self.cross_recv, self.own_sem = sems
+        self.pieces = lambda source, target, layer: weight_pieces(
+            source, target, ring.count, heads, srcs, dsts, layer
+        )
+        self.started, self.local = [], {}
+        count = ring.count
+        sizes = [math.prod(there.shape) for _, there in self.pieces(ring.me, ring.me, self.layer)]
+        arrivals = []
+        for kind in range(KINDS):
+            for k in range(count - 1):
+                part = (k + 1) / (count // 2) if k < count // 2 else 1.0
+                due = sum(sizes[:kind]) + part * sizes[kind]
+                arrivals.append((due if k < count // 2 else due * 0.5, kind, k))
+        self.arrivals = sorted(arrivals)
+
+    def go(self, copy):
+        copy.start()
+        self.started.append(copy)
+
+    def own(self, kinds):
+        last = self.ring.count - 1
+        for kind in kinds:
+            source, target = self.pieces(self.ring.me, self.ring.me, self.layer)[kind]
+            self.go(
+                remote(
+                    source, target, self.cross_send.at[kind, last], self.cross_recv.at[kind, last],
+                    self.across,
+                )
+            )
+            self.local[kind] = pltpu.make_async_copy(source, target, self.own_sem.at[kind])
+            self.local[kind].start()
+
+    def out(self, kinds):
+        for kind in kinds:
+            for k, peer in enumerate(self.peers):
+                source, target = self.pieces(self.ring.me, peer, self.layer)[kind]
+                self.go(remote(source, target, self.send.at[kind, k], self.recv.at[kind, k], {DP: peer}))
+
+    def pass_on(self, kinds):
+        for _, kind, k in self.arrivals:
+            if kind not in kinds:
+                continue
+            here = self.pieces(self.origins[k], self.ring.me, self.layer)[kind][1]
+            remote(
+                here, here, self.send.at[kind, k], self.recv.at[kind, k], {DP: self.origins[k]}
+            ).wait_recv()
+            self.go(
+                remote(
+                    here, here, self.cross_send.at[kind, k], self.cross_recv.at[kind, k], self.across
+                )
+            )
+
+    def here(self, kinds):
+        for kind in kinds:
+            self.local[kind].wait()
+            for k in range(self.ring.count):
+                origin = self.origins[k] if k < self.ring.count - 1 else self.ring.me
+                there = self.pieces(origin, self.ring.me, 1 - self.layer)[kind][1]
+                remote(
+                    there, there, self.cross_send.at[kind, k], self.cross_recv.at[kind, k], self.across
+                ).wait_recv()
+
+    def sent(self):
+        for copy in self.started:
+            copy.wait_send()
+
+
+def chip_rows(index, local):
+    return aligned(index * 2 * local, 2 * local)
+
+
+def feed_forward_use(s, local, after):
+    width = s.hidden.shape[1]
+    tile = 256
+    number = width // tile
+
+    def use(indices):
+        def one(at):
+            rows = chip_rows(chosen(at // number, indices), local)
+            start = lax.rem(at, number) * tile
+            cols, right = aligned(start, tile), aligned(start + width, tile)
+            value = s.normed2[rows, :]
+            gate = dot(value, s.gu[:, cols], ((1,), (0,)))
+            upper = dot(value, s.gu[:, right], ((1,), (0,)))
+            s.hidden[rows, cols] = (gate * jax.nn.sigmoid(gate) * upper).astype(NARROW)
+            after(rows, cols, right, gate, upper)
+
+        loop(0, number * len(indices), one)
+
+    return use
+
+
+def feed_forward_back(s, rows, cols, right, gate, upper):
+    hidden_grad = dot(s.out_grad[rows, :], s.down[cols, :], ((1,), (1,)))
+    sigma = jax.nn.sigmoid(gate)
+    gate_grad = hidden_grad * upper * sigma * (1.0 + gate * (1.0 - sigma))
+    s.gu_grad[rows, cols] = gate_grad.astype(NARROW)
+    s.gu_grad[rows, right] = (hidden_grad * gate * sigma).astype(NARROW)
+
+
+def opening_body(s):
+    ring = Ring()
+    layer = lax.axis_index(SECTION)
+    peers, origins = partners(ring.me, ring.count)
+    holders = [{DP: peer} for peer in peers] + [
+        {SECTION: 1 - layer, DP: peer} for peer in [*peers, ring.me]
+    ]
+    greet([*holders, ring.side])
+    copies = Copies(s.copy_sem)
+    rows_in = copies(s.inputs.at[layer], s.rows)
+    given_in = copies(s.cotangent.at[layer], s.given)
+    spread = Spread(
+        ring, s.kept0.shape[1] // 4, (s.qkv, s.wo, s.gate, s.up, s.down_in),
+        (s.out_qkv, s.out_wo, s.out_gu, s.out_down), s.spread_sems,
+    )
+    attention, feed = range(ATTENTION_KINDS), range(ATTENTION_KINDS, KINDS)
+    local, depth = s.rows.shape[0], s.gain_attn.shape[1]
+
+    s.gain_piece[...] = jnp.zeros_like(s.gain_piece)
+    s.gain_piece[0:1, :] = s.gain_attn[...].astype(WIDE)
+    s.gain_piece[1:2, :] = s.gain_mlp[...].astype(WIDE)
+    gain_send, gain_recv = s.gain_sems
+    spot = lambda at, source: s.gains.at[at, :, aligned(source * depth, depth)]
+    for k, holder in enumerate(holders):
+        spread.go(remote(s.gain_piece, spot(layer, ring.me), gain_send.at[k], gain_recv.at[k], holder))
+    own_gains = copies(s.gain_piece, spot(layer, ring.me))
+    spread.own(attention)
+    own_gains.wait()
+    for k, holder in enumerate(holders):
+        at, place = (layer, k) if k < ring.count - 1 else (1 - layer, k - ring.count + 1)
+        here = spot(at, origins[place] if place < ring.count - 1 else ring.me)
+        remote(here, here, gain_send.at[k], gain_recv.at[k], holder).wait_recv()
+
+    rows_in.wait()
+    unit, _ = unit_rows(s.rows[...])
+    s.shard0[...] = (unit * s.gains[0, 0:1, :]).astype(NARROW)
+    first = Gather(ring, s.shard0, s.normed1, s.first_sems)
+    first.start()
+    spread.out(attention)
+    for hop in range(1, ring.far + 1):
+        first.hop(hop)
+    given_in.wait()
+    s.shard1[...] = s.given[...].astype(NARROW)
+    grads = Gather(ring, s.shard1, s.out_grad, s.grads_sems)
+    grads.start()
+    spread.pass_on(attention)
+    spread.out(feed)
+    spread.own(feed)
+    first.finish()
+    spread.here(attention)
+    loads = [
+        copies(s.out_qkv.at[0], s.qkv_w), copies(s.out_qkv.at[1], s.next_qkv_w),
+        copies(s.out_wo.at[0], s.wo_w),
+    ]
+    stores = [copies(s.normed1, s.normed1_out)]
+    for load in loads:
+        load.wait()
+    tile = 2 * local
+
+    def project(at):
+        rows = aligned(at * tile, tile)
+        s.projected[rows, :] = dot(s.normed1[rows, :], s.qkv_w[...], ((1,), (1,)))
+
+    loop(0, s.projected.shape[0] // tile, project)
+    attend_here(s.slots, s.projected, s.cosine, s.sine, s.kept0, s.lse0, s.by_number, s.key2, s.value2)
+    put_back(s.by_number, s.mixed0, s.row)
+    stores[0].wait()
+    grads.hop(1)
+    spread.pass_on(feed)
+
+    reduce = Reduce(ring, s.reduce)
+    none = Work()
+
+    def second(span, value):
+        s.second[span, :] = s.rows[span, :] + value
+
+    loads = {}
+
+    def gate_up_here():
+        spread.here(feed[:2])
+        loads[0] = copies(s.out_gu.at[0], s.gu)
+
+    left = reduce.run(
+        products(s.mixed0, s.wo_w, False), second, none, 0,
+        [functools.partial(grads.hop, hop) for hop in range(2, ring.far + 1)] + [gate_up_here],
+    )
+    for do in left:
+        do()
+    unit, _ = unit_rows(s.second[...])
+    s.shard2[...] = (unit * s.gains[0, 1:2, :]).astype(NARROW)
+    loads[0].wait()
+    spread.here(feed[2:])
+    load = copies(s.out_down.at[0], s.down)
+
+    def keep(rows, cols, right, gate, upper):
+        s.gate_up[rows, cols] = gate
+        s.gate_up[rows, right] = upper
+
+    Gather(ring, s.shard2, s.normed2, s.gather_sems).run(feed_forward_use(s, local, keep), none, 0)
+    grads.finish()
+    stores += [
+        copies(s.out_grad, s.out_grad_out), copies(s.normed2, s.normed2_out),
+        copies(s.gate_up, s.gate_up_out),
+    ]
+    load.wait()
+
+    def result(span, value):
+        s.result[span, :] = s.second[span, :] + value
+
+    reduce.run(products(s.hidden, s.down, False), result, none, 0)
+    unit, _ = unit_rows(s.result[...])
+    s.shard0[...] = (unit * s.gains[1, 0:1, :]).astype(NARROW)
+
+    def use(indices):
+        def one(at):
+            rows = chip_rows(chosen(at, indices), local)
+            s.projected[rows, :] = dot(s.normed1[rows, :], s.next_qkv_w[...], ((1,), (1,)))
+
+        loop(0, len(indices), one)
+
+    Gather(ring, s.shard0, s.normed1, s.first_sems).run(use, none, 0)
+    stores.append(copies(s.normed1, s.next_normed1_out))
+    attend_here(s.slots, s.projected, s.cosine, s.sine, s.kept1, s.lse1, s.by_number, s.key2, s.value2)
+    put_back(s.by_number, s.mixed1, s.row)
+    for store in stores[1:]:
+        store.wait()
+    spread.sent()
+
+
+def opening(slots, row, cosine, sine, inputs, cotangent, qkv, wo, gate, up, down, gain_attn, gain_mlp, count, head):
+    local, width = inputs.shape[1:]
+    tokens = count * 2 * local
+    depth = gate.shape[1]
+    hidden = gate.shape[2] // count
+    q_rows = wo.shape[1] // count
+    vmem, dma = pltpu.VMEM, pltpu.SemaphoreType.DMA
+    lse = shape_of(count, 2 * tokens // count, 1, kind=WIDE)
+    return call_fused(
+        "opening", opening_body, 0, 360,
+        dict(
+            slots=(slots, SMEM), row=(row, SMEM), cosine=(cosine, VMEM), sine=(sine, VMEM),
+            inputs=(inputs, HBM), cotangent=(cotangent, HBM), qkv=(qkv, HBM), wo=(wo, HBM),
+            gate=(gate, HBM), up=(up, HBM), down_in=(down, HBM),
+            gain_attn=(gain_attn, VMEM), gain_mlp=(gain_mlp, VMEM),
+        ),
+        dict(
+            out_qkv=(shape_of(2, q_rows + 2 * head, width), HBM),
+            out_wo=(shape_of(2, q_rows, width), HBM),
+            out_gu=(shape_of(2, width, 2 * hidden), HBM),
+            out_down=(shape_of(2, hidden, width), HBM),
+            gains=(shape_of(2, 8, width, kind=WIDE), VMEM),
+            normed1_out=(shape_of(tokens, width), HBM),
+            next_normed1_out=(shape_of(tokens, width), HBM),
+            normed2_out=(shape_of(tokens, width), HBM),
+            out_grad_out=(shape_of(tokens, width), HBM),
+            gate_up_out=(shape_of(tokens, 2 * hidden, kind=WIDE), HBM),
+            second=(shape_of(local, width, kind=WIDE), VMEM),
+            result=(shape_of(local, width, kind=WIDE), VMEM),
+            hidden=(shape_of(tokens, hidden), VMEM),
+            mixed0=(shape_of(tokens, 2 * head), VMEM), mixed1=(shape_of(tokens, 2 * head), VMEM),
+            kept0=(shape_of(tokens, 4 * head), VMEM), kept1=(shape_of(tokens, 4 * head), VMEM),
+            lse0=(lse, VMEM), lse1=(lse, VMEM),
+        ),
+        dict(
+            rows=vmem((local, width), WIDE), given=vmem((local, width), WIDE),
+            gain_piece=vmem((8, depth), WIDE),
+            shard0=vmem((local, width), NARROW), shard1=vmem((local, width), NARROW),
+            shard2=vmem((local, width), NARROW),
+            normed1=vmem((tokens, width), NARROW), normed2=vmem((tokens, width), NARROW),
+            out_grad=vmem((tokens, width), NARROW), gate_up=vmem((tokens, 2 * hidden), WIDE),
+            qkv_w=vmem((q_rows + 2 * head, width), NARROW),
+            next_qkv_w=vmem((q_rows + 2 * head, width), NARROW),
+            wo_w=vmem((q_rows, width), NARROW), gu=vmem((width, 2 * hidden), NARROW),
+            down=vmem((hidden, width), NARROW), projected=vmem((tokens, 4 * head), WIDE),
+            key2=vmem((tokens, 2 * head), NARROW), value2=vmem((tokens, 2 * head), NARROW),
+            by_number=vmem((tokens, 2 * head), NARROW),
+            reduce=reduce_scratch(count, local, width),
+            first_sems=gather_scratch(count), grads_sems=gather_scratch(count),
+            gather_sems=gather_scratch(count),
+            gain_sems=[dma((2 * count - 1,)), dma((2 * count - 1,))],
+            spread_sems=[
+                dma((KINDS, count - 1)), dma((KINDS, count - 1)),
+                dma((KINDS, count)), dma((KINDS, count)), dma((KINDS,)),
+            ],
+            copy_sem=dma((16,)),
+        ),
+    )
+
+
+def back_through_feed_forward(at, s, ring, reduce, work, beside):
+    local = s.given.shape[0]
+    add_gradient(work, s.hidden, s.out_grad, s.grad_down)
+    add_gradient(work, s.normed2, s.gu_grad, s.grad_gu)
+
+    def keep(span, value):
+        s.normed_grad[span, :] = value
+
+    left = reduce.run(products(s.gu_grad, s.gu, True), keep, work, 3, beside)
+    part, s.gain_mlp_grad[...] = through_norm(
+        s.normed_grad[...], s.second[...], s.gains[at, 1:2, :]
+    )
+    s.second_grad[...] = s.given[...] + part
+    s.shard2[...] = s.second_grad[...].astype(NARROW)
+
+    def use(indices):
+        def one(at):
+            rows = chip_rows(chosen(at, indices), local)
+            s.mixed_grad[rows, :] = dot(s.attn_grad[rows, :], s.wo[...], ((1,), (1,))).astype(NARROW)
+
+        loop(0, len(indices), one)
+
+    for do in reversed(left):
+        work.first(lambda _, do=do: do())
+    Gather(ring, s.shard2, s.attn_grad, s.gather_sems).run(use, work, 3)
+    work.do()
+
+
+def turn_body(at, s):
+    ring = Ring()
+    greet(ring.everyone())
+    copies = Copies(s.copy_sem)
+    wo_in = copies(s.wo_in.at[at], s.wo)
+    ins = [
+        copies(s.gu_in.at[at], s.gu), copies(s.down_in.at[at], s.down),
+        copies(s.out_grad_in, s.out_grad), copies(s.cotangent.at[lax.axis_index(SECTION)], s.given),
+    ]
+    reduce, other = Reduce(ring, s.reduce), Reduce(ring, s.other)
+    work = Work()
+
+    def second(span, value):
+        s.second[span, :] = s.rows[span, :] + value
+
+    wo_in.wait()
+    reduce.run(products(s.mixed, s.wo, False), second, work, 0)
+    unit, _ = unit_rows(s.second[...])
+    s.shard[...] = (unit * s.gains[at, 1:2, :]).astype(NARROW)
+    for load in ins:
+        load.wait()
+    Gather(ring, s.shard, s.normed2, s.first_sems).run(
+        feed_forward_use(s, s.rows.shape[0], functools.partial(feed_forward_back, s)), work, 0
+    )
+
+    def result(span, value):
+        s.result[span, :] = s.second[span, :] + value
+
+    beside = [lambda: other.begin(products(s.hidden, s.down, False))]
+    beside += [functools.partial(other.middle, step) for step in range(1, ring.far + 1)]
+    beside += [lambda: other.end(result)]
+    back_through_feed_forward(at, s, ring, reduce, work, beside)
+    stores = [
+        copies(s.grad_down, s.grad_down_out), copies(s.grad_gu, s.grad_gu_out),
+        copies(s.attn_grad, s.attn_grad_out),
+    ]
+    attend_back_here(
+        s.slots, s.mixed_grad, s.kept, s.lse, s.cosine, s.sine, s.by_number, s.key2, s.value2,
+        s.key_sum, s.value_sum,
+    )
+    put_back(s.by_number, s.qkv_grad, s.row)
+    for store in stores:
+        store.wait()
+
+
+def turn(at, known, rows, mixed, kept, lse, out_grad, cotangent, weights, count):
+    _, wo, gu, down, gains = weights
+    local, width = rows.shape
+    tokens = mixed.shape[0]
+    hidden = down.shape[1]
+    head = mixed.shape[1] // 2
+    vmem, dma = pltpu.VMEM, pltpu.SemaphoreType.DMA
+    return call_fused(
+        "turn", functools.partial(turn_body, at), 1, 140,
+        dict(
+            **known, rows=(rows, VMEM), mixed=(mixed, VMEM), kept=(kept, VMEM), lse=(lse, VMEM),
+            gains=(gains, VMEM), out_grad_in=(out_grad, HBM), cotangent=(cotangent, HBM),
+            wo_in=(wo, HBM), gu_in=(gu, HBM), down_in=(down, HBM),
+        ),
+        dict(
+            result=(shape_of(local, width, kind=WIDE), VMEM),
+            second_grad=(shape_of(local, width, kind=WIDE), VMEM),
+            qkv_grad=(shape_of(tokens, 4 * head), VMEM),
+            attn_grad_out=(shape_of(tokens, width), HBM),
+            gain_mlp_grad=(shape_of(1, width, kind=WIDE), VMEM),
+            grad_down_out=(shape_of(hidden, width), HBM),
+            grad_gu_out=(shape_of(width, 2 * hidden), HBM),
+        ),
+        dict(
+            reduce=reduce_scratch(count, local, width), other=reduce_scratch(count, local, width),
+            first_sems=gather_scratch(count), gather_sems=gather_scratch(count),
+            gu=vmem(gu.shape[1:], NARROW), down=vmem(down.shape[1:], NARROW), wo=vmem(wo.shape[1:], NARROW),
+            out_grad=vmem((tokens, width), NARROW), normed2=vmem((tokens, width), NARROW),
+            attn_grad=vmem((tokens, width), NARROW), mixed_grad=vmem((tokens, 2 * head), NARROW),
+            hidden=vmem((tokens, hidden), NARROW), gu_grad=vmem((tokens, 2 * hidden), NARROW),
+            grad_down=vmem((hidden, width), NARROW), grad_gu=vmem((width, 2 * hidden), NARROW),
+            given=vmem((local, width), WIDE), second=vmem((local, width), WIDE),
+            normed_grad=vmem((local, width), WIDE),
+            shard=vmem((local, width), NARROW), shard2=vmem((local, width), NARROW),
+            **attend_scratch(tokens, head, True),
+            copy_sem=dma((8,)),
+        ),
+    )
+
+
+def attention_back(at, s, reduce, work, beside=()):
+    def keep(span, value):
+        s.normed_grad[span, :] = value
+
+    reduce.run(products(s.qkv_grad, s.qkv_w, False), keep, work, 3, beside)
+    part, s.gain_attn_grad[...] = through_norm(s.normed_grad[...], s.rows[...], s.gains[at, 0:1, :])
+    s.input_grad[...] = s.second_grad_in[...] + part
+
+
+def backward_body(upper, lower, s):
+    ring = Ring()
+    local = s.rows.shape[0]
+    greet(ring.everyone())
+    copies = Copies(s.copy_sem)
+    qkv_in = copies(s.qkv_w_in.at[upper], s.qkv_w)
+    upper_in = [copies(s.attn_grad_in, s.attn_grad), copies(s.normed1_in, s.normed2)]
+    first_in = [copies(s.down_in.at[lower], s.down), copies(s.gate_up_in, s.gate_up)]
+    then_in = [copies(s.gu_in.at[lower], s.gu), copies(s.wo_in.at[lower], s.wo)]
+    reduce = Reduce(ring, s.reduce)
+    work = Work()
+
+    def wait(_):
+        for load in upper_in:
+            load.wait()
+
+    work.add(wait)
+    add_gradient(work, s.mixed, s.attn_grad, s.grad_wo)
+    add_gradient(work, s.normed2, s.qkv_grad, s.grad_qkv)
+    qkv_in.wait()
+    attention_back(upper, s, reduce, work)
+    work.do()
+    then_in.append(copies(s.normed2_in, s.normed2))
+    stores = [copies(s.grad_wo, s.grad_wo_out), copies(s.grad_qkv, s.grad_qkv_out)]
+    s.shard[...] = s.input_grad[...].astype(NARROW)
+    s.given[...] = s.input_grad[...]
+    for load in first_in:
+        load.wait()
+    width = s.hidden.shape[1]
+    tile = 256
+    number = width // tile
+
+    def use(indices):
+        def one(at):
+            rows = chip_rows(chosen(at // number, indices), local)
+            start = lax.rem(at, number) * tile
+            cols, right = aligned(start, tile), aligned(start + width, tile)
+            feed_forward_back(s, rows, cols, right, s.gate_up[rows, cols], s.gate_up[rows, right])
+
+        loop(0, number * len(indices), one)
+
+    Gather(ring, s.shard, s.out_grad, s.first_sems).run(use, work, 0)
+    for load in then_in:
+        load.wait()
+    back_through_feed_forward(lower, s, ring, reduce, work, [])
+    stores += [
+        copies(s.grad_down, s.grad_down_out), copies(s.grad_gu, s.grad_gu_out),
+        copies(s.attn_grad, s.attn_grad_out),
+    ]
+    for store in stores:
+        store.wait()
+
+
+def backward_between(at, upper, lower, weights, count):
+    qkv_w, wo, gu, down, gains = weights
+    local, width = upper.rows.shape
+    tokens = upper.mixed.shape[0]
+    hidden = down.shape[1]
+    q_rows = wo.shape[1]
+    vmem, dma = pltpu.VMEM, pltpu.SemaphoreType.DMA
+    return call_fused(
+        "backward_between", functools.partial(backward_body, at, at - 1), 2, 115,
+        dict(
+            rows=(upper.rows, VMEM), second_grad_in=(upper.second_grad, VMEM),
+            qkv_grad=(upper.qkv_grad, VMEM), mixed=(upper.mixed, VMEM), gains=(gains, VMEM),
+            attn_grad_in=(upper.attn_grad, HBM), normed1_in=(upper.normed1, HBM),
+            second=(lower.second, VMEM), hidden=(lower.hidden, VMEM),
+            gate_up_in=(lower.gate_up, HBM), normed2_in=(lower.normed2, HBM),
+            qkv_w_in=(qkv_w, HBM), wo_in=(wo, HBM), gu_in=(gu, HBM), down_in=(down, HBM),
+        ),
+        dict(
+            input_grad=(shape_of(local, width, kind=WIDE), VMEM),
+            second_grad=(shape_of(local, width, kind=WIDE), VMEM),
+            mixed_grad=(shape_of(tokens, q_rows), VMEM),
+            attn_grad_out=(shape_of(tokens, width), HBM),
+            gain_attn_grad=(shape_of(1, width, kind=WIDE), VMEM),
+            gain_mlp_grad=(shape_of(1, width, kind=WIDE), VMEM),
+            grad_wo_out=(shape_of(q_rows, width), HBM),
+            grad_qkv_out=(shape_of(width, qkv_w.shape[1]), HBM),
+            grad_down_out=(shape_of(hidden, width), HBM),
+            grad_gu_out=(shape_of(width, 2 * hidden), HBM),
+        ),
+        dict(
+            reduce=reduce_scratch(count, local, width),
+            first_sems=gather_scratch(count), gather_sems=gather_scratch(count),
+            gu=vmem(gu.shape[1:], NARROW), down=vmem(down.shape[1:], NARROW), wo=vmem(wo.shape[1:], NARROW),
+            qkv_w=vmem(qkv_w.shape[1:], NARROW), gate_up=vmem((tokens, 2 * hidden), WIDE),
+            out_grad=vmem((tokens, width), NARROW), normed2=vmem((tokens, width), NARROW),
+            attn_grad=vmem((tokens, width), NARROW), gu_grad=vmem((tokens, 2 * hidden), NARROW),
+            grad_wo=vmem((q_rows, width), NARROW), grad_qkv=vmem((width, qkv_w.shape[1]), NARROW),
+            grad_down=vmem((hidden, width), NARROW), grad_gu=vmem((width, 2 * hidden), NARROW),
+            given=vmem((local, width), WIDE), normed_grad=vmem((local, width), WIDE),
+            shard=vmem((local, width), NARROW), shard2=vmem((local, width), NARROW),
+            copy_sem=dma((16,)),
+        ),
+    )
+
+
+def gradient_pieces(target, count, refs):
+    down, gu, wo, qkv = refs
+    depth = down.shape[1] // count
+    hidden = down.shape[0]
+    cols = aligned(target * depth, depth)
+    return (
+        down.at[:, cols],
+        gu.at[cols, pl.ds(0, hidden)],
+        gu.at[cols, pl.ds(hidden, hidden)],
+        wo.at[:, cols],
+        qkv.at[cols, :],
+    )
+
+
+def owned_pieces(source, refs, sizes):
+    down, gate, up, wo, qkv = refs
+    return (
+        down.at[aligned(source * sizes[0][0], sizes[0][0]), :],
+        gate.at[:, aligned(source * sizes[1][1], sizes[1][1])],
+        up.at[:, aligned(source * sizes[2][1], sizes[2][1])],
+        wo.at[aligned(source * sizes[3][0], sizes[3][0]), :],
+        qkv.at[source],
+    )
+
+
+GRADS, FEED_GRADS = 5, 3
+
+
+class Return:
+    def __init__(self, ring, partial, outs, landed, mine, sems):
+        self.ring = ring
+        self.layer = lax.axis_index(SECTION)
+        self.across = {SECTION: 1 - self.layer}
+        peers, self.origins = partners(ring.me, ring.count)
+        self.order = [*peers, ring.me]
+        self.partial, self.outs, self.landed, self.mine = partial, outs, landed, mine
+        self.cross_send, self.cross_recv, self.load_sem, self.send, self.recv, self.own_sem = sems
+        self.sizes = [ref.shape[1:] for ref in mine]
+        self.crossing, self.loads, self.sends, self.events = {}, {}, [], []
+
+    def cross(self, kinds):
+        count = self.ring.count
+        for kind in kinds:
+            for k, owner in enumerate(self.order):
+                pieces = [gradient_pieces(owner, count, refs)[kind] for refs in self.partial]
+                for at in range(2):
+                    copy = remote(
+                        pieces[1 - at], self.landed[kind].at[k],
+                        self.cross_send.at[kind, k], self.cross_recv.at[kind, k], self.across,
+                    )
+                    load = pltpu.make_async_copy(
+                        pieces[at], self.mine[kind].at[k], self.load_sem.at[kind, k]
+                    )
+
+                    @pl.when(self.layer == at)
+                    def _():
+                        copy.start()
+                        load.start()
+
+                self.crossing[kind, k], self.loads[kind, k] = copy, load
+                self.events.append((kind, k))
+
+    def some(self, number):
+        for kind, k in self.events[:number]:
+            self.loads[kind, k].wait()
+            self.crossing[kind, k].wait_recv()
+            mine = self.mine[kind]
+            total = mine[k].astype(WIDE) + self.landed[kind][k].astype(WIDE)
+            mine[k] = total.astype(NARROW)
+            target = owned_pieces(self.ring.me, self.outs, self.sizes)[kind]
+            if k < self.ring.count - 1:
+                copy = remote(
+                    mine.at[k], target, self.send.at[kind, k], self.recv.at[kind, k],
+                    {DP: self.order[k]},
+                )
+            else:
+                copy = pltpu.make_async_copy(mine.at[k], target, self.own_sem.at[kind])
+            copy.start()
+            self.sends.append((k, copy))
+        self.events = self.events[number:]
+
+    def finish(self):
+        for copy in self.crossing.values():
+            copy.wait_send()
+        for k, copy in self.sends:
+            if k < self.ring.count - 1:
+                copy.wait_send()
+            else:
+                copy.wait()
+        for kind in range(GRADS):
+            for k in range(self.ring.count - 1):
+                here = owned_pieces(self.origins[k], self.outs, self.sizes)[kind]
+                remote(
+                    self.mine[kind].at[k], here, self.send.at[kind, k], self.recv.at[kind, k],
+                    {DP: self.origins[k]},
+                ).wait_recv()
+
+
+def closing_body(at, s):
+    ring = Ring()
+    layer = lax.axis_index(SECTION)
+    count = ring.count
+    everyone = 4 * count
+    this = (layer * count + ring.me) * 2 + ring.core
+
+    def device(k):
+        other = lax.rem(this + k, everyone)
+        return {SECTION: other // (2 * count), DP: lax.rem(other // 2, count), TENSOR: lax.rem(other, 2)}
+
+    greet([device(k) for k in range(1, everyone)])
+    copies = Copies(s.copy_sem)
+    qkv_in = copies(s.qkv_w_in.at[at], s.qkv_w)
+    ins = [copies(s.attn_grad_in, s.attn_grad), copies(s.normed1_in, s.normed1)]
+    rows_in = copies(s.inputs.at[layer], s.rows)
+    back = Return(
+        ring,
+        ((s.down0, s.gu0, s.grad_wo, s.grad_qkv), (s.down1, s.gu1, s.wo1, s.qkv1)),
+        (s.down_out, s.gate_out, s.up_out, s.wo_out, s.qkv_out), s.landed, s.mine, s.back_sems,
+    )
+    back.cross(range(FEED_GRADS))
+
+    swap_send, swap_recv = s.swap_sems
+    swaps = []
+
+    def swap(which, out, values):
+        for section in range(2):
+            copy = remote(
+                values[1 - section], out.at[section], swap_send.at[which], swap_recv.at[which],
+                {SECTION: 1 - layer},
+            )
+            own = pltpu.make_async_copy(values[section], out.at[section], s.own_sems.at[which])
+
+            @pl.when(layer == section)
+            def _():
+                copy.start()
+                own.start()
+
+        swaps.append((copy, own))
+
+    swap(0, s.results, (s.result0, s.result1))
+    attend_back_here(
+        s.slots, s.mixed_grad, s.kept, s.lse, s.cosine, s.sine, s.by_number, s.key2, s.value2,
+        s.key_sum, s.value_sum,
+    )
+    put_back(s.by_number, s.qkv_grad, s.row)
+    work = Work()
+    for load in ins:
+        load.wait()
+    add_gradient(work, s.mixed, s.attn_grad, s.grad_wo)
+    add_gradient(work, s.normed1, s.qkv_grad, s.grad_qkv)
+    qkv_in.wait()
+    rows_in.wait()
+
+    def rest():
+        work.do()
+        back.cross(range(FEED_GRADS, GRADS))
+        back.some(1)
+
+    beside = [functools.partial(back.some, 1)] * 2 + [rest] + [functools.partial(back.some, 1)] * (ring.far - 3)
+    attention_back(at, s, Reduce(ring, s.reduce), work, beside)
+    swap(1, s.input_grads, (s.input_grad, s.input_grad1))
+
+    lanes = s.gain_out.shape[1]
+    for section, (attn, mlp) in enumerate(((s.gain_attn_grad, s.gain_mlp0), (s.gain_attn1, s.gain_mlp1))):
+        for owner in range(2 * count):
+            s.gain_in[section * 2 * count + owner] = jnp.zeros_like(s.gain_out)
+            cols = slice(owner * lanes, (owner + 1) * lanes)
+            s.gain_in[section * 2 * count + owner, 0:1, :] = attn[:, cols]
+            s.gain_in[section * 2 * count + owner, 1:2, :] = mlp[:, cols]
+    gain_send, gain_recv = s.gain_sems
+    gain_copies = []
+    for k in range(1, everyone):
+        copy = remote(
+            s.gain_in.at[lax.rem(this + k, everyone)], s.gain_landed.at[k - 1],
+            gain_send.at[k - 1], gain_recv.at[k - 1], device(k),
+        )
+        copy.start()
+        gain_copies.append(copy)
+    back.some(len(back.events))
+    total = s.gain_in[this]
+    for k, copy in enumerate(gain_copies):
+        copy.wait_recv()
+        total = total + s.gain_landed[k]
+    s.gain_out[...] = total
+    for copy in gain_copies:
+        copy.wait_send()
+    for copy, own in swaps:
+        copy.wait()
+        own.wait()
+    back.finish()
+
+
+def closing(at, known, inputs, first, last, feed0, grads1, gains_of, weights, count):
+    qkv_w, _, _, _, gains = weights
+    local, width = inputs.shape[1:]
+    tokens = first.mixed.shape[0]
+    head = first.mixed.shape[1] // 2
+    down0, gu0 = feed0
+    down1, gu1, wo1, qkv1 = grads1
+    hidden, q_rows, qkv_rows = down0.shape[0], wo1.shape[0], qkv1.shape[1]
+    depth = width // count
+    sizes = [(hidden, depth), (depth, hidden), (depth, hidden), (q_rows, depth), (depth, qkv_rows)]
+    everyone = 4 * count
+    lanes = width // (2 * count)
+    vmem, dma = pltpu.VMEM, pltpu.SemaphoreType.DMA
+    pieces = lambda: [vmem((count, *size), NARROW) for size in sizes]
+    return call_fused(
+        "closing", functools.partial(closing_body, at), 3, 210,
+        dict(
+            **known, inputs=(inputs, HBM), gains=(gains, VMEM), qkv_w_in=(qkv_w, HBM),
+            second_grad_in=(first.second_grad, VMEM), mixed_grad=(first.mixed_grad, VMEM),
+            mixed=(first.mixed, VMEM), kept=(first.kept, VMEM), lse=(first.lse, VMEM),
+            attn_grad_in=(first.attn_grad, HBM), normed1_in=(first.normed1, HBM),
+            result0=(first.result, VMEM), result1=(last.result, VMEM),
+            input_grad1=(last.input_grad, VMEM),
+            down0=(down0, HBM), gu0=(gu0, HBM),
+            down1=(down1, HBM), gu1=(gu1, HBM), wo1=(wo1, HBM), qkv1=(qkv1, HBM),
+            gain_mlp0=(gains_of[0], VMEM), gain_attn1=(gains_of[1], VMEM), gain_mlp1=(gains_of[2], VMEM),
+        ),
+        dict(
+            results=(shape_of(2, local, width, kind=WIDE), HBM),
+            input_grads=(shape_of(2, local, width, kind=WIDE), HBM),
+            down_out=(shape_of(count * hidden, depth), HBM),
+            gate_out=(shape_of(depth, count * hidden), HBM),
+            up_out=(shape_of(depth, count * hidden), HBM),
+            wo_out=(shape_of(count * q_rows, depth), HBM),
+            qkv_out=(shape_of(count, depth, qkv_rows), HBM),
+            gain_out=(shape_of(8, lanes, kind=WIDE), VMEM),
+        ),
+        dict(
+            reduce=reduce_scratch(count, local, width),
+            qkv_w=vmem(qkv_w.shape[1:], NARROW), rows=vmem((local, width), WIDE),
+            attn_grad=vmem((tokens, width), NARROW), normed1=vmem((tokens, width), NARROW),
+            qkv_grad=vmem((tokens, 4 * head), NARROW),
+            grad_wo=vmem((q_rows, width), NARROW), grad_qkv=vmem((width, qkv_rows), NARROW),
+            normed_grad=vmem((local, width), WIDE), input_grad=vmem((local, width), WIDE),
+            gain_attn_grad=vmem((1, width), WIDE),
+            landed=pieces(), mine=pieces(),
+            gain_in=vmem((everyone, 8, lanes), WIDE), gain_landed=vmem((everyone - 1, 8, lanes), WIDE),
+            **attend_scratch(tokens, head, True),
+            back_sems=[
+                dma((GRADS, count)), dma((GRADS, count)), dma((GRADS, count)),
+                dma((GRADS, count - 1)), dma((GRADS, count - 1)), dma((GRADS,)),
+            ],
+            gain_sems=[dma((everyone - 1,)), dma((everyone - 1,))],
+            swap_sems=[dma((2,)), dma((2,))], own_sems=dma((2,)),
+            copy_sem=dma((8,)),
+        ),
+    )
+
+
+def fast_shards(inputs, table, cotangent, wq, wk, wv, wo, w_gate, w_up, w_down, gain_attn, gain_mlp):
+    count = lax.axis_size(DP)
+    parts = lax.axis_size(TENSOR)
+    head = HEAD_SIZE
+    section = lax.axis_index(SECTION)
+    block = inputs.shape[1] * parts
+    depth = wq.shape[1]
+    q_cols = wq.shape[2] // count
+
+    row = lax.dynamic_index_in_dim(table, section, 0, keepdims=False)
+    ids = jnp.arange(count, dtype=jnp.int32)
+    slots = jnp.sum(jnp.where(row[None, :] == ids[:, None], ids[None, :], 0), axis=1)
+    cosine, sine = rope_tables(count // 2 * block, head)
+    qkv_t = jnp.concatenate([wq[0], wk[0], wv[0]], axis=1).T
+    s = opening(
+        slots, row, cosine, sine, inputs, cotangent, qkv_t, wo, w_gate, w_up, w_down,
+        gain_attn, gain_mlp, count, head,
+    )
+    weights = (s.out_qkv, s.out_wo, s.out_gu, s.out_down, s.gains)
+    known = dict(
+        slots=(slots, SMEM), row=(row, SMEM), cosine=(cosine, VMEM), sine=(sine, VMEM)
+    )
+    top = turn(
+        1, known, s.result, s.mixed1, s.kept1, s.lse1, s.out_grad_out, cotangent, weights, count
+    )
+    upper = Names(
+        rows=s.result, second_grad=top.second_grad, qkv_grad=top.qkv_grad, mixed=s.mixed1,
+        attn_grad=top.attn_grad_out, normed1=s.next_normed1_out,
+    )
+    lower = Names(
+        second=s.second, hidden=s.hidden, gate_up=s.gate_up_out, normed2=s.normed2_out
+    )
+    back = backward_between(1, upper, lower, weights, count)
+    first = Names(
+        second_grad=back.second_grad, mixed_grad=back.mixed_grad, mixed=s.mixed0, kept=s.kept0,
+        lse=s.lse0, attn_grad=back.attn_grad_out, normed1=s.normed1_out, result=s.result,
+    )
+    last = Names(result=top.result, input_grad=back.input_grad)
+    end = closing(
+        0, known, inputs, first, last,
+        (back.grad_down_out, back.grad_gu_out),
+        (top.grad_down_out, top.grad_gu_out, back.grad_wo_out, back.grad_qkv_out),
+        (back.gain_mlp_grad, back.gain_attn_grad, top.gain_mlp_grad),
+        weights, count,
+    )
+    grad_wq = end.qkv_out[:, :, :q_cols].astype(WIDE).transpose(1, 0, 2).reshape(depth, -1)
+    shared = count * head // wk.shape[2]
+    joined = end.qkv_out[:, :, q_cols:].astype(WIDE).reshape(count // shared, shared, depth, 2, head)
+    joined = jnp.sum(joined, axis=1)
+    grad_wk = joined[:, :, 0].transpose(1, 0, 2).reshape(depth, -1)
+    grad_wv = joined[:, :, 1].transpose(1, 0, 2).reshape(depth, -1)
+    wide = lambda value: value.astype(WIDE)[None]
+    return (
+        end.results[None],
+        end.input_grads[None],
+        grad_wq[None],
+        grad_wk[None],
+        grad_wv[None],
+        wide(end.wo_out),
+        wide(end.gate_out),
+        wide(end.up_out),
+        wide(end.down_out),
+        end.gain_out[:1],
+        end.gain_out[1:2],
+    )
+
+
+def fits(mesh, inputs, table, cotangent, wq, wk, wv, wo, w_gate, w_up, w_down, gain_attn, gain_mlp):
+    sections, count, parts = (mesh.shape[axis] for axis in (SECTION, DP, TENSOR))
+    head = HEAD_SIZE
+    if sections != 2 or parts != 2 or inputs.shape[0] != sections or count % 4 or count < 8:
+        return False
+    devices = count * parts
+    queries, keys = wq.shape[2] // head, wk.shape[2] // head
+    if queries != 2 * devices or devices % keys or keys % parts or 4 * head != 256:
+        return False
+    return (
+        wq.shape[1] % (128 * count) == 0
+        and wq.shape[1] % 512 == 0
+        and w_gate.shape[2] % (256 * devices) == 0
+        and inputs.shape[1] % (64 * devices) == 0
+    )
+
+
+def shards(mesh, whole, *args):
+    if fits(mesh, *whole):
+        return fast_shards(*args)
+    return general_shards(*args)
+
+
 def solution(mesh):
     in_specs = (
-        P(None, ("dp", "tensor"), None),
+        P(None, (DP, TENSOR), None),
         P(),
-        P(None, ("dp", "tensor"), None),
-        P("section", "dp", "tensor"),
-        P("section", "dp", "tensor"),
-        P("section", "dp", "tensor"),
-        P("section", "tensor", "dp"),
-        P("section", "dp", "tensor"),
-        P("section", "dp", "tensor"),
-        P("section", "tensor", "dp"),
-        P("section", "dp"),
-        P("section", "dp"),
+        P(None, (DP, TENSOR), None),
+        P(SECTION, DP, TENSOR),
+        P(SECTION, DP, TENSOR),
+        P(SECTION, DP, TENSOR),
+        P(SECTION, TENSOR, DP),
+        P(SECTION, DP, TENSOR),
+        P(SECTION, DP, TENSOR),
+        P(SECTION, TENSOR, DP),
+        P(SECTION, DP),
+        P(SECTION, DP),
     )
     out_specs = (
-        P("section", None, ("dp", "tensor"), None),
-        P("section", None, ("dp", "tensor"), None),
-        P("section", "dp", "tensor"),
-        P("section", "dp", "tensor"),
-        P("section", "dp", "tensor"),
-        P("section", "tensor", "dp"),
-        P("section", "dp", "tensor"),
-        P("section", "dp", "tensor"),
-        P("section", "tensor", "dp"),
-        P("section", ("dp", "tensor")),
-        P("section", ("dp", "tensor")),
-    )
-    return jax.shard_map(shards, mesh=mesh, in_specs=in_specs, out_specs=out_specs, check_vma=False)
+        P(SECTION, None, (DP, TENSOR), None),
+        P(SECTION, None, (DP, TENSOR), None),
+        P(SECTION, DP, TENSOR),
+        P(SECTION, DP, TENSOR),
+        P(SECTION, DP, TENSOR),
+        P(SECTION, TENSOR, DP),
+        P(SECTION, DP, TENSOR),
+        P(SECTION, DP, TENSOR),
+        P(SECTION, TENSOR, DP),
+        P(SECTION, (DP, TENSOR)),
+        P(SECTION, (DP, TENSOR)),
+    )
+
+    def step(*args):
+        return jax.shard_map(
+            functools.partial(shards, mesh, args),
+            mesh=mesh,
+            in_specs=in_specs,
+            out_specs=out_specs,
+            check_vma=False,
+        )(*args)
+
+    return step

time: 3320 us -> 843 us (0.25)
  waiting for transfers between devices: 2230 us -> 0 us
  Pallas kernels: 0 us -> 805 us
  matrix products: 567 us -> 0 us
  blocking collectives: 266 us -> 0 us
  local copies, waits for them, and re-layouts: 110 us -> 10.7 us
  other arithmetic: 94.2 us -> 16.2 us
    reduce_scatter x25 -> x0, waiting for transfers between devices: 1370 us -> none  [the longest x1 281 us: reduce_grads(): lax.psum_scatter(pieces[4].astype(jnp.bfloat16), 'dp', scatter_dimension=...]
    all_gather x13 -> x0, waiting for transfers between devices: 815 us -> none  [the longest x1 218 us: shards(): lax.all_gather(w_up[0], 'dp', axis=0, tiled=True)]
    pallas_call x0 -> x4, Pallas kernels: none -> 805 us  [call_fused(): pl.pallas_call(kernel, out_shape=tuple((shape for shape, _ in outs.values...]
    dot_general x147 -> x0, matrix products: 567 us -> none  [the longest x63 442 us: matmul(): return jnp.dot(left, right, preferred_element_type=jnp.float32)]
    all_gather x14 -> x0, blocking collectives: 240 us -> none  [the longest x3 97.5 us: layer_forward(): lax.all_gather(value_rows, 'dp', axis=0, tiled=True)]
    ppermute x4 -> x0, waiting for transfers between devices: 41.2 us -> none  [passed_along(): lax.ppermute(value, axis, [(source, source + steps) for source in range(i...]
  transfers between devices with their start and end apart: 42 -> 0, of which waited for: 35 -> 0; matrix products, arithmetic and copies ran while one was open for 10% -> 0% of each run, Pallas kernels for 0% -> 0%
where the time goes in v3:
time: 843 us; the launch traced here: 833 us
  Pallas kernels  805 us (95%)
  other arithmetic  16.2 us (2%)
  local copies, waits for them, and re-layouts  10.7 us (1%)
    pallas_call x4, Pallas kernels, call_fused(): pl.pallas_call(kernel, out_shape=tuple((shape for shape, _ in outs.values...  805 us

profile of v3, /device:TPU:0, one launch (start us, length us, event | category | flops | bytes accessed | tf_op | source)
XLA Modules:
  0.0 832.8 jit_solution(5223508885964074655)
XLA Ops:
  0.6 0.0 copy-start
  0.7 0.7 copy-done
  1.3 0.0 copy-start.7
  1.3 0.6 select_reduce_fusion.refs_0_
  2.0 1.0 copy.43
  3.0 1.0 copy.44
  4.0 1.2 copy.42
  5.3 0.9 maximum_bitcast_fusion.refs_6_
  6.2 1.0 fusion.2
  7.2 1.3 pad_maximum_fusion
  8.4 0.0 copy-done.7
  8.5 328.4 %opening.1 = (bf16[2,256,2048]{2,1,0:T(8,128)(2,1)}, bf16[2,128,2048]{2,1,0:T(8,128)(2,1)}, bf16[2,2048,1024]{2,1,0:T(8,128)(2,1)}, bf16[2,512,2048]{2,1,0:T(8,1...) custom-call(s32[8]{0:T(128)} %select_reduce_fusion.refs_0_, ...), custom_call_target="tpu_custom_call" | custom-call | bytes 1328400000 | tf_op jit(solution)/shard_map/opening/pallas_call | solution.py:864
  336.8 145.5 %turn.1 = (f32[64,2048]{1,0:T(8,128)}, f32[64,2048]{1,0:T(8,128)}, bf16[1024,256]{1,0:T(8,128)(2,1)}, bf16[1024,2048]{1,0:T(8,128)(2,1)}, f32[1,2048]{1,0:T(1,12...) custom-call(s32[8]{0:T(128)} %select_reduce_fusion.refs_0_, s32[8]{0:T(128)} %copy-done.7, ...), custom_call_target="tpu_custom_call" | custom-call | bytes 516600000 | tf_op jit(solution)/shard_map/turn/pallas_call | solution.py:864
  482.4 117.9 %backward_between.1 = (f32[64,2048]{1,0:T(8,128)}, f32[64,2048]{1,0:T(8,128)}, bf16[1024,128]{1,0:T(8,128)(2,1)}, bf16[1024,2048]{1,0:T(8,128)(2,1)}, f32[1,2048...) custom-call(f32[64,2048]{1,0:T(8,128)} %get-tuple-element.57.refs_4_, ...), custom_call_target="tpu_custom_call" | custom-call | bytes 424350016 | tf_op jit(solution)/shard_map/backward_between/pallas_call | solution.py:864
  600.3 213.1 %closing.1 = (f32[2,64,2048]{2,1,0:T(8,128)}, f32[2,64,2048]{2,1,0:T(8,128)}, bf16[4096,256]{1,0:T(8,128)(2,1)}, bf16[256,4096]{1,0:T(8,128)(2,1)}, bf16[256,409...) custom-call(s32[8]{0:T(128)} %select_reduce_fusion.refs_0_, ...), custom_call_target="tpu_custom_call" | custom-call | bytes 774899968 | tf_op jit(solution)/shard_map/closing/pallas_call | solution.py:864
  813.4 1.3 fusion.4
  814.7 1.2 convert_reduce_fusion
  815.9 0.0 copy-start.6
  815.9 1.2 convert_bitcast_fusion
  817.1 0.3 copy.45
  817.4 1.3 copy.47
  818.7 0.2 copy.50
  819.0 0.8 copy.49
  819.8 0.0 copy-start.3
  819.8 0.8 copy.48
  820.6 0.0 copy-done.6
  820.6 1.0 bitcast_convert_fusion.3
  821.7 4.1 bitcast_convert_fusion.2
  825.8 0.0 copy-done.3
  825.8 0.0 copy-start.2
  825.8 0.0 copy-start.1
  825.8 2.5 bitcast_convert_fusion.1
  828.3 0.0 copy-done.2
  828.3 0.0 copy-start.5
  828.3 0.0 copy-start.4
  828.3 2.3 bitcast_convert_fusion
  830.7 0.0 copy-done.5
  830.7 1.0 copy.53
  831.6 0.0 copy-done.4
  831.6 1.0 copy.54
  832.6 0.0 copy-done.1
  (3 shorter events, 0.1 us)
Async XLA Ops:
  0.6 0.7 copy-start
  1.3 7.1 copy-start.7
  815.9 4.8 copy-start.6
  819.8 6.0 copy-start.3
  825.8 2.5 copy-start.2
  825.8 6.8 copy-start.1
  828.3 2.3 copy-start.5
  828.3 3.3 copy-start.4

commit v4 on v3

--- a/solution.py
+++ b/solution.py
@@ -429,7 +429,7 @@
 
 
 MESH = pl.DeviceIdType.MESH
-SUBS = 2
+SUBS = 4
 HBM = pl.BlockSpec(memory_space=pl.ANY)
 VMEM = pl.BlockSpec(memory_space=pltpu.VMEM)
 SMEM = pl.BlockSpec(memory_space=pltpu.SMEM)
@@ -621,7 +621,7 @@
         )
         self.own.start()
 
-    def hop(self, hop):
+    def hop(self, hop, between=None):
         far, count = self.ring.far, self.ring.count
         for sub, way in self.ring.orders():
             if not self.travels(way, hop, sub):
@@ -635,6 +635,8 @@
             if hop < far and self.travels(way, hop + 1, sub):
                 self.pass_on(way, hop + 1, sub)
             self.hand_over(steps, sub, hop if way == 0 or hop == far else count - hop)
+            if way == 1 and between is not None:
+                between()
 
     def side_arrived(self, steps):
         slot = -steps if steps <= 0 else self.ring.count - steps
@@ -661,22 +663,25 @@
                 self.side_arrived(steps)
         self.sent()
 
-    def run(self, use, work, some):
+    def run(self, use, work):
         self.start()
         self.own.wait()
-        self.side_arrived(0)
-        use([self.ring.index(0)])
+        waiting = [0]
+
+        def between():
+            if waiting:
+                steps = waiting.pop(0)
+                self.side_arrived(steps)
+                use(self.ring.index(steps))
+            else:
+                work.do(1)
+
         for hop in range(1, self.ring.far + 1):
-            work.do(some)
-            self.hop(hop)
-            for steps in self.around(hop):
-                self.side_arrived(steps)
-            use([self.ring.index(steps) for steps in self.around(hop)])
+            self.hop(hop, between)
+            waiting += self.around(hop)
+        while waiting:
+            between()
         self.sent()
-
-
-def chosen(at, indices):
-    return indices[0] if len(indices) == 1 else indices[0] + (indices[1] - indices[0]) * at
 
 
 def reduce_scratch(count, rows, width):
@@ -708,18 +713,20 @@
             return aligned(start, self.rows)
         return aligned(start + sub * self.piece, self.piece)
 
-    def make(self, *several):
-        self.produce([self.ring.index(steps) for steps in several], self.parts)
-        for steps in several:
-            slot = len(self.slots)
-            copy = remote(
-                self.parts.at[self.spot(steps, 1 - self.ring.core), :], self.beside.at[slot],
-                self.side_send.at[slot], self.side_recv.at[slot], self.ring.side,
-            )
-            copy.start()
-            self.slots[steps] = (slot, copy)
+    def make(self):
+        steps = self.to_make.pop(0)
+        self.produce(self.ring.index(steps), self.parts)
+        slot = len(self.slots)
+        copy = remote(
+            self.parts.at[self.spot(steps, 1 - self.ring.core), :], self.beside.at[slot],
+            self.side_send.at[slot], self.side_recv.at[slot], self.ring.side,
+        )
+        copy.start()
+        self.slots[steps] = (slot, copy)
 
     def mine(self, steps, sub):
+        while steps not in self.slots:
+            self.make()
         slot, copy = self.slots[steps]
         if steps not in self.joined:
             copy.wait_recv()
@@ -755,24 +762,27 @@
             copy = self.ring_copy(way, step, sub)
             copy.start()
             self.sends.append(copy)
-
-    def begin(self, produce):
-        self.produce = produce
+            if way == 1:
+                if self.to_make:
+                    self.make()
+                else:
+                    self.work.do(1)
+
+    def begin(self, produce, work):
+        self.produce, self.work = produce, work
         self.slots, self.joined, self.sends = {}, set(), []
         far = self.ring.far
-        self.make(far)
-        self.make(far - 1, 1 - far)
-
-    def middle(self, step):
-        left = self.ring.far - 1 - step
-        self.step(step)
-        if left > 0:
-            self.make(left, -left)
-        elif left == 0:
-            self.make(0)
+        self.to_make = [far]
+        for steps in range(far - 1, 0, -1):
+            self.to_make += [steps, -steps]
+        self.to_make.append(0)
+        self.make()
+        self.make()
 
     def end(self, finish):
         far = self.ring.far
+        while self.to_make:
+            self.make()
         for sub in range(SUBS):
             value = self.mine(0, sub)
             for way in range(2):
@@ -784,14 +794,13 @@
         for _, copy in self.slots.values():
             copy.wait_send()
 
-    def run(self, produce, finish, work, some, beside=()):
+    def run(self, produce, finish, work, beside=()):
         beside = list(beside)
-        self.begin(produce)
+        self.begin(produce, work)
         for step in range(1, self.ring.far + 1):
-            self.middle(step)
+            self.step(step)
             if beside:
                 beside.pop(0)()
-            work.do(some)
         self.end(finish)
         return beside
 
@@ -800,19 +809,19 @@
     width = right.shape[0] if transposed else right.shape[1]
     number = width // tile
 
-    def produce(indices, parts):
+    def produce(index, parts):
         block = parts.shape[0] // lax.axis_size(DP)
+        rows = aligned(index * block, block)
 
         def one(at):
-            rows = aligned(chosen(at // number, indices) * block, block)
-            cols = aligned(lax.rem(at, number) * tile, tile)
+            cols = aligned(at * tile, tile)
             if transposed:
                 part = dot(left[rows, :], right[cols, :], ((1,), (1,)))
             else:
                 part = dot(left[rows, :], right[:, cols], ((1,), (0,)))
             parts[rows, cols] = part.astype(NARROW)
 
-        loop(0, number * len(indices), one)
+        loop(0, number, one)
 
     return produce
 
@@ -1145,10 +1154,11 @@
     tile = 256
     number = width // tile
 
-    def use(indices):
+    def use(index):
+        rows = chip_rows(index, local)
+
         def one(at):
-            rows = chip_rows(chosen(at // number, indices), local)
-            start = lax.rem(at, number) * tile
+            start = at * tile
             cols, right = aligned(start, tile), aligned(start + width, tile)
             value = s.normed2[rows, :]
             gate = dot(value, s.gu[:, cols], ((1,), (0,)))
@@ -1156,7 +1166,7 @@
             s.hidden[rows, cols] = (gate * jax.nn.sigmoid(gate) * upper).astype(NARROW)
             after(rows, cols, right, gate, upper)
 
-        loop(0, number * len(indices), one)
+        loop(0, number, one)
 
     return use
 
@@ -1252,7 +1262,7 @@
         loads[0] = copies(s.out_gu.at[0], s.gu)
 
     left = reduce.run(
-        products(s.mixed0, s.wo_w, False), second, none, 0,
+        products(s.mixed0, s.wo_w, False), second, none,
         [functools.partial(grads.hop, hop) for hop in range(2, ring.far + 1)] + [gate_up_here],
     )
     for do in left:
@@ -1267,7 +1277,7 @@
         s.gate_up[rows, cols] = gate
         s.gate_up[rows, right] = upper
 
-    Gather(ring, s.shard2, s.normed2, s.gather_sems).run(feed_forward_use(s, local, keep), none, 0)
+    Gather(ring, s.shard2, s.normed2, s.gather_sems).run(feed_forward_use(s, local, keep), none)
     grads.finish()
     stores += [
         copies(s.out_grad, s.out_grad_out), copies(s.normed2, s.normed2_out),
@@ -1278,18 +1288,15 @@
     def result(span, value):
         s.result[span, :] = s.second[span, :] + value
 
-    reduce.run(products(s.hidden, s.down, False), result, none, 0)
+    reduce.run(products(s.hidden, s.down, False), result, none)
     unit, _ = unit_rows(s.result[...])
     s.shard0[...] = (unit * s.gains[1, 0:1, :]).astype(NARROW)
 
-    def use(indices):
-        def one(at):
-            rows = chip_rows(chosen(at, indices), local)
-            s.projected[rows, :] = dot(s.normed1[rows, :], s.next_qkv_w[...], ((1,), (1,)))
-
-        loop(0, len(indices), one)
-
-    Gather(ring, s.shard0, s.normed1, s.first_sems).run(use, none, 0)
+    def use(index):
+        rows = chip_rows(index, local)
+        s.projected[rows, :] = dot(s.normed1[rows, :], s.next_qkv_w[...], ((1,), (1,)))
+
+    Gather(ring, s.shard0, s.normed1, s.first_sems).run(use, none)
     stores.append(copies(s.normed1, s.next_normed1_out))
     attend_here(s.slots, s.projected, s.cosine, s.sine, s.kept1, s.lse1, s.by_number, s.key2, s.value2)
     put_back(s.by_number, s.mixed1, s.row)
@@ -1366,23 +1373,20 @@
     def keep(span, value):
         s.normed_grad[span, :] = value
 
-    left = reduce.run(products(s.gu_grad, s.gu, True), keep, work, 3, beside)
+    left = reduce.run(products(s.gu_grad, s.gu, True), keep, work, beside)
     part, s.gain_mlp_grad[...] = through_norm(
         s.normed_grad[...], s.second[...], s.gains[at, 1:2, :]
     )
     s.second_grad[...] = s.given[...] + part
     s.shard2[...] = s.second_grad[...].astype(NARROW)
 
-    def use(indices):
-        def one(at):
-            rows = chip_rows(chosen(at, indices), local)
-            s.mixed_grad[rows, :] = dot(s.attn_grad[rows, :], s.wo[...], ((1,), (1,))).astype(NARROW)
-
-        loop(0, len(indices), one)
+    def use(index):
+        rows = chip_rows(index, local)
+        s.mixed_grad[rows, :] = dot(s.attn_grad[rows, :], s.wo[...], ((1,), (1,))).astype(NARROW)
 
     for do in reversed(left):
         work.first(lambda _, do=do: do())
-    Gather(ring, s.shard2, s.attn_grad, s.gather_sems).run(use, work, 3)
+    Gather(ring, s.shard2, s.attn_grad, s.gather_sems).run(use, work)
     work.do()
 
 
@@ -1402,20 +1406,20 @@
         s.second[span, :] = s.rows[span, :] + value
 
     wo_in.wait()
-    reduce.run(products(s.mixed, s.wo, False), second, work, 0)
+    reduce.run(products(s.mixed, s.wo, False), second, work)
     unit, _ = unit_rows(s.second[...])
     s.shard[...] = (unit * s.gains[at, 1:2, :]).astype(NARROW)
     for load in ins:
         load.wait()
     Gather(ring, s.shard, s.normed2, s.first_sems).run(
-        feed_forward_use(s, s.rows.shape[0], functools.partial(feed_forward_back, s)), work, 0
+        feed_forward_use(s, s.rows.shape[0], functools.partial(feed_forward_back, s)), work
     )
 
     def result(span, value):
         s.result[span, :] = s.second[span, :] + value
 
-    beside = [lambda: other.begin(products(s.hidden, s.down, False))]
-    beside += [functools.partial(other.middle, step) for step in range(1, ring.far + 1)]
+    beside = [lambda: other.begin(products(s.hidden, s.down, False), Work())]
+    beside += [functools.partial(other.step, step) for step in range(1, ring.far + 1)]
     beside += [lambda: other.end(result)]
     back_through_feed_forward(at, s, ring, reduce, work, beside)
     stores = [
@@ -1475,7 +1479,7 @@
     def keep(span, value):
         s.normed_grad[span, :] = value
 
-    reduce.run(products(s.qkv_grad, s.qkv_w, False), keep, work, 3, beside)
+    reduce.run(products(s.qkv_grad, s.qkv_w, False), keep, work, beside)
     part, s.gain_attn_grad[...] = through_norm(s.normed_grad[...], s.rows[...], s.gains[at, 0:1, :])
     s.input_grad[...] = s.second_grad_in[...] + part
 
@@ -1512,16 +1516,17 @@
     tile = 256
     number = width // tile
 
-    def use(indices):
+    def use(index):
+        rows = chip_rows(index, local)
+
         def one(at):
-            rows = chip_rows(chosen(at // number, indices), local)
-            start = lax.rem(at, number) * tile
+            start = at * tile
             cols, right = aligned(start, tile), aligned(start + width, tile)
             feed_forward_back(s, rows, cols, right, s.gate_up[rows, cols], s.gate_up[rows, right])
 
-        loop(0, number * len(indices), one)
-
-    Gather(ring, s.shard, s.out_grad, s.first_sems).run(use, work, 0)
+        loop(0, number, one)
+
+    Gather(ring, s.shard, s.out_grad, s.first_sems).run(use, work)
     for load in then_in:
         load.wait()
     back_through_feed_forward(lower, s, ring, reduce, work, [])
@@ -1644,9 +1649,15 @@
         for kind, k in self.events[:number]:
             self.loads[kind, k].wait()
             self.crossing[kind, k].wait_recv()
-            mine = self.mine[kind]
-            total = mine[k].astype(WIDE) + self.landed[kind][k].astype(WIDE)
-            mine[k] = total.astype(NARROW)
+            mine, theirs = self.mine[kind], self.landed[kind]
+            tile = 64
+
+            def add(at):
+                rows = aligned(at * tile, tile)
+                total = mine[k, rows, :].astype(WIDE) + theirs[k, rows, :].astype(WIDE)
+                mine[k, rows, :] = total.astype(NARROW)
+
+            loop(0, mine.shape[1] // tile, add)
             target = owned_pieces(self.ring.me, self.outs, self.sizes)[kind]
             if k < self.ring.count - 1:
                 copy = remote(
@@ -1829,14 +1840,76 @@
     )
 
 
+def widen_kernel(heads, down, gate, up, wo, qkv, every, gain, *outs):
+    down_out, gate_out, up_out, wo_out, wq_out, wk_out, wv_out, attn_out, mlp_out = outs
+    for source, out in ((down, down_out), (gate, gate_out), (up, up_out), (wo, wo_out)):
+        out[0] = source[...].astype(WIDE)
+    queries = wq_out.shape[2]
+    wq_out[0] = qkv[0, :, :queries].astype(WIDE)
+
+    @pl.when(pl.program_id(0) == 0)
+    def _():
+        attn_out[...] = gain[0:1, :]
+        mlp_out[...] = gain[1:2, :]
+        width = 2 * heads
+        shared = every.shape[0] * heads // wk_out.shape[2]
+
+        def one(head):
+            chips = range(head * shared, (head + 1) * shared)
+            return sum(every[chip, :, queries:].astype(WIDE) for chip in chips)
+
+        for pair in range(wk_out.shape[2] // width):
+            left, right = one(2 * pair), one(2 * pair + 1)
+            low = low_lanes(left.shape, heads)
+            cols = slice(pair * width, (pair + 1) * width)
+            wk_out[0, :, cols] = jnp.where(low, left, pltpu.roll(right, heads, 1))
+            wv_out[0, :, cols] = jnp.where(low, pltpu.roll(left, heads, 1), right)
+
+
+def widen(end, kv_cols, count, head):
+    depth = end.gate_out.shape[0]
+    hidden = end.gate_out.shape[1] // count
+    q_rows = end.wo_out.shape[0] // count
+    lanes = end.gain_out.shape[1]
+    down = (hidden, depth)
+    across = (depth, hidden)
+    result = lambda *dims: shape_of(1, *dims, kind=WIDE)
+    by_rows = lambda at: (at, 0)
+    by_cols = lambda at: (0, at)
+    none = lambda at: (0, 0)
+    flat = lambda index: lambda at: (0, *index(at))
+    return pl.pallas_call(
+        functools.partial(widen_kernel, head),
+        grid=(count,),
+        out_shape=(
+            result(count * hidden, depth), result(depth, count * hidden), result(depth, count * hidden),
+            result(count * q_rows, depth), result(depth, count * q_rows),
+            result(depth, kv_cols), result(depth, kv_cols), result(lanes), result(lanes),
+        ),
+        in_specs=[
+            pl.BlockSpec(down, by_rows), pl.BlockSpec(across, by_cols), pl.BlockSpec(across, by_cols),
+            pl.BlockSpec((q_rows, depth), by_rows),
+            pl.BlockSpec((1, *end.qkv_out.shape[1:]), lambda at: (at, 0, 0)),
+            pl.BlockSpec(end.qkv_out.shape, lambda at: (0, 0, 0)),
+            pl.BlockSpec(end.gain_out.shape, none),
+        ],
+        out_specs=(
+            pl.BlockSpec((1, *down), flat(by_rows)), pl.BlockSpec((1, *across), flat(by_cols)),
+            pl.BlockSpec((1, *across), flat(by_cols)), pl.BlockSpec((1, q_rows, depth), flat(by_rows)),
+            pl.BlockSpec((1, depth, q_rows), flat(by_cols)),
+            pl.BlockSpec((1, depth, kv_cols), flat(none)), pl.BlockSpec((1, depth, kv_cols), flat(none)),
+            pl.BlockSpec((1, lanes), none), pl.BlockSpec((1, lanes), none),
+        ),
+        name="widen",
+    )(end.down_out, end.gate_out, end.up_out, end.wo_out, end.qkv_out, end.qkv_out, end.gain_out)
+
+
 def fast_shards(inputs, table, cotangent, wq, wk, wv, wo, w_gate, w_up, w_down, gain_attn, gain_mlp):
     count = lax.axis_size(DP)
     parts = lax.axis_size(TENSOR)
     head = HEAD_SIZE
     section = lax.axis_index(SECTION)
     block = inputs.shape[1] * parts
-    depth = wq.shape[1]
-    q_cols = wq.shape[2] // count
 
     row = lax.dynamic_index_in_dim(table, section, 0, keepdims=False)
     ids = jnp.arange(count, dtype=jnp.int32)
@@ -1874,25 +1947,21 @@
         (back.gain_mlp_grad, back.gain_attn_grad, top.gain_mlp_grad),
         weights, count,
     )
-    grad_wq = end.qkv_out[:, :, :q_cols].astype(WIDE).transpose(1, 0, 2).reshape(depth, -1)
-    shared = count * head // wk.shape[2]
-    joined = end.qkv_out[:, :, q_cols:].astype(WIDE).reshape(count // shared, shared, depth, 2, head)
-    joined = jnp.sum(joined, axis=1)
-    grad_wk = joined[:, :, 0].transpose(1, 0, 2).reshape(depth, -1)
-    grad_wv = joined[:, :, 1].transpose(1, 0, 2).reshape(depth, -1)
-    wide = lambda value: value.astype(WIDE)[None]
+    grad_down, grad_gate, grad_up, grad_wo, grad_wq, grad_wk, grad_wv, sum_attn, sum_mlp = widen(
+        end, wk.shape[2], count, head
+    )
     return (
         end.results[None],
         end.input_grads[None],
-        grad_wq[None],
-        grad_wk[None],
-        grad_wv[None],
-        wide(end.wo_out),
-        wide(end.gate_out),
-        wide(end.up_out),
-        wide(end.down_out),
-        end.gain_out[:1],
-        end.gain_out[1:2],
+        grad_wq,
+        grad_wk,
+        grad_wv,
+        grad_wo,
+        grad_gate,
+        grad_up,
+        grad_down,
+        sum_attn,
+        sum_mlp,
     )
 
 

time: 843 us -> 834 us (0.989)
  other arithmetic: 16.2 us -> 3.84 us
    pallas_call x0 -> x1, Pallas kernels: none -> 10.8 us  [widen(): pl.pallas_call(functools.partial(widen_kernel, head), grid=(count,), out_...]
    broadcast_in_dim x4 -> x0, other arithmetic: 9.99 us -> none  [fast_shards(): wide = lambda value: value.astype(WIDE)[None]]
where the time goes in v4:
time: 834 us; the launch traced here: 821 us
  Pallas kernels  810 us (97%)
    pallas_call x4, Pallas kernels, call_fused(): pl.pallas_call(kernel, out_shape=tuple((shape for shape, _ in outs.values...  800 us

profile of v4, /device:TPU:0, one launch (start us, length us, event | category | flops | bytes accessed | tf_op | source)
XLA Modules:
  0.0 821.0 jit_solution(2107675236293407777)
XLA Ops:
  0.6 0.0 copy-start
  0.7 0.7 copy-done
  1.3 0.0 copy-start.4
  1.3 0.6 select_reduce_fusion.refs_0_
  2.0 1.0 copy.27
  3.0 1.0 copy.28
  4.0 1.2 copy.26
  5.3 0.9 maximum_bitcast_fusion.refs_6_
  6.2 1.0 fusion.2
  7.2 1.3 pad_maximum_fusion
  8.4 0.0 copy-done.4
  8.5 327.3 %opening.1 = (bf16[2,256,2048]{2,1,0:T(8,128)(2,1)}, bf16[2,128,2048]{2,1,0:T(8,128)(2,1)}, bf16[2,2048,1024]{2,1,0:T(8,128)(2,1)}, bf16[2,512,2048]{2,1,0:T(8,1...) custom-call(s32[8]{0:T(128)} %select_reduce_fusion.refs_0_, ...), custom_call_target="tpu_custom_call" | custom-call | bytes 1328400000 | tf_op jit(solution)/shard_map/opening/pallas_call | solution.py:873
  335.8 142.5 %turn.1 = (f32[64,2048]{1,0:T(8,128)}, f32[64,2048]{1,0:T(8,128)}, bf16[1024,256]{1,0:T(8,128)(2,1)}, bf16[1024,2048]{1,0:T(8,128)(2,1)}, f32[1,2048]{1,0:T(1,12...) custom-call(s32[8]{0:T(128)} %select_reduce_fusion.refs_0_, s32[8]{0:T(128)} %copy-done.4, ...), custom_call_target="tpu_custom_call" | custom-call | bytes 516600000 | tf_op jit(solution)/shard_map/turn/pallas_call | solution.py:873
  478.2 116.8 %backward_between.1 = (f32[64,2048]{1,0:T(8,128)}, f32[64,2048]{1,0:T(8,128)}, bf16[1024,128]{1,0:T(8,128)(2,1)}, bf16[1024,2048]{1,0:T(8,128)(2,1)}, f32[1,2048...) custom-call(f32[64,2048]{1,0:T(8,128)} %get-tuple-element.66.refs_4_, ...), custom_call_target="tpu_custom_call" | custom-call | bytes 424350016 | tf_op jit(solution)/shard_map/backward_between/pallas_call | solution.py:873
  595.0 213.0 %closing.1 = (f32[2,64,2048]{2,1,0:T(8,128)}, f32[2,64,2048]{2,1,0:T(8,128)}, bf16[4096,256]{1,0:T(8,128)(2,1)}, bf16[256,4096]{1,0:T(8,128)(2,1)}, bf16[256,409...) custom-call(s32[8]{0:T(128)} %select_reduce_fusion.refs_0_, ...), custom_call_target="tpu_custom_call" | custom-call | bytes 774899968 | tf_op jit(solution)/shard_map/closing/pallas_call | solution.py:873
  808.0 0.0 copy-start.3
  808.1 0.0 copy-start.2
  808.1 0.0 copy-start.1
  808.1 10.8 %widen.1 = (f32[1,4096,256]{2,1,0:T(8,128)}, f32[1,256,4096]{2,1,0:T(8,128)}, f32[1,256,4096]{2,1,0:T(8,128)}, f32[1,1024,256]{2,1,0:T(8,128)}, f32[1,256,1024]{...) custom-call(bf16[4096,256]{1,0:T(8,128)(2,1)} %get-tuple-element.102.down, ...), custom_call_target="tpu_custom_call" | custom-call | tf_op jit(solution)/shard_map/widen/pallas_call | solution.py:1881
  818.8 0.0 copy-done.3
  818.9 1.0 copy.31
  819.8 0.0 copy-done.2
  819.8 1.0 copy.32
  820.8 0.0 copy-done.1
  (2 shorter events, 0.0 us)
Async XLA Ops:
  0.6 0.7 copy-start
  1.3 7.1 copy-start.4
  808.0 10.8 %copy-start.3 = (f32[2,64,2048]{2,1,0:T(8,128)S(1)}, f32[2,64,2048]{2,1,0:T(8,128)}, u32[]{:S(2)}) copy-start(f32[2,64,2048]{2,1,0:T(8,128)} %get-tuple-element.100) | copy-start | bytes 3145732
  808.1 11.8 %copy-start.2 = (f32[2,64,2048]{2,1,0:T(8,128)S(1)}, f32[2,64,2048]{2,1,0:T(8,128)}, u32[]{:S(2)}) copy-start(f32[2,64,2048]{2,1,0:T(8,128)} %get-tuple-element.101) | copy-start | bytes 3145732
  808.1 12.7 %copy-start.1 = (s32[2,8]{1,0:T(2,128)S(1)}, s32[2,8]{1,0:T(2,128)}, u32[]{:S(2)}) copy-start(s32[2,8]{1,0:T(2,128)} %param.13) | copy-start | bytes 196

commit v5 on v4

--- a/solution.py
+++ b/solution.py
@@ -548,9 +548,11 @@
         return ring_index(self.place + steps, self.count)
 
     def orders(self):
-        for k in range(SUBS):
-            yield k, 0
-            yield SUBS - 1 - k, 1
+        half = SUBS // 2
+        for k in range(half):
+            for sub in (k, k + half):
+                yield sub, 0
+                yield sub, 1
 
 
 def gather_scratch(count):
@@ -609,11 +611,18 @@
             )
         )
 
+    def start_piece(self, sub):
+        for way in range(2):
+            self.pass_on(way, 1, sub)
+        self.hand_over(0, sub, 0)
+
     def start(self):
         for sub, way in self.ring.orders():
-            self.pass_on(way, 1, sub)
-        for sub in range(SUBS):
-            self.hand_over(0, sub, 0)
+            if way == 0:
+                self.start_piece(sub)
+        self.started()
+
+    def started(self):
         self.own = pltpu.make_async_copy(
             self.x_ref,
             self.o_ref.at[aligned((self.ring.me * 2 + self.ring.core) * self.rows, self.rows), :],
@@ -664,7 +673,7 @@
         self.sent()
 
     def run(self, use, work):
-        self.start()
+        self.started()
         self.own.wait()
         waiting = [0]
 
@@ -682,6 +691,111 @@
         while waiting:
             between()
         self.sent()
+
+
+def line_scratch(count):
+    lines = count // 2
+    dma = pltpu.SemaphoreType.DMA
+    return [
+        dma((2, lines)), dma((2, lines)), dma((2 * lines,)), dma((2 * lines,)),
+        dma((2, 2 * lines)), dma((2, 2 * lines)), dma((1,)),
+    ]
+
+
+class LineGather:
+    def __init__(self, ring, x_ref, o_ref, sems):
+        self.ring = ring
+        self.x_ref, self.o_ref = x_ref, o_ref
+        self.lines = ring.count // 2
+        self.line, self.column = ring.me // 2, lax.rem(ring.me, 2)
+        self.next = {DP: ring.me + 1 - 2 * self.column}
+        self.send, self.recv, self.next_send, self.next_recv = sems[:4]
+        self.side_send, self.side_recv, self.own_sem = sems[4:]
+        self.rows = x_ref.shape[0]
+        self.sends = []
+
+    def spot(self, steps, core, column):
+        index = (self.line + steps) * 2 + column
+        return self.o_ref.at[aligned((index * 2 + core) * self.rows, self.rows), :]
+
+    def there(self, steps):
+        if steps == 0:
+            return None
+        return self.line >= -steps if steps < 0 else self.line + steps < self.lines
+
+    def if_there(self, condition, do):
+        if condition is None:
+            do()
+        else:
+            pl.when(condition)(do)
+
+    def go(self, condition, copy):
+        self.if_there(condition, copy.start)
+        self.sends.append((condition, copy))
+
+    def spread(self, steps):
+        ring, slot = self.ring, steps + self.lines
+        source = self.x_ref if steps == 0 else self.spot(steps, ring.core, self.column)
+        target = self.spot(steps, ring.core, self.column)
+        here = self.there(steps)
+        both = lambda other: other if here is None else jnp.logical_and(here, other)
+        for way, ahead in enumerate((self.line + 1 < self.lines, self.line > 0)):
+            passed = -steps if way == 0 else steps
+            if passed >= 0 and passed < self.lines - 1:
+                self.go(
+                    both(ahead),
+                    remote(
+                        source, target, self.send.at[way, passed], self.recv.at[way, passed],
+                        {DP: ring.me + 2 - 4 * way},
+                    ),
+                )
+        self.go(
+            here, remote(source, target, self.next_send.at[slot], self.next_recv.at[slot], self.next)
+        )
+        self.go(
+            here,
+            remote(source, target, self.side_send.at[0, slot], self.side_recv.at[0, slot], ring.side),
+        )
+
+    def start(self):
+        self.spread(0)
+        self.own = pltpu.make_async_copy(
+            self.x_ref, self.spot(0, self.ring.core, self.column), self.own_sem.at[0]
+        )
+        self.own.start()
+
+    def hop(self, hop):
+        for way, steps in enumerate((-hop, hop)):
+            here = self.spot(steps, self.ring.core, self.column)
+            copy = remote(
+                here, here, self.send.at[way, hop - 1], self.recv.at[way, hop - 1], self.next
+            )
+            self.if_there(self.there(steps), copy.wait_recv)
+            self.spread(steps)
+
+    def finish(self):
+        ring = self.ring
+        every = range(1 - self.lines, self.lines)
+        for steps in every:
+            slot = steps + self.lines
+            here = self.spot(steps, ring.core, 1 - self.column)
+            copy = remote(here, here, self.next_send.at[slot], self.next_recv.at[slot], self.next)
+            self.if_there(self.there(steps), copy.wait_recv)
+            self.go(
+                self.there(steps),
+                remote(here, here, self.side_send.at[1, slot], self.side_recv.at[1, slot], ring.side),
+            )
+        for which, column in enumerate((self.column, 1 - self.column)):
+            for steps in every:
+                slot = steps + self.lines
+                here = self.spot(steps, 1 - ring.core, column)
+                copy = remote(
+                    here, here, self.side_send.at[which, slot], self.side_recv.at[which, slot], ring.side
+                )
+                self.if_there(self.there(steps), copy.wait_recv)
+        for condition, copy in self.sends:
+            self.if_there(condition, copy.wait_send)
+        self.own.wait()
 
 
 def reduce_scratch(count, rows, width):
@@ -783,12 +897,14 @@
         far = self.ring.far
         while self.to_make:
             self.make()
-        for sub in range(SUBS):
+        for sub, way in self.ring.orders():
+            if way == 1:
+                continue
             value = self.mine(0, sub)
             for way in range(2):
                 self.ring_copy(way, far, sub).wait_recv()
                 value = value + self.incoming[way, far - 1, self.span(sub), :].astype(jnp.float32)
-            finish(self.span(sub), value)
+            finish(sub, self.span(sub), value)
         for copy in self.sends:
             copy.wait_send()
         for _, copy in self.slots.values():
@@ -954,15 +1070,18 @@
         query = two_heads(kept[here, :wide], head)
         score = dot(query, key2[first : first + keys, :], ((1,), (1,))) * scale
         allowed = triangle(block, keys)
-        total = jnp.sum(jnp.where(allowed, jnp.exp(score), 0.0), axis=1, keepdims=True)
+        power = jnp.where(allowed, jnp.exp(score), 0.0)
+        total = jnp.sum(power, axis=1, keepdims=True)
         log_total = jnp.log(total)
-        probs = jnp.where(allowed, jnp.exp(score - log_total), 0.0).astype(jnp.bfloat16)
+        probs = (power * (1.0 / total)).astype(jnp.bfloat16)
         value = dot(probs, value2[first : first + keys, :], ((1,), (0,)))
         mixed[here, :] = one_row(value, head).astype(mixed.dtype)
         lse[spot] = log_total
 
 
-def attend_back_here(slots, grad, kept, lse, cosine, sine, out, key2, value2, key_sum, value_sum):
+def attend_back_here(
+    slots, grad, kept, lse, cosine, sine, out, key2, value2, key_sum, value_sum, between=None
+):
     groups = slots.shape[0]
     tokens = kept.shape[0]
     block = tokens // groups
@@ -1003,6 +1122,8 @@
         query_grad = one_row(dot(score_grad, key, ((1,), (0,))), head)
         query_grad = query_grad * cosine[turn_rows, :] - swap_halves(query_grad, head) * sine[turn_rows, :]
         out[here, :wide] = query_grad.astype(out.dtype)
+        if between is not None:
+            between(spot)
     for spot in range(groups):
         here = slice(spot * block, (spot + 1) * block)
         turn_rows = slice(spot % span * block, (spot % span + 1) * block)
@@ -1083,15 +1204,8 @@
             source, target, ring.count, heads, srcs, dsts, layer
         )
         self.started, self.local = [], {}
-        count = ring.count
-        sizes = [math.prod(there.shape) for _, there in self.pieces(ring.me, ring.me, self.layer)]
-        arrivals = []
-        for kind in range(KINDS):
-            for k in range(count - 1):
-                part = (k + 1) / (count // 2) if k < count // 2 else 1.0
-                due = sum(sizes[:kind]) + part * sizes[kind]
-                arrivals.append((due if k < count // 2 else due * 0.5, kind, k))
-        self.arrivals = sorted(arrivals)
+        half = ring.count // 2
+        self.near, self.far = list(range(half, ring.count - 1)), list(range(half))
 
     def go(self, copy):
         copy.start()
@@ -1110,16 +1224,18 @@
             self.local[kind] = pltpu.make_async_copy(source, target, self.own_sem.at[kind])
             self.local[kind].start()
 
-    def out(self, kinds):
-        for kind in kinds:
-            for k, peer in enumerate(self.peers):
-                source, target = self.pieces(self.ring.me, peer, self.layer)[kind]
-                self.go(remote(source, target, self.send.at[kind, k], self.recv.at[kind, k], {DP: peer}))
-
-    def pass_on(self, kinds):
-        for _, kind, k in self.arrivals:
-            if kind not in kinds:
-                continue
+    def out(self, kind, places):
+        for k in places:
+            source, target = self.pieces(self.ring.me, self.peers[k], self.layer)[kind]
+            self.go(
+                remote(
+                    source, target, self.send.at[kind, k], self.recv.at[kind, k],
+                    {DP: self.peers[k]},
+                )
+            )
+
+    def pass_on(self, kind, places):
+        for k in places:
             here = self.pieces(self.origins[k], self.ring.me, self.layer)[kind][1]
             remote(
                 here, here, self.send.at[kind, k], self.recv.at[kind, k], {DP: self.origins[k]}
@@ -1215,17 +1331,20 @@
     rows_in.wait()
     unit, _ = unit_rows(s.rows[...])
     s.shard0[...] = (unit * s.gains[0, 0:1, :]).astype(NARROW)
-    first = Gather(ring, s.shard0, s.normed1, s.first_sems)
+    first = LineGather(ring, s.shard0, s.normed1, s.line_sems)
     first.start()
-    spread.out(attention)
-    for hop in range(1, ring.far + 1):
+    for kind in attention:
+        spread.out(kind, spread.far + spread.near)
+    for hop in range(1, ring.far):
         first.hop(hop)
     given_in.wait()
     s.shard1[...] = s.given[...].astype(NARROW)
-    grads = Gather(ring, s.shard1, s.out_grad, s.grads_sems)
+    grads = LineGather(ring, s.shard1, s.out_grad, s.grads_sems)
     grads.start()
-    spread.pass_on(attention)
-    spread.out(feed)
+    for kind in attention:
+        spread.pass_on(kind, spread.near + spread.far)
+    gate, up, down = feed
+    spread.out(gate, spread.far + spread.near)
     spread.own(feed)
     first.finish()
     spread.here(attention)
@@ -1247,37 +1366,51 @@
     put_back(s.by_number, s.mixed0, s.row)
     stores[0].wait()
     grads.hop(1)
-    spread.pass_on(feed)
 
     reduce = Reduce(ring, s.reduce)
     none = Work()
 
-    def second(span, value):
-        s.second[span, :] = s.rows[span, :] + value
-
-    loads = {}
-
-    def gate_up_here():
-        spread.here(feed[:2])
-        loads[0] = copies(s.out_gu.at[0], s.gu)
+    second_rows = Gather(ring, s.shard2, s.normed2, s.gather_sems)
+    next_rows = Gather(ring, s.shard0, s.normed1, s.first_sems)
+
+    def second(sub, span, value):
+        value = s.rows[span, :] + value
+        s.second[span, :] = value
+        unit, _ = unit_rows(value)
+        s.shard2[span, :] = (unit * s.gains[0, 1:2, :]).astype(NARROW)
+        second_rows.start_piece(sub)
+
+    middle = len(spread.far) // 2
+    early, late = spread.near + spread.far[:middle], spread.far[middle:]
+
+    def stage(number):
+        kind, places = ((up, early), (up, late), (down, early), (down, late))[number]
+        spread.out(kind, places)
+        if number == 0:
+            spread.pass_on(gate, spread.near + spread.far)
+        else:
+            kind, places = ((up, early), (up, late), (down, early))[number - 1]
+            spread.pass_on(kind, places)
+        if number + 2 < ring.far:
+            grads.hop(number + 2)
 
     left = reduce.run(
         products(s.mixed0, s.wo_w, False), second, none,
-        [functools.partial(grads.hop, hop) for hop in range(2, ring.far + 1)] + [gate_up_here],
+        [functools.partial(stage, number) for number in range(4)],
     )
     for do in left:
         do()
-    unit, _ = unit_rows(s.second[...])
-    s.shard2[...] = (unit * s.gains[0, 1:2, :]).astype(NARROW)
-    loads[0].wait()
-    spread.here(feed[2:])
-    load = copies(s.out_down.at[0], s.down)
+    spread.pass_on(down, late)
+    spread.here((gate, up))
+    copies(s.out_gu.at[0], s.gu).wait()
 
     def keep(rows, cols, right, gate, upper):
         s.gate_up[rows, cols] = gate
         s.gate_up[rows, right] = upper
 
-    Gather(ring, s.shard2, s.normed2, s.gather_sems).run(feed_forward_use(s, local, keep), none)
+    second_rows.run(feed_forward_use(s, local, keep), none)
+    spread.here((down,))
+    load = copies(s.out_down.at[0], s.down)
     grads.finish()
     stores += [
         copies(s.out_grad, s.out_grad_out), copies(s.normed2, s.normed2_out),
@@ -1285,18 +1418,20 @@
     ]
     load.wait()
 
-    def result(span, value):
-        s.result[span, :] = s.second[span, :] + value
+    def result(sub, span, value):
+        value = s.second[span, :] + value
+        s.result[span, :] = value
+        unit, _ = unit_rows(value)
+        s.shard0[span, :] = (unit * s.gains[1, 0:1, :]).astype(NARROW)
+        next_rows.start_piece(sub)
 
     reduce.run(products(s.hidden, s.down, False), result, none)
-    unit, _ = unit_rows(s.result[...])
-    s.shard0[...] = (unit * s.gains[1, 0:1, :]).astype(NARROW)
 
     def use(index):
         rows = chip_rows(index, local)
         s.projected[rows, :] = dot(s.normed1[rows, :], s.next_qkv_w[...], ((1,), (1,)))
 
-    Gather(ring, s.shard0, s.normed1, s.first_sems).run(use, none)
+    next_rows.run(use, none)
     stores.append(copies(s.normed1, s.next_normed1_out))
     attend_here(s.slots, s.projected, s.cosine, s.sine, s.kept1, s.lse1, s.by_number, s.key2, s.value2)
     put_back(s.by_number, s.mixed1, s.row)
@@ -1353,8 +1488,8 @@
             key2=vmem((tokens, 2 * head), NARROW), value2=vmem((tokens, 2 * head), NARROW),
             by_number=vmem((tokens, 2 * head), NARROW),
             reduce=reduce_scratch(count, local, width),
-            first_sems=gather_scratch(count), grads_sems=gather_scratch(count),
-            gather_sems=gather_scratch(count),
+            first_sems=gather_scratch(count), gather_sems=gather_scratch(count),
+            line_sems=line_scratch(count), grads_sems=line_scratch(count),
             gain_sems=[dma((2 * count - 1,)), dma((2 * count - 1,))],
             spread_sems=[
                 dma((KINDS, count - 1)), dma((KINDS, count - 1)),
@@ -1370,15 +1505,18 @@
     add_gradient(work, s.hidden, s.out_grad, s.grad_down)
     add_gradient(work, s.normed2, s.gu_grad, s.grad_gu)
 
-    def keep(span, value):
-        s.normed_grad[span, :] = value
-
-    left = reduce.run(products(s.gu_grad, s.gu, True), keep, work, beside)
-    part, s.gain_mlp_grad[...] = through_norm(
-        s.normed_grad[...], s.second[...], s.gains[at, 1:2, :]
-    )
-    s.second_grad[...] = s.given[...] + part
-    s.shard2[...] = s.second_grad[...].astype(NARROW)
+    gather = Gather(ring, s.shard2, s.attn_grad, s.gather_sems)
+    s.gain_mlp_grad[...] = jnp.zeros_like(s.gain_mlp_grad)
+
+    def through(sub, span, value):
+        part, gain_part = through_norm(value, s.second[span, :], s.gains[at, 1:2, :])
+        value = s.given[span, :] + part
+        s.second_grad[span, :] = value
+        s.shard2[span, :] = value.astype(NARROW)
+        gather.start_piece(sub)
+        s.gain_mlp_grad[...] += gain_part
+
+    left = reduce.run(products(s.gu_grad, s.gu, True), through, work, beside)
 
     def use(index):
         rows = chip_rows(index, local)
@@ -1386,7 +1524,7 @@
 
     for do in reversed(left):
         work.first(lambda _, do=do: do())
-    Gather(ring, s.shard2, s.attn_grad, s.gather_sems).run(use, work)
+    gather.run(use, work)
     work.do()
 
 
@@ -1402,20 +1540,24 @@
     reduce, other = Reduce(ring, s.reduce), Reduce(ring, s.other)
     work = Work()
 
-    def second(span, value):
-        s.second[span, :] = s.rows[span, :] + value
+    second_rows = Gather(ring, s.shard, s.normed2, s.first_sems)
+
+    def second(sub, span, value):
+        value = s.rows[span, :] + value
+        s.second[span, :] = value
+        unit, _ = unit_rows(value)
+        s.shard[span, :] = (unit * s.gains[at, 1:2, :]).astype(NARROW)
+        second_rows.start_piece(sub)
 
     wo_in.wait()
     reduce.run(products(s.mixed, s.wo, False), second, work)
-    unit, _ = unit_rows(s.second[...])
-    s.shard[...] = (unit * s.gains[at, 1:2, :]).astype(NARROW)
     for load in ins:
         load.wait()
-    Gather(ring, s.shard, s.normed2, s.first_sems).run(
+    second_rows.run(
         feed_forward_use(s, s.rows.shape[0], functools.partial(feed_forward_back, s)), work
     )
 
-    def result(span, value):
+    def result(sub, span, value):
         s.result[span, :] = s.second[span, :] + value
 
     beside = [lambda: other.begin(products(s.hidden, s.down, False), Work())]
@@ -1467,7 +1609,6 @@
             hidden=vmem((tokens, hidden), NARROW), gu_grad=vmem((tokens, 2 * hidden), NARROW),
             grad_down=vmem((hidden, width), NARROW), grad_gu=vmem((width, 2 * hidden), NARROW),
             given=vmem((local, width), WIDE), second=vmem((local, width), WIDE),
-            normed_grad=vmem((local, width), WIDE),
             shard=vmem((local, width), NARROW), shard2=vmem((local, width), NARROW),
             **attend_scratch(tokens, head, True),
             copy_sem=dma((8,)),
@@ -1475,13 +1616,17 @@
     )
 
 
-def attention_back(at, s, reduce, work, beside=()):
-    def keep(span, value):
-        s.normed_grad[span, :] = value
-
-    reduce.run(products(s.qkv_grad, s.qkv_w, False), keep, work, beside)
-    part, s.gain_attn_grad[...] = through_norm(s.normed_grad[...], s.rows[...], s.gains[at, 0:1, :])
-    s.input_grad[...] = s.second_grad_in[...] + part
+def attention_back(at, s, reduce, work, then, beside=()):
+    s.gain_attn_grad[...] = jnp.zeros_like(s.gain_attn_grad)
+
+    def through(sub, span, value):
+        part, gain_part = through_norm(value, s.rows[span, :], s.gains[at, 0:1, :])
+        value = s.second_grad_in[span, :] + part
+        s.input_grad[span, :] = value
+        then(sub, span, value)
+        s.gain_attn_grad[...] += gain_part
+
+    reduce.run(products(s.qkv_grad, s.qkv_w, False), through, work, beside)
 
 
 def backward_body(upper, lower, s):
@@ -1504,12 +1649,17 @@
     add_gradient(work, s.mixed, s.attn_grad, s.grad_wo)
     add_gradient(work, s.normed2, s.qkv_grad, s.grad_qkv)
     qkv_in.wait()
-    attention_back(upper, s, reduce, work)
+    gather = Gather(ring, s.shard, s.out_grad, s.first_sems)
+
+    def go_on(sub, span, value):
+        s.shard[span, :] = value.astype(NARROW)
+        s.given[span, :] = value
+        gather.start_piece(sub)
+
+    attention_back(upper, s, reduce, work, go_on)
     work.do()
     then_in.append(copies(s.normed2_in, s.normed2))
     stores = [copies(s.grad_wo, s.grad_wo_out), copies(s.grad_qkv, s.grad_qkv_out)]
-    s.shard[...] = s.input_grad[...].astype(NARROW)
-    s.given[...] = s.input_grad[...]
     for load in first_in:
         load.wait()
     width = s.hidden.shape[1]
@@ -1526,7 +1676,7 @@
 
         loop(0, number, one)
 
-    Gather(ring, s.shard, s.out_grad, s.first_sems).run(use, work)
+    gather.run(use, work)
     for load in then_in:
         load.wait()
     back_through_feed_forward(lower, s, ring, reduce, work, [])
@@ -1576,7 +1726,7 @@
             attn_grad=vmem((tokens, width), NARROW), gu_grad=vmem((tokens, 2 * hidden), NARROW),
             grad_wo=vmem((q_rows, width), NARROW), grad_qkv=vmem((width, qkv_w.shape[1]), NARROW),
             grad_down=vmem((hidden, width), NARROW), grad_gu=vmem((width, 2 * hidden), NARROW),
-            given=vmem((local, width), WIDE), normed_grad=vmem((local, width), WIDE),
+            given=vmem((local, width), WIDE),
             shard=vmem((local, width), NARROW), shard2=vmem((local, width), NARROW),
             copy_sem=dma((16,)),
         ),
@@ -1731,7 +1881,7 @@
     swap(0, s.results, (s.result0, s.result1))
     attend_back_here(
         s.slots, s.mixed_grad, s.kept, s.lse, s.cosine, s.sine, s.by_number, s.key2, s.value2,
-        s.key_sum, s.value_sum,
+        s.key_sum, s.value_sum, lambda spot: back.some(1) if spot == 1 else None,
     )
     put_back(s.by_number, s.qkv_grad, s.row)
     work = Work()
@@ -1748,7 +1898,7 @@
         back.some(1)
 
     beside = [functools.partial(back.some, 1)] * 2 + [rest] + [functools.partial(back.some, 1)] * (ring.far - 3)
-    attention_back(at, s, Reduce(ring, s.reduce), work, beside)
+    attention_back(at, s, Reduce(ring, s.reduce), work, lambda *_: None, beside)
     swap(1, s.input_grads, (s.input_grad, s.input_grad1))
 
     lanes = s.gain_out.shape[1]
@@ -1824,7 +1974,7 @@
             attn_grad=vmem((tokens, width), NARROW), normed1=vmem((tokens, width), NARROW),
             qkv_grad=vmem((tokens, 4 * head), NARROW),
             grad_wo=vmem((q_rows, width), NARROW), grad_qkv=vmem((width, qkv_rows), NARROW),
-            normed_grad=vmem((local, width), WIDE), input_grad=vmem((local, width), WIDE),
+            input_grad=vmem((local, width), WIDE),
             gain_attn_grad=vmem((1, width), WIDE),
             landed=pieces(), mine=pieces(),
             gain_in=vmem((everyone, 8, lanes), WIDE), gain_landed=vmem((everyone - 1, 8, lanes), WIDE),

time: 834 us -> 810 us (0.971)
  Pallas kernels: 810 us -> 788 us
    pallas_call x4, Pallas kernels: 800 us -> 778 us  [call_fused(): pl.pallas_call(kernel, out_shape=tuple((shape for shape, _ in outs.values...]
where the time goes in v5:
time: 810 us; the launch traced here: 799 us
  Pallas kernels  788 us (97%)
    pallas_call x4, Pallas kernels, call_fused(): pl.pallas_call(kernel, out_shape=tuple((shape for shape, _ in outs.values...  778 us

profile of v5, /device:TPU:0, one launch (start us, length us, event | category | flops | bytes accessed | tf_op | source)
XLA Modules:
  0.0 799.0 jit_solution(4465892908764921097)
XLA Ops:
  0.6 0.0 copy-start
  0.7 0.7 copy-done
  1.3 0.0 copy-start.4
  1.3 0.6 select_reduce_fusion.refs_0_
  2.0 1.0 copy.27
  3.0 1.0 copy.28
  4.0 1.2 copy.26
  5.3 0.9 maximum_bitcast_fusion.refs_6_
  6.2 1.0 fusion.2
  7.2 1.3 pad_maximum_fusion
  8.4 0.0 copy-done.4
  8.5 310.7 %opening.1 = (bf16[2,256,2048]{2,1,0:T(8,128)(2,1)}, bf16[2,128,2048]{2,1,0:T(8,128)(2,1)}, bf16[2,2048,1024]{2,1,0:T(8,128)(2,1)}, bf16[2,512,2048]{2,1,0:T(8,1...) custom-call(s32[8]{0:T(128)} %select_reduce_fusion.refs_0_, ...), custom_call_target="tpu_custom_call" | custom-call | bytes 1328400000 | tf_op jit(solution)/shard_map/opening/pallas_call | solution.py:989
  319.1 141.7 %turn.1 = (f32[64,2048]{1,0:T(8,128)}, f32[64,2048]{1,0:T(8,128)}, bf16[1024,256]{1,0:T(8,128)(2,1)}, bf16[1024,2048]{1,0:T(8,128)(2,1)}, f32[1,2048]{1,0:T(1,12...) custom-call(s32[8]{0:T(128)} %select_reduce_fusion.refs_0_, s32[8]{0:T(128)} %copy-done.4, ...), custom_call_target="tpu_custom_call" | custom-call | bytes 516600000 | tf_op jit(solution)/shard_map/turn/pallas_call | solution.py:989
  460.8 110.1 %backward_between.1 = (f32[64,2048]{1,0:T(8,128)}, f32[64,2048]{1,0:T(8,128)}, bf16[1024,128]{1,0:T(8,128)(2,1)}, bf16[1024,2048]{1,0:T(8,128)(2,1)}, f32[1,2048...) custom-call(f32[64,2048]{1,0:T(8,128)} %get-tuple-element.66.refs_4_, ...), custom_call_target="tpu_custom_call" | custom-call | bytes 424350016 | tf_op jit(solution)/shard_map/backward_between/pallas_call | solution.py:989
  571.0 215.0 %closing.1 = (f32[2,64,2048]{2,1,0:T(8,128)}, f32[2,64,2048]{2,1,0:T(8,128)}, bf16[4096,256]{1,0:T(8,128)(2,1)}, bf16[256,4096]{1,0:T(8,128)(2,1)}, bf16[256,409...) custom-call(s32[8]{0:T(128)} %select_reduce_fusion.refs_0_, ...), custom_call_target="tpu_custom_call" | custom-call | bytes 774899968 | tf_op jit(solution)/shard_map/closing/pallas_call | solution.py:989
  786.0 0.0 copy-start.3
  786.0 0.0 copy-start.2
  786.0 0.0 copy-start.1
  786.0 10.8 %widen.1 = (f32[1,4096,256]{2,1,0:T(8,128)}, f32[1,256,4096]{2,1,0:T(8,128)}, f32[1,256,4096]{2,1,0:T(8,128)}, f32[1,1024,256]{2,1,0:T(8,128)}, f32[1,256,1024]{...) custom-call(bf16[4096,256]{1,0:T(8,128)(2,1)} %get-tuple-element.102.down, ...), custom_call_target="tpu_custom_call" | custom-call | tf_op jit(solution)/shard_map/widen/pallas_call | solution.py:2031
  796.8 0.0 copy-done.3
  796.8 1.0 copy.31
  797.8 0.0 copy-done.2
  797.8 1.0 copy.32
  798.7 0.0 copy-done.1
  (2 shorter events, 0.0 us)
Async XLA Ops:
  0.6 0.7 copy-start
  1.3 7.1 copy-start.4
  786.0 10.8 %copy-start.3 = (f32[2,64,2048]{2,1,0:T(8,128)S(1)}, f32[2,64,2048]{2,1,0:T(8,128)}, u32[]{:S(2)}) copy-start(f32[2,64,2048]{2,1,0:T(8,128)} %get-tuple-element.100) | copy-start | bytes 3145732
  786.0 11.8 %copy-start.2 = (f32[2,64,2048]{2,1,0:T(8,128)S(1)}, f32[2,64,2048]{2,1,0:T(8,128)}, u32[]{:S(2)}) copy-start(f32[2,64,2048]{2,1,0:T(8,128)} %get-tuple-element.101) | copy-start | bytes 3145732
  786.0 12.7 %copy-start.1 = (s32[2,8]{1,0:T(2,128)S(1)}, s32[2,8]{1,0:T(2,128)}, u32[]{:S(2)}) copy-start(s32[2,8]{1,0:T(2,128)} %param.13) | copy-start | bytes 196

commit v6 on v5

--- a/solution.py
+++ b/solution.py
@@ -3,6 +3,7 @@
 
 import jax
 import jax.numpy as jnp
+import numpy as np
 from jax import lax
 from jax.experimental import pallas as pl
 from jax.experimental.pallas import tpu as pltpu
@@ -1158,12 +1159,18 @@
 
 
 def rope_tables(tokens, head):
-    angle = jnp.arange(tokens, dtype=jnp.float32)[:, None] * rope_frequencies(head)[None, :]
-    cosine = jnp.cos(angle)
-    sine = jnp.sin(angle)
+    index = np.arange(head // 2, dtype=np.float32)
+    base = (1.0 / np.float32(500000.0) ** (index * 2.0 / head)).astype(np.float32)
+    wavelength = 2.0 * math.pi / base
+    blend = (8192.0 / wavelength - 1.0) / 3.0
+    middle = (1.0 - blend) * base / 32.0 + blend * base
+    slow = np.where(wavelength > 8192.0, base / 32.0, middle)
+    frequencies = np.where(wavelength < 2048.0, base, slow).astype(np.float32)
+    angle = np.arange(tokens, dtype=np.float32)[:, None] * frequencies[None, :]
+    cosine, sine = np.cos(angle), np.sin(angle)
     return (
-        jnp.concatenate([cosine] * 4, axis=1),
-        jnp.concatenate([-sine, sine] * 2, axis=1),
+        jnp.asarray(np.concatenate([cosine] * 4, axis=1)),
+        jnp.asarray(np.concatenate([-sine, sine] * 2, axis=1)),
     )
 
 
@@ -1522,8 +1529,8 @@
         rows = chip_rows(index, local)
         s.mixed_grad[rows, :] = dot(s.attn_grad[rows, :], s.wo[...], ((1,), (1,))).astype(NARROW)
 
-    for do in reversed(left):
-        work.first(lambda _, do=do: do())
+    for do in left:
+        do()
     gather.run(use, work)
     work.do()
 
@@ -1563,15 +1570,24 @@
     beside = [lambda: other.begin(products(s.hidden, s.down, False), Work())]
     beside += [functools.partial(other.step, step) for step in range(1, ring.far + 1)]
     beside += [lambda: other.end(result)]
-    back_through_feed_forward(at, s, ring, reduce, work, beside)
+    early = ring.far - 1
+    back_through_feed_forward(at, s, ring, reduce, work, beside[:early])
+    beside = beside[early:]
+
+    def between(spot):
+        if beside and spot % 2:
+            beside.pop(0)()
+
     stores = [
         copies(s.grad_down, s.grad_down_out), copies(s.grad_gu, s.grad_gu_out),
         copies(s.attn_grad, s.attn_grad_out),
     ]
     attend_back_here(
         s.slots, s.mixed_grad, s.kept, s.lse, s.cosine, s.sine, s.by_number, s.key2, s.value2,
-        s.key_sum, s.value_sum,
-    )
+        s.key_sum, s.value_sum, between,
+    )
+    for do in beside:
+        do()
     put_back(s.by_number, s.qkv_grad, s.row)
     for store in stores:
         store.wait()

time: 810 us -> 802 us (level)
  no operation moved by 1% of the time
where the time goes in v6:
time: 802 us; the launch traced here: 793 us
  Pallas kernels  784 us (98%)
    pallas_call x4, Pallas kernels, call_fused(): pl.pallas_call(kernel, out_shape=tuple((shape for shape, _ in outs.values...  774 us

profile of v6, /device:TPU:0, one launch (start us, length us, event | category | flops | bytes accessed | tf_op | source)
XLA Modules:
  0.0 792.9 jit_solution(13097845336578964383)
XLA Ops:
  0.6 0.0 copy-start
  0.7 0.7 copy-done
  1.3 0.0 copy-start.4
  1.3 0.6 select_reduce_fusion.refs_0_
  2.0 1.0 copy.29
  3.0 1.0 copy.30
  4.0 1.2 copy.28
  5.2 0.9 maximum_bitcast_fusion.refs_6_
  6.2 0.0 copy-done.4
  6.2 310.7 %opening.1 = (bf16[2,256,2048]{2,1,0:T(8,128)(2,1)}, bf16[2,128,2048]{2,1,0:T(8,128)(2,1)}, bf16[2,2048,1024]{2,1,0:T(8,128)(2,1)}, bf16[2,512,2048]{2,1,0:T(8,1...) custom-call(s32[8]{0:T(128)} %select_reduce_fusion.refs_0_, ...), custom_call_target="tpu_custom_call" | custom-call | bytes 1328400000 | tf_op jit(solution)/shard_map/opening/pallas_call | solution.py:990
  316.8 136.4 %turn.1 = (f32[64,2048]{1,0:T(8,128)}, f32[64,2048]{1,0:T(8,128)}, bf16[1024,256]{1,0:T(8,128)(2,1)}, bf16[1024,2048]{1,0:T(8,128)(2,1)}, f32[1,2048]{1,0:T(1,12...) custom-call(s32[8]{0:T(128)} %select_reduce_fusion.refs_0_, s32[8]{0:T(128)} %copy-done.4, ...), custom_call_target="tpu_custom_call" | custom-call | bytes 516600000 | tf_op jit(solution)/shard_map/turn/pallas_call | solution.py:990
  453.2 111.5 %backward_between.1 = (f32[64,2048]{1,0:T(8,128)}, f32[64,2048]{1,0:T(8,128)}, bf16[1024,128]{1,0:T(8,128)(2,1)}, bf16[1024,2048]{1,0:T(8,128)(2,1)}, f32[1,2048...) custom-call(f32[64,2048]{1,0:T(8,128)} %get-tuple-element.66.refs_4_, ...), custom_call_target="tpu_custom_call" | custom-call | bytes 424350016 | tf_op jit(solution)/shard_map/backward_between/pallas_call | solution.py:990
  564.7 215.2 %closing.1 = (f32[2,64,2048]{2,1,0:T(8,128)}, f32[2,64,2048]{2,1,0:T(8,128)}, bf16[4096,256]{1,0:T(8,128)(2,1)}, bf16[256,4096]{1,0:T(8,128)(2,1)}, bf16[256,409...) custom-call(s32[8]{0:T(128)} %select_reduce_fusion.refs_0_, ...), custom_call_target="tpu_custom_call" | custom-call | bytes 774899968 | tf_op jit(solution)/shard_map/closing/pallas_call | solution.py:990
  779.9 0.0 copy-start.3
  779.9 0.0 copy-start.2
  779.9 0.0 copy-start.1
  779.9 10.8 %widen.1 = (f32[1,4096,256]{2,1,0:T(8,128)}, f32[1,256,4096]{2,1,0:T(8,128)}, f32[1,256,4096]{2,1,0:T(8,128)}, f32[1,1024,256]{2,1,0:T(8,128)}, f32[1,256,1024]{...) custom-call(bf16[4096,256]{1,0:T(8,128)(2,1)} %get-tuple-element.102.down, ...), custom_call_target="tpu_custom_call" | custom-call | tf_op jit(solution)/shard_map/widen/pallas_call | solution.py:2047
  790.7 0.0 copy-done.3
  790.7 1.0 copy.33
  791.7 0.0 copy-done.2
  791.7 1.0 copy.34
  792.7 0.0 copy-done.1
  (1 shorter events, 0.0 us)
Async XLA Ops:
  0.6 0.7 copy-start
  1.3 4.8 copy-start.4
  779.9 10.8 %copy-start.3 = (f32[2,64,2048]{2,1,0:T(8,128)S(1)}, f32[2,64,2048]{2,1,0:T(8,128)}, u32[]{:S(2)}) copy-start(f32[2,64,2048]{2,1,0:T(8,128)} %get-tuple-element.100) | copy-start | bytes 3145732
  779.9 11.8 %copy-start.2 = (f32[2,64,2048]{2,1,0:T(8,128)S(1)}, f32[2,64,2048]{2,1,0:T(8,128)}, u32[]{:S(2)}) copy-start(f32[2,64,2048]{2,1,0:T(8,128)} %get-tuple-element.101) | copy-start | bytes 3145732
  779.9 12.7 %copy-start.1 = (s32[2,8]{1,0:T(2,128)S(1)}, s32[2,8]{1,0:T(2,128)}, u32[]{:S(2)}) copy-start(s32[2,8]{1,0:T(2,128)} %param.15) | copy-start | bytes 196

commit v7 on v6

--- a/solution.py
+++ b/solution.py
@@ -922,8 +922,9 @@
         return beside
 
 
-def products(left, right, transposed, tile=512):
+def products(left, right, transposed, tile=2048):
     width = right.shape[0] if transposed else right.shape[1]
+    tile = math.gcd(tile, width)
     number = width // tile
 
     def produce(index, parts):
@@ -943,7 +944,8 @@
     return produce
 
 
-def add_gradient(work, left, right, out, tile=256):
+def add_gradient(work, left, right, out, tile=512):
+    tile = math.gcd(tile, max(out.shape))
     if out.shape[0] >= out.shape[1]:
 
         def piece(at):
@@ -1507,10 +1509,10 @@
     )
 
 
-def back_through_feed_forward(at, s, ring, reduce, work, beside):
+def back_through_feed_forward(at, s, ring, reduce, work, beside, tile, piece):
     local = s.given.shape[0]
-    add_gradient(work, s.hidden, s.out_grad, s.grad_down)
-    add_gradient(work, s.normed2, s.gu_grad, s.grad_gu)
+    add_gradient(work, s.hidden, s.out_grad, s.grad_down, piece)
+    add_gradient(work, s.normed2, s.gu_grad, s.grad_gu, piece)
 
     gather = Gather(ring, s.shard2, s.attn_grad, s.gather_sems)
     s.gain_mlp_grad[...] = jnp.zeros_like(s.gain_mlp_grad)
@@ -1523,7 +1525,7 @@
         gather.start_piece(sub)
         s.gain_mlp_grad[...] += gain_part
 
-    left = reduce.run(products(s.gu_grad, s.gu, True), through, work, beside)
+    left = reduce.run(products(s.gu_grad, s.gu, True, tile), through, work, beside)
 
     def use(index):
         rows = chip_rows(index, local)
@@ -1546,6 +1548,7 @@
     ]
     reduce, other = Reduce(ring, s.reduce), Reduce(ring, s.other)
     work = Work()
+    tile = 512
 
     second_rows = Gather(ring, s.shard, s.normed2, s.first_sems)
 
@@ -1557,7 +1560,7 @@
         second_rows.start_piece(sub)
 
     wo_in.wait()
-    reduce.run(products(s.mixed, s.wo, False), second, work)
+    reduce.run(products(s.mixed, s.wo, False, tile), second, work)
     for load in ins:
         load.wait()
     second_rows.run(
@@ -1567,11 +1570,11 @@
     def result(sub, span, value):
         s.result[span, :] = s.second[span, :] + value
 
-    beside = [lambda: other.begin(products(s.hidden, s.down, False), Work())]
+    beside = [lambda: other.begin(products(s.hidden, s.down, False, tile), Work())]
     beside += [functools.partial(other.step, step) for step in range(1, ring.far + 1)]
     beside += [lambda: other.end(result)]
     early = ring.far - 1
-    back_through_feed_forward(at, s, ring, reduce, work, beside[:early])
+    back_through_feed_forward(at, s, ring, reduce, work, beside[:early], tile, 256)
     beside = beside[early:]
 
     def between(spot):
@@ -1695,7 +1698,7 @@
     gather.run(use, work)
     for load in then_in:
         load.wait()
-    back_through_feed_forward(lower, s, ring, reduce, work, [])
+    back_through_feed_forward(lower, s, ring, reduce, work, [], 2048, 512)
     stores += [
         copies(s.grad_down, s.grad_down_out), copies(s.grad_gu, s.grad_gu_out),
         copies(s.attn_grad, s.attn_grad_out),

time: 802 us -> 806 us (level)
  no operation moved by 1% of the time
where the time goes in v7:
time: 806 us; the launch traced here: 797 us
  Pallas kernels  789 us (98%)
    pallas_call x4, Pallas kernels, call_fused(): pl.pallas_call(kernel, out_shape=tuple((shape for shape, _ in outs.values...  778 us

profile of v7, /device:TPU:0, one launch (start us, length us, event | category | flops | bytes accessed | tf_op | source)
XLA Modules:
  0.0 797.2 jit_solution(12567821800897966738)
XLA Ops:
  0.6 0.0 copy-start
  0.7 0.7 copy-done
  1.3 0.0 copy-start.4
  1.3 0.6 select_reduce_fusion.refs_0_
  2.0 1.0 copy.29
  3.0 1.0 copy.30
  4.0 1.2 copy.28
  5.2 0.9 maximum_bitcast_fusion.refs_6_
  6.2 0.0 copy-done.4
  6.2 310.2 %opening.1 = (bf16[2,256,2048]{2,1,0:T(8,128)(2,1)}, bf16[2,128,2048]{2,1,0:T(8,128)(2,1)}, bf16[2,2048,1024]{2,1,0:T(8,128)(2,1)}, bf16[2,512,2048]{2,1,0:T(8,1...) custom-call(s32[8]{0:T(128)} %select_reduce_fusion.refs_0_, ...), custom_call_target="tpu_custom_call" | custom-call | bytes 1328400000 | tf_op jit(solution)/shard_map/opening/pallas_call | solution.py:992
  316.4 144.8 %turn.1 = (f32[64,2048]{1,0:T(8,128)}, f32[64,2048]{1,0:T(8,128)}, bf16[1024,256]{1,0:T(8,128)(2,1)}, bf16[1024,2048]{1,0:T(8,128)(2,1)}, f32[1,2048]{1,0:T(1,12...) custom-call(s32[8]{0:T(128)} %select_reduce_fusion.refs_0_, s32[8]{0:T(128)} %copy-done.4, ...), custom_call_target="tpu_custom_call" | custom-call | bytes 516600000 | tf_op jit(solution)/shard_map/turn/pallas_call | solution.py:992
  461.2 108.1 %backward_between.1 = (f32[64,2048]{1,0:T(8,128)}, f32[64,2048]{1,0:T(8,128)}, bf16[1024,128]{1,0:T(8,128)(2,1)}, bf16[1024,2048]{1,0:T(8,128)(2,1)}, f32[1,2048...) custom-call(f32[64,2048]{1,0:T(8,128)} %get-tuple-element.66.refs_4_, ...), custom_call_target="tpu_custom_call" | custom-call | bytes 424350016 | tf_op jit(solution)/shard_map/backward_between/pallas_call | solution.py:992
  569.3 214.7 %closing.1 = (f32[2,64,2048]{2,1,0:T(8,128)}, f32[2,64,2048]{2,1,0:T(8,128)}, bf16[4096,256]{1,0:T(8,128)(2,1)}, bf16[256,4096]{1,0:T(8,128)(2,1)}, bf16[256,409...) custom-call(s32[8]{0:T(128)} %select_reduce_fusion.refs_0_, ...), custom_call_target="tpu_custom_call" | custom-call | bytes 774899968 | tf_op jit(solution)/shard_map/closing/pallas_call | solution.py:992
  784.0 0.0 copy-start.3
  784.0 0.0 copy-start.2
  784.1 0.0 copy-start.1
  784.1 10.8 %widen.1 = (f32[1,4096,256]{2,1,0:T(8,128)}, f32[1,256,4096]{2,1,0:T(8,128)}, f32[1,256,4096]{2,1,0:T(8,128)}, f32[1,1024,256]{2,1,0:T(8,128)}, f32[1,256,1024]{...) custom-call(bf16[4096,256]{1,0:T(8,128)(2,1)} %get-tuple-element.102.down, ...), custom_call_target="tpu_custom_call" | custom-call | tf_op jit(solution)/shard_map/widen/pallas_call | solution.py:2050
  794.8 0.0 copy-done.3
  794.9 1.0 copy.33
  795.8 0.0 copy-done.2
  795.8 1.0 copy.34
  796.8 0.0 copy-done.1
  (1 shorter events, 0.0 us)
Async XLA Ops:
  0.6 0.7 copy-start
  1.3 4.8 copy-start.4
  784.0 10.8 %copy-start.3 = (f32[2,64,2048]{2,1,0:T(8,128)S(1)}, f32[2,64,2048]{2,1,0:T(8,128)}, u32[]{:S(2)}) copy-start(f32[2,64,2048]{2,1,0:T(8,128)} %get-tuple-element.100) | copy-start | bytes 3145732
  784.0 11.8 %copy-start.2 = (f32[2,64,2048]{2,1,0:T(8,128)S(1)}, f32[2,64,2048]{2,1,0:T(8,128)}, u32[]{:S(2)}) copy-start(f32[2,64,2048]{2,1,0:T(8,128)} %get-tuple-element.101) | copy-start | bytes 3145732
  784.1 12.7 %copy-start.1 = (s32[2,8]{1,0:T(2,128)S(1)}, s32[2,8]{1,0:T(2,128)}, u32[]{:S(2)}) copy-start(s32[2,8]{1,0:T(2,128)} %param.15) | copy-start | bytes 196
